TPU v7x, 32 devices: a whole 2x2x4 slice. The times are simulated.
32 devices in a mesh: space: 8 (over y, x, core), tm: 4 (over z).
Axes of the slice: x: 2, y: 2, z: 4, core: 2. Of those that a mesh axis runs over, the one named last changes fastest.
Arguments:
- tensor: float32 [512, 64, 512], P('space', None, 'tm'), may hold values from -6 to 6
- species_factor: float32 [64, 256], replicated, may hold values from -6 to 6
- time_factor: float32 [512, 256], P('tm'), may hold values from -6 to 6
Outputs:
- space_out: float32 [512, 256], P('space')
- species_out: float32 [64, 256], replicated
- time_out: float32 [512, 256], P('tm')
All inputs are finite; a program needn't handle non-finite values.
Results may differ from a plain program's by a relative error of at most 0.0001.
Values sent between devices are 32-bit elements; how exact they have to be, the bound alone decides.
No kernel may reach another device: no remote copies, remote signals or barrier semaphores. Data moves between devices by JAX's collectives and lax.ppermute only.
A program may use at most 64 MiB of HBM per device.

v0:
```python
import jax
import jax.numpy as jnp
from jax import lax
from jax.experimental import pallas as pl
from jax.experimental.pallas import tpu as pltpu
from jax.sharding import PartitionSpec as P


ridge_share = 0.1
epsilon = 1e-06
contraction_bound = 1e-3
highest = lax.Precision.HIGHEST
f32 = jnp.float32
bf16 = jnp.bfloat16

vmem = pl.BlockSpec(memory_space=pltpu.VMEM)
flops_per_micro = 1e9
vmem_limit = 24 * 1024 * 1024


def dot(a, b, dims=((1,), (0,))):
    return lax.dot_general(a, b, (dims, ((), ())), precision=highest, preferred_element_type=f32)


def dot_fast(a, b, dims=((1,), (0,))):
    return lax.dot_general(a, b, (dims, ((), ())), preferred_element_type=f32)


def gram(factor):
    return dot(factor, factor, ((0,), (0,)))


def split(x):
    high = x.astype(bf16)
    return high, (x - high.astype(f32)).astype(bf16)


def tree_sum(values):
    values = list(values)
    while len(values) > 1:
        values = [a + b for a, b in zip(values[0::2], values[1::2])]
    return values[0]


def eye_mask(n):
    return lax.broadcasted_iota(jnp.int32, (n, n), 0) == lax.broadcasted_iota(jnp.int32, (n, n), 1)


def regularized(matrix):
    n = matrix.shape[0]
    eye = eye_mask(n)
    diagonal = jnp.where(eye, matrix, 0.0)
    ridge = ridge_share * jnp.sum(diagonal) / n
    return matrix + jnp.where(eye, ridge, 0.0)


def invert(matrix, x_ref, work_ref):
    n = matrix.shape[0]
    eye = eye_mask(n)
    diagonal = jnp.where(eye, matrix, 0.0)
    by_column = lax.rsqrt(jnp.sum(diagonal, axis=0, keepdims=True))
    by_row = lax.rsqrt(jnp.sum(diagonal, axis=1, keepdims=True))
    e1 = jnp.where(eye, 0.0, -(matrix * by_column) * by_row)
    e1_half = e1.astype(bf16)
    e2 = dot_fast(e1_half, e1_half)
    e2_half = e2.astype(bf16)
    e4 = dot_fast(e2_half, e2_half)
    e4_half = e4.astype(bf16)
    part = e1 + e2 + dot_fast(e1_half, e2_half)
    part = part + e4 + dot_fast(part.astype(bf16), e4_half)
    left = jnp.sum(e4 * e4)
    x_ref[...] = (part + jnp.where(eye, 1.0, 0.0)) * by_column * by_row

    @pl.when(jnp.logical_not(left < contraction_bound))
    def _():
        work_ref[...] = jnp.where(eye, 1.0, 0.0) - e1
        lane = lax.broadcasted_iota(jnp.int32, (n, n), 1)
        sublane = lax.broadcasted_iota(jnp.int32, (n, n), 0)
        lane_row = lax.broadcasted_iota(jnp.int32, (1, n), 1)

        def step(k, carry):
            work = work_ref[...]
            row = work_ref[pl.ds(k, 1), :]
            pivot = jnp.sum(jnp.where(lane_row == k, row, 0.0), axis=1, keepdims=True)
            column = jnp.sum(jnp.where(lane == k, work, 0.0), axis=1, keepdims=True)
            inverse = 1.0 / pivot
            new_row = jnp.where(lane_row == k, inverse, row * inverse)
            others = jnp.where(lane == k, 0.0, work) - column * new_row
            work_ref[...] = jnp.where(sublane == k, new_row, others)
            return carry

        lax.fori_loop(0, n, step, 0)
        x_ref[...] = work_ref[...] * by_column * by_row


def solve(right, matrix, inverse):
    first = dot(right, inverse)
    return first + dot(right - dot(first, matrix), inverse)


def place_of(axis):
    return lax.axis_index(axis)


def at_rows(block, rows):
    return pl.ds(pl.multiple_of(block * rows, rows), rows)


def space_kernel(chunk, tensor_hbm, time_hbm, species_hbm,
                 m_a_ref, side_ref, tensor_ref, time_ref, species_ref, arrived):
    rows, species_count, steps = tensor_ref.shape
    copies = [
        pltpu.make_async_copy(time_hbm, time_ref, arrived.at[0]),
        pltpu.make_async_copy(species_hbm, species_ref, arrived.at[1]),
    ]
    for i in range(rows // chunk):
        block = pl.ds(i * chunk, chunk)
        copies.append(pltpu.make_async_copy(tensor_hbm.at[block], tensor_ref.at[block], arrived.at[2 + i]))
    for copy in copies:
        copy.start()
    copies[0].wait()
    copies[1].wait()
    time_high, time_low = split(time_ref[...])
    weights = jnp.concatenate([time_high, time_low, time_low, time_high], axis=0)
    species = species_ref[...]
    for i in range(rows // chunk):
        copies[2 + i].wait()
        start = i * chunk
        high, low = split(tensor_ref[start:start + chunk].reshape(chunk * species_count, steps))
        side = dot_fast(jnp.concatenate([high, low, high, low], axis=1), weights)
        side = side.reshape(chunk, species_count, side.shape[1])
        side_ref[start:start + chunk] = side
        m_a_ref[start:start + chunk, :] = jnp.sum(side * species[None], axis=1)


def pack_kernel(after_ref, *refs):
    *parts, out_ref = refs
    rows = parts[0].shape[0]
    for j, part in enumerate(parts):
        out_ref[j * rows:(j + 1) * rows, :] = part[...]


def sum_kernel(*refs):
    *parts, out_ref = refs
    out_ref[...] = tree_sum([part[...] for part in parts])


def transpose_kernel(after_ref, tensor_ref, high_ref, low_ref):
    rows, species_count, steps = tensor_ref.shape
    chunk = 8
    width = chunk * species_count
    for start in range(0, rows, chunk):
        turned = tensor_ref[start:start + chunk].reshape(width, steps).T
        high, low = split(turned)
        high_ref[:, start * species_count:start * species_count + width] = high
        low_ref[:, start * species_count:start * species_count + width] = low


def first_inverse_kernel(species_ref, own_ref, mine_ref, partner_ref,
                         c_gram_ref, matrix_ref, inverse_ref, factor_ref, work_ref):
    block, core = place_of("tm"), place_of("space") % 2
    rows = own_ref.shape[0]
    half = rows // 2
    factor_ref[at_rows(block, rows), :] = own_ref[...]
    for j in range(mine_ref.shape[0] // half):
        other = jnp.bitwise_xor(block, j + 1) * 2
        factor_ref[at_rows(other + core, half), :] = mine_ref[j * half:(j + 1) * half, :]
        factor_ref[at_rows(other + 1 - core, half), :] = partner_ref[j * half:(j + 1) * half, :]
    c_gram = gram(factor_ref[...])
    c_gram_ref[...] = c_gram
    matrix = regularized(gram(species_ref[...]) * c_gram)
    matrix_ref[...] = matrix
    invert(matrix, inverse_ref, work_ref)


def space_solve_kernel(matrix_ref, inverse_ref, side_ref, *refs):
    *parts, raw_ref, m_b_ref = refs
    m_a = tree_sum([part[...] for part in parts])
    raw_ref[...] = solve(m_a, matrix_ref[...], inverse_ref[...])
    total = jnp.zeros(m_b_ref.shape, f32)
    for s in range(side_ref.shape[0]):
        total = total + side_ref[s] * raw_ref[pl.ds(s, 1), :]
    m_b_ref[...] = total


def space_gram_kernel(rows, c_gram_ref, mine_ref, partner_ref,
                      a_gram_ref, matrix_ref, scale_ref, raw_ref, out_ref, factor_ref):
    place = place_of("space")
    for j in range(mine_ref.shape[0] // rows):
        block = jnp.bitwise_xor(place, 2 * j)
        factor_ref[at_rows(block, rows), :] = mine_ref[j * rows:(j + 1) * rows, :]
        factor_ref[at_rows(jnp.bitwise_xor(block, 1), rows), :] = partner_ref[j * rows:(j + 1) * rows, :]
    raw_gram = gram(factor_ref[...])
    eye = eye_mask(raw_gram.shape[0])
    diagonal = jnp.where(eye, raw_gram, 0.0)
    total_rows = factor_ref.shape[0]
    by_column = lax.rsqrt(jnp.sum(diagonal, axis=0, keepdims=True) / total_rows + epsilon)
    by_row = lax.rsqrt(jnp.sum(diagonal, axis=1, keepdims=True) / total_rows + epsilon)
    scale_ref[...] = jnp.broadcast_to(by_column, scale_ref.shape)
    space = mine_ref[:rows, :] * by_column
    raw_ref[...] = space
    out_ref[...] = space
    a_gram = raw_gram * by_column * by_row
    a_gram_ref[...] = a_gram
    matrix_ref[...] = regularized(a_gram * c_gram_ref[...])


def inverse_kernel(matrix_ref, inverse_ref, work_ref):
    invert(matrix_ref[...], inverse_ref, work_ref)


def species_kernel(mine_ref, partner_ref, scale_ref, matrix_ref, inverse_ref, space_ref, high_ref, low_ref,
                   species_ref, out_ref, keep_ref, send_ref, product_ref):
    core = place_of("space") % 2
    m_b = (mine_ref[...] + partner_ref[...]) * scale_ref[0:1, :]
    raw = solve(m_b, matrix_ref[...], inverse_ref[...])
    species = raw * lax.rsqrt(jnp.mean(raw * raw, axis=0, keepdims=True) + epsilon)
    species_ref[...] = species
    out_ref[...] = species
    rows = space_ref.shape[0]
    species_count = species.shape[0]
    chunk = 8
    width = chunk * species_count
    total = jnp.zeros(product_ref.shape, f32)
    for start in range(0, rows, chunk):
        weights = species[None] * space_ref[start:start + chunk, :][:, None, :]
        weights_high, weights_low = split(weights.reshape(width, species.shape[1]))
        columns = slice(start * species_count, start * species_count + width)
        high, low = high_ref[:, columns], low_ref[:, columns]
        total = total + (dot_fast(high, weights_high) + (dot_fast(high, weights_low) + dot_fast(low, weights_high)))
    product_ref[...] = total
    half = keep_ref.shape[0]
    keep_ref[...] = product_ref[at_rows(core, half), :]
    send_ref[...] = product_ref[at_rows(1 - core, half), :]


def species_gram_kernel(a_gram_ref, species_ref, matrix_ref):
    matrix_ref[...] = regularized(a_gram_ref[...] * gram(species_ref[...]))


def time_solve_kernel(matrix_ref, inverse_ref, mine_ref, partner_ref, raw_ref, squares_ref, m_c_ref):
    core = place_of("space") % 2
    half = mine_ref.shape[0]
    m_c_ref[at_rows(core, half), :] = mine_ref[...]
    m_c_ref[at_rows(1 - core, half), :] = partner_ref[...]
    raw = solve(m_c_ref[...], matrix_ref[...], inverse_ref[...])
    raw_ref[...] = raw
    squares_ref[...] = jnp.broadcast_to(jnp.sum(raw * raw, axis=0, keepdims=True), squares_ref.shape)


def time_scale_kernel(total_steps, raw_ref, *refs):
    *parts, out_ref = refs
    squares = tree_sum([part[0:1, :] for part in parts])
    out_ref[...] = raw_ref[...] * lax.rsqrt(squares / total_steps + epsilon)


def exchange(value, axis, step, count):
    return lax.ppermute(value, axis, [(i, i ^ step) for i in range(count)])


def run(kernel, outs, micros, scratch=()):
    call = pl.pallas_call(
        kernel,
        out_shape=outs,
        out_specs=[vmem] * len(outs),
        scratch_shapes=list(scratch),
        cost_estimate=pl.CostEstimate(flops=int(micros * flops_per_micro), bytes_accessed=0, transcendentals=0),
        compiler_params=pltpu.CompilerParams(vmem_limit_bytes=vmem_limit),
    )

    def placed(*operands):
        return call(*[pltpu.with_memory_space_constraint(x, pltpu.VMEM) for x in operands])

    return placed


def on_device(tensor, species_factor, time_factor):
    row_count, species_count, step_count = tensor.shape
    rank = species_factor.shape[1]
    devices = lax.axis_size("space")
    blocks = lax.axis_size("tm")
    chips = devices // 2
    total_rows = row_count * devices
    total_steps = step_count * blocks
    core = lax.axis_index("space") % 2

    def local(*dims):
        return pltpu.VMEM(dims, f32)

    def result(*dims):
        return jax.ShapeDtypeStruct(dims, f32)

    square = local(rank, rank)

    def over_time(value):
        return [value] + [exchange(value, "tm", j, blocks) for j in range(1, blocks)]

    def over_chips(value):
        return [value] + [exchange(value, "space", 2 * j, devices) for j in range(1, chips)]

    def to_partner(value):
        return exchange(value, "space", 1, devices)

    def pack(after, parts):
        return run(pack_kernel, [local(len(parts) * parts[0].shape[0], rank)], 0.3)(after, *parts)[0]

    def add(parts):
        return run(sum_kernel, [local(*parts[0].shape)], 0.3)(*parts)[0]

    half_steps = step_count // 2
    own_half = lax.dynamic_slice_in_dim(time_factor, core * half_steps, half_steps)
    halves = over_time(own_half)[1:]

    chunk = 8
    outside = pl.BlockSpec(memory_space=pltpu.HBM)
    m_a, side, tensor_here, time_here, species_here = pl.pallas_call(
        lambda *refs: space_kernel(chunk, *refs),
        in_specs=[outside] * 3,
        out_specs=[vmem] * 5,
        out_shape=[
            local(row_count, rank),
            local(row_count, species_count, rank),
            local(row_count, species_count, step_count),
            local(step_count, rank),
            local(species_count, rank),
        ],
        scratch_shapes=[pltpu.SemaphoreType.DMA((2 + row_count // chunk,))],
        cost_estimate=pl.CostEstimate(flops=int(3 * flops_per_micro), bytes_accessed=0, transcendentals=0),
        compiler_params=pltpu.CompilerParams(vmem_limit_bytes=vmem_limit),
        name="space_products",
    )(*[pltpu.with_memory_space_constraint(x, pltpu.HBM) for x in (tensor, time_factor, species_factor)])
    m_a_parts = over_time(m_a)

    halves = pack(m_a, halves)
    partner_halves = to_partner(halves)
    c_gram, matrix, inverse = run(
        first_inverse_kernel, [square] * 3, 2, [local(total_steps, rank), square]
    )(species_here, time_here, halves, partner_halves)

    raw, m_b = run(
        space_solve_kernel, [local(row_count, rank), local(species_count, rank)], 1
    )(matrix, inverse, side, *m_a_parts)
    m_b_parts = over_time(m_b)
    raw_chips = over_chips(raw)
    turned = pltpu.VMEM((step_count, row_count * species_count), bf16)
    high, low = run(transpose_kernel, [turned] * 2, 1)(m_b, tensor_here)
    m_b_parts = over_chips(add(m_b_parts))
    raw_mine = pack(m_b, raw_chips)
    raw_partner = to_partner(raw_mine)
    a_gram, matrix, scale, space, space_out = run(
        lambda *refs: space_gram_kernel(row_count, *refs),
        [square, square, local(8, rank), local(row_count, rank), result(row_count, rank)],
        1.5,
        [local(total_rows, rank)],
    )(c_gram, raw_mine, raw_partner)
    (inverse,) = run(inverse_kernel, [square], 1, [square])(matrix)
    m_b = add(m_b_parts)
    m_b_partner = to_partner(m_b)

    species, species_out, m_c_keep, m_c_send = run(
        species_kernel,
        [local(species_count, rank), result(species_count, rank), local(half_steps, rank), local(half_steps, rank)],
        3,
        [local(step_count, rank)],
    )(m_b, m_b_partner, scale, matrix, inverse, space, high, low)

    m_c_received = to_partner(m_c_send)
    (matrix,) = run(species_gram_kernel, [square], 0.5)(a_gram, species)
    m_c_parts = over_chips(add([m_c_keep, m_c_received]))
    (inverse,) = run(inverse_kernel, [square], 1, [square])(matrix)
    m_c = add(m_c_parts)
    m_c_partner = to_partner(m_c)
    raw_time, squares = run(
        time_solve_kernel, [local(step_count, rank), local(8, rank)], 1, [local(step_count, rank)]
    )(matrix, inverse, m_c, m_c_partner)

    squares = over_time(squares)
    (time_out,) = run(
        lambda *refs: time_scale_kernel(total_steps, *refs), [result(step_count, rank)], 0.5
    )(raw_time, *squares)
    return (space_out, species_out, time_out)


def solution(mesh):
    placed = (P("space", None, "tm"), P(), P("tm", None))
    return jax.shard_map(
        on_device,
        mesh=mesh,
        in_specs=placed,
        out_specs=(P("space", None), P(), P("tm", None)),
        check_vma=False,
    )
```

profile of v0, /device:TPU:0, one launch (start us, length us, event | category | flops | bytes accessed | tf_op | source)
XLA Modules:
  0.0 104.4 jit_solution(7750329281232684258)
XLA Ops:
  0.6 0.8 constant_dynamic-slice_fusion
  1.5 3.1 %collective-permute-start = (f32[64,256]{1,0:T(8,128)S(1)}, f32[64,256]{1,0:T(8,128)S(1)}, u32[]{:S(2)}, u32[]{:S(2)}) collective-permute-start(f32[64,256]{1,0:T(8,128)S(1)} %constant_dynamic-slice_fusion), channel_id=1, source_target_pairs={{0,1},{1,0},{2,3},{3,2},{4,5},{5,4},{6,7},{7,6},{8,9},{9,8},{10,11... | collective-permute-start | bytes 196616 | tf_op jit(solution)/shard_map/ppermute | solution.py:258
  4.5 2.6 %collective-permute-start.1 = (f32[64,256]{1,0:T(8,128)S(1)}, f32[64,256]{1,0:T(8,128)S(1)}, u32[]{:S(2)}, u32[]{:S(2)}) collective-permute-start(f32[64,256]{1,0:T(8,128)S(1)} %constant_dynamic-slice_fusion), channel_id=1, source_target_pairs={{0,2},{1,3},{2,0},{3,1},{4,6},{5,7},{6,4},{7,5},{8,10},{9,11},{10,... | collective-permute-start | bytes 196616 | tf_op jit(solution)/shard_map/ppermute | solution.py:258
  7.1 4.6 %space_products.1 = (f32[64,256]{1,0:T(8,128)S(1)}, f32[64,64,256]{2,1,0:T(8,128)S(1)}, f32[64,64,128]{2,1,0:T(8,128)S(1)}, f32[128,256]{1,0:T(8,128)S(1)}, f32[64,256]{1,0:T(8,128)S(1)}) custom-call(f32[64,64,128]{2,1,0:T(8,128)} %refs_0_.1, f32[128,256]{1,0:T(8,128)} %refs_1_.1, f32[64,256]{1,0:T(8,128)} %refs_2_.1), custom_call_target="tpu_custom_call" | custom-call | flops 3000000000 | tf_op jit(solution)/shard_map/space_products/pallas_call | solution.py:316
  11.8 1.4 %collective-permute-done.2.refs_2_ = f32[64,256]{1,0:T(8,128)S(1)} collective-permute-done((f32[64,256]{1,0:T(8,128)S(1)}, f32[64,256]{1,0:T(8,128)S(1)}, u32[]{:S(2)}, u32[]{:S(2)}) %collective-permute-start.2) | collective-permute-done | bytes 65568 | tf_op jit(solution)/shard_map/ppermute | solution.py:258
  13.4 2.9 %collective-permute-start.5 = (f32[64,256]{1,0:T(8,128)S(1)}, f32[64,256]{1,0:T(8,128)S(1)}, u32[]{:S(2)}, u32[]{:S(2)}) collective-permute-start(f32[64,256]{1,0:T(8,128)S(1)} %get-tuple-element.28.after_ref.refs_0_), channel_id=1, source_target_pairs={{0,2},{1,3},{2,0},{3,1},{4,6},{5,7},{6,4},{7,5},{8,10},{9,11},{10,... | collective-permute-start | bytes 196616 | tf_op jit(solution)/shard_map/ppermute | solution.py:258
  16.3 1.5 %collective-permute-start.6 = (f32[64,256]{1,0:T(8,128)S(1)}, f32[64,256]{1,0:T(8,128)S(1)}, u32[]{:S(2)}, u32[]{:S(2)}) collective-permute-start(f32[64,256]{1,0:T(8,128)S(1)} %get-tuple-element.28.after_ref.refs_0_), channel_id=1, source_target_pairs={{0,3},{1,2},{2,1},{3,0},{4,7},{5,6},{6,5},{7,4},{8,11},{9,10},{10,... | collective-permute-start | bytes 196616 | tf_op jit(solution)/shard_map/ppermute | solution.py:258
  17.8 35.9 %shard_map.59 = (f32[256,256]{1,0:T(8,128)S(1)}, f32[256,256]{1,0:T(8,128)S(1)}, f32[256,256]{1,0:T(8,128)S(1)}) custom-call(f32[64,256]{1,0:T(8,128)S(1)} %get-tuple-element.26.species_ref, f32[128,256]{1,0:T(8,128)S(1)} %get-tuple-element.27.own_ref, f32[192,256]{1,0:T(8,128)S(1)} %shard_map.58.mine_ref, f32[192,256]{1,0:T(8,128)S(1)} %collective-permute-done.3.partner_ref), custom_call_target="tpu_custom_call" | custom-call | flops 2000000000 | tf_op jit(solution)/shard_map/pallas_call | solution.py:272
  53.7 1.1 %shard_map.60 = (f32[64,256]{1,0:T(8,128)S(1)}, f32[64,256]{1,0:T(8,128)S(1)}) custom-call(f32[256,256]{1,0:T(8,128)S(1)} %get-tuple-element.30.matrix_ref, f32[256,256]{1,0:T(8,128)S(1)} %get-tuple-element.31.inverse_ref, f32[64,64,256]{2,1,0:T(8,128)S(1)} %get-tuple-element.32.side_ref, f32[64,256]{1,0:T(8,128)S(1)} %get-tuple-element.28.after_ref.refs_0_, ...), custom_call_target="tpu_custom_call" | custom-call | flops 1000000000 | tf_op jit(solution)/shard_map/pallas_call | solution.py:272
  54.8 1.6 %collective-permute-start.7 = (f32[64,256]{1,0:T(8,128)S(1)}, f32[64,256]{1,0:T(8,128)S(1)}, u32[]{:S(2)}, u32[]{:S(2)}) collective-permute-start(f32[64,256]{1,0:T(8,128)S(1)} %get-tuple-element.34.refs_0_), channel_id=1, source_target_pairs={{0,8},{4,12},{8,0},{12,4},{16,24},{20,28},{24,16},{28,20},{1,9},{5... | collective-permute-start | bytes 196616 | tf_op jit(solution)/shard_map/ppermute | solution.py:258
  56.4 1.5 %collective-permute-start.8 = (f32[64,256]{1,0:T(8,128)S(1)}, f32[64,256]{1,0:T(8,128)S(1)}, u32[]{:S(2)}, u32[]{:S(2)}) collective-permute-start(f32[64,256]{1,0:T(8,128)S(1)} %get-tuple-element.34.refs_0_), channel_id=1, source_target_pairs={{0,16},{4,20},{8,24},{12,28},{16,0},{20,4},{24,8},{28,12},{1,17},{... | collective-permute-start | bytes 196616 | tf_op jit(solution)/shard_map/ppermute | solution.py:258
  57.9 0.5 collective-permute-start.9
  58.4 0.8 collective-permute-done.7.refs_1_
  59.2 2.2 %collective-permute-done.8.refs_2_ = f32[64,256]{1,0:T(8,128)S(1)} collective-permute-done((f32[64,256]{1,0:T(8,128)S(1)}, f32[64,256]{1,0:T(8,128)S(1)}, u32[]{:S(2)}, u32[]{:S(2)}) %collective-permute-start.8) | collective-permute-done | bytes 65568 | tf_op jit(solution)/shard_map/ppermute | solution.py:258
  61.4 1.7 %collective-permute-done.9.refs_3_ = f32[64,256]{1,0:T(8,128)S(1)} collective-permute-done((f32[64,256]{1,0:T(8,128)S(1)}, f32[64,256]{1,0:T(8,128)S(1)}, u32[]{:S(2)}, u32[]{:S(2)}) %collective-permute-start.9) | collective-permute-done | bytes 65568 | tf_op jit(solution)/shard_map/ppermute | solution.py:258
  63.3 2.9 %collective-permute-start.12 = (f32[64,256]{1,0:T(8,128)S(1)}, f32[64,256]{1,0:T(8,128)S(1)}, u32[]{:S(2)}, u32[]{:S(2)}) collective-permute-start(f32[64,256]{1,0:T(8,128)S(1)} %get-tuple-element.33.after_ref.refs_0_), channel_id=1, source_target_pairs={{0,2},{1,3},{2,0},{3,1},{4,6},{5,7},{6,4},{7,5},{8,10},{9,11},{10,... | collective-permute-start | bytes 196616 | tf_op jit(solution)/shard_map/ppermute | solution.py:258
  66.2 1.5 %collective-permute-start.13 = (f32[64,256]{1,0:T(8,128)S(1)}, f32[64,256]{1,0:T(8,128)S(1)}, u32[]{:S(2)}, u32[]{:S(2)}) collective-permute-start(f32[64,256]{1,0:T(8,128)S(1)} %get-tuple-element.33.after_ref.refs_0_), channel_id=1, source_target_pairs={{0,3},{1,2},{2,1},{3,0},{4,7},{5,6},{6,5},{7,4},{8,11},{9,10},{10,... | collective-permute-start | bytes 196616 | tf_op jit(solution)/shard_map/ppermute | solution.py:258
  67.6 1.2 %collective-permute-done.11.refs_1_ = f32[64,256]{1,0:T(8,128)S(1)} collective-permute-done((f32[64,256]{1,0:T(8,128)S(1)}, f32[64,256]{1,0:T(8,128)S(1)}, u32[]{:S(2)}, u32[]{:S(2)}) %collective-permute-start.11) | collective-permute-done | bytes 65568 | tf_op jit(solution)/shard_map/ppermute | solution.py:258
  68.9 1.5 %collective-permute-done.12.refs_2_ = f32[64,256]{1,0:T(8,128)S(1)} collective-permute-done((f32[64,256]{1,0:T(8,128)S(1)}, f32[64,256]{1,0:T(8,128)S(1)}, u32[]{:S(2)}, u32[]{:S(2)}) %collective-permute-start.12) | collective-permute-done | bytes 65568 | tf_op jit(solution)/shard_map/ppermute | solution.py:258
  70.3 1.9 %collective-permute-done.13.refs_3_ = f32[64,256]{1,0:T(8,128)S(1)} collective-permute-done((f32[64,256]{1,0:T(8,128)S(1)}, f32[64,256]{1,0:T(8,128)S(1)}, u32[]{:S(2)}, u32[]{:S(2)}) %collective-permute-start.13) | collective-permute-done | bytes 65568 | tf_op jit(solution)/shard_map/ppermute | solution.py:258
  72.3 0.6 collective-permute-start.14
  72.9 0.5 collective-permute-start.15
  73.4 2.4 %collective-permute-start.16 = (f32[64,256]{1,0:T(8,128)S(1)}, f32[64,256]{1,0:T(8,128)S(1)}, u32[]{:S(2)}, u32[]{:S(2)}) collective-permute-start(f32[64,256]{1,0:T(8,128)S(1)} %shard_map.63.refs_0_), channel_id=1, source_target_pairs={{0,24},{4,28},{8,16},{12,20},{16,8},{20,12},{24,0},{28,4},{1,25},{... | collective-permute-start | bytes 196616 | tf_op jit(solution)/shard_map/ppermute | solution.py:258
  75.8 0.6 shard_map.66
  76.4 0.2 collective-permute-done.14.refs_1_
  76.6 0.5 collective-permute-done.15.refs_2_
  77.1 1.4 %collective-permute-done.16.refs_3_ = f32[64,256]{1,0:T(8,128)S(1)} collective-permute-done((f32[64,256]{1,0:T(8,128)S(1)}, f32[64,256]{1,0:T(8,128)S(1)}, u32[]{:S(2)}, u32[]{:S(2)}) %collective-permute-start.16) | collective-permute-done | bytes 65568 | tf_op jit(solution)/shard_map/ppermute | solution.py:258
  78.7 1.4 %shard_map.62 = (f32[256,256]{1,0:T(8,128)S(1)}, f32[256,256]{1,0:T(8,128)S(1)}, f32[8,256]{1,0:T(8,128)S(1)}, f32[64,256]{1,0:T(8,128)S(1)}, f32[64,256]{1,0:T(8,128)}) custom-call(f32[256,256]{1,0:T(8,128)S(1)} %get-tuple-element.29.refs_0_, f32[256,256]{1,0:T(8,128)S(1)} %shard_map.61.refs_1_, f32[256,256]{1,0:T(8,128)S(1)} %collective-permute-done.10.refs_2_), custom_call_target="tpu_custom_call" | custom-call | flops 1500000000 | tf_op jit(solution)/shard_map/pallas_call | solution.py:272
  80.1 0.7 shard_map.65.inverse_ref
  80.8 2.8 %shard_map.67 = (f32[64,256]{1,0:T(8,128)S(1)}, f32[64,256]{1,0:T(8,128)}, f32[64,256]{1,0:T(8,128)S(1)}, f32[64,256]{1,0:T(8,128)S(1)}) custom-call(f32[64,256]{1,0:T(8,128)S(1)} %shard_map.64.mine_ref, f32[64,256]{1,0:T(8,128)S(1)} %collective-permute-done.17.partner_ref, f32[8,256]{1,0:T(8,128)S(1)} %get-tuple-element.36.scale_ref, ...), custom_call_target="tpu_custom_call" | custom-call | flops 3000000000 | tf_op jit(solution)/shard_map/pallas_call | solution.py:272
  83.6 0.5 collective-permute-start.18
  84.1 0.9 collective-permute-done.18.refs_1_
  85.0 1.6 %collective-permute-start.19 = (f32[64,256]{1,0:T(8,128)S(1)}, f32[64,256]{1,0:T(8,128)S(1)}, u32[]{:S(2)}, u32[]{:S(2)}) collective-permute-start(f32[64,256]{1,0:T(8,128)S(1)} %shard_map.70.refs_0_), channel_id=1, source_target_pairs={{0,8},{4,12},{8,0},{12,4},{16,24},{20,28},{24,16},{28,20},{1,9},{5... | collective-permute-start | bytes 196616 | tf_op jit(solution)/shard_map/ppermute | solution.py:258
  86.6 1.5 %collective-permute-start.20 = (f32[64,256]{1,0:T(8,128)S(1)}, f32[64,256]{1,0:T(8,128)S(1)}, u32[]{:S(2)}, u32[]{:S(2)}) collective-permute-start(f32[64,256]{1,0:T(8,128)S(1)} %shard_map.70.refs_0_), channel_id=1, source_target_pairs={{0,16},{4,20},{8,24},{12,28},{16,0},{20,4},{24,8},{28,12},{1,17},{... | collective-permute-start | bytes 196616 | tf_op jit(solution)/shard_map/ppermute | solution.py:258
  88.1 0.5 collective-permute-start.21
  88.6 0.6 shard_map.68.matrix_ref
  89.2 0.3 collective-permute-done.19.refs_1_
  89.5 1.4 %collective-permute-done.20.refs_2_ = f32[64,256]{1,0:T(8,128)S(1)} collective-permute-done((f32[64,256]{1,0:T(8,128)S(1)}, f32[64,256]{1,0:T(8,128)S(1)}, u32[]{:S(2)}, u32[]{:S(2)}) %collective-permute-start.20) | collective-permute-done | bytes 65568 | tf_op jit(solution)/shard_map/ppermute | solution.py:258
  90.9 2.4 %collective-permute-done.21.refs_3_ = f32[64,256]{1,0:T(8,128)S(1)} collective-permute-done((f32[64,256]{1,0:T(8,128)S(1)}, f32[64,256]{1,0:T(8,128)S(1)}, u32[]{:S(2)}, u32[]{:S(2)}) %collective-permute-start.21) | collective-permute-done | bytes 65568 | tf_op jit(solution)/shard_map/ppermute | solution.py:258
  93.4 0.7 shard_map.69.inverse_ref
  94.1 0.5 collective-permute-done.22.partner_ref
  94.6 0.9 shard_map.72
  95.5 1.2 %collective-permute-start.23 = (f32[8,256]{1,0:T(8,128)S(1)}, f32[8,256]{1,0:T(8,128)S(1)}, u32[]{:S(2)}, u32[]{:S(2)}) collective-permute-start(f32[8,256]{1,0:T(8,128)S(1)} %get-tuple-element.48.refs_1_), channel_id=1, source_target_pairs={{0,1},{1,0},{2,3},{3,2},{4,5},{5,4},{6,7},{7,6},{8,9},{9,8},{10,11... | collective-permute-start | bytes 24584 | tf_op jit(solution)/shard_map/ppermute | solution.py:258
  96.8 1.5 %collective-permute-start.24 = (f32[8,256]{1,0:T(8,128)S(1)}, f32[8,256]{1,0:T(8,128)S(1)}, u32[]{:S(2)}, u32[]{:S(2)}) collective-permute-start(f32[8,256]{1,0:T(8,128)S(1)} %get-tuple-element.48.refs_1_), channel_id=1, source_target_pairs={{0,2},{1,3},{2,0},{3,1},{4,6},{5,7},{6,4},{7,5},{8,10},{9,11},{10,... | collective-permute-start | bytes 24584 | tf_op jit(solution)/shard_map/ppermute | solution.py:258
  98.3 1.7 %collective-permute-start.25 = (f32[8,256]{1,0:T(8,128)S(1)}, f32[8,256]{1,0:T(8,128)S(1)}, u32[]{:S(2)}, u32[]{:S(2)}) collective-permute-start(f32[8,256]{1,0:T(8,128)S(1)} %get-tuple-element.48.refs_1_), channel_id=1, source_target_pairs={{0,3},{1,2},{2,1},{3,0},{4,7},{5,6},{6,5},{7,4},{8,11},{9,10},{10,... | collective-permute-start | bytes 24584 | tf_op jit(solution)/shard_map/ppermute | solution.py:258
  100.0 1.4 %collective-permute-done.24.refs_3_ = f32[8,256]{1,0:T(8,128)S(1)} collective-permute-done((f32[8,256]{1,0:T(8,128)S(1)}, f32[8,256]{1,0:T(8,128)S(1)}, u32[]{:S(2)}, u32[]{:S(2)}) %collective-permute-start.24) | collective-permute-done | bytes 8224 | tf_op jit(solution)/shard_map/ppermute | solution.py:258
  101.4 2.4 %collective-permute-done.25.refs_4_ = f32[8,256]{1,0:T(8,128)S(1)} collective-permute-done((f32[8,256]{1,0:T(8,128)S(1)}, f32[8,256]{1,0:T(8,128)S(1)}, u32[]{:S(2)}, u32[]{:S(2)}) %collective-permute-start.25) | collective-permute-done | bytes 8224 | tf_op jit(solution)/shard_map/ppermute | solution.py:258
  103.7 0.7 shard_map.73
  (22 shorter events, 0.6 us)
Async XLA Ops:
  1.5 10.2 %collective-permute-start = (f32[64,256]{1,0:T(8,128)S(1)}, f32[64,256]{1,0:T(8,128)S(1)}, u32[]{:S(2)}, u32[]{:S(2)}) collective-permute-start(f32[64,256]{1,0:T(8,128)S(1)} %constant_dynamic-slice_fusion), channel_id=1, source_target_pairs={{0,1},{1,0},{2,3},{3,2},{4,5},{5,4},{6,7},{7,6},{8,9},{9,8},{10,11... | collective-permute-start | bytes 196616 | tf_op jit(solution)/shard_map/ppermute | solution.py:258
  4.5 7.3 %collective-permute-start.1 = (f32[64,256]{1,0:T(8,128)S(1)}, f32[64,256]{1,0:T(8,128)S(1)}, u32[]{:S(2)}, u32[]{:S(2)}) collective-permute-start(f32[64,256]{1,0:T(8,128)S(1)} %constant_dynamic-slice_fusion), channel_id=1, source_target_pairs={{0,2},{1,3},{2,0},{3,1},{4,6},{5,7},{6,4},{7,5},{8,10},{9,11},{10,... | collective-permute-start | bytes 196616 | tf_op jit(solution)/shard_map/ppermute | solution.py:258
  7.1 6.1 %collective-permute-start.2 = (f32[64,256]{1,0:T(8,128)S(1)}, f32[64,256]{1,0:T(8,128)S(1)}, u32[]{:S(2)}, u32[]{:S(2)}) collective-permute-start(f32[64,256]{1,0:T(8,128)S(1)} %constant_dynamic-slice_fusion), channel_id=1, source_target_pairs={{0,3},{1,2},{2,1},{3,0},{4,7},{5,6},{6,5},{7,4},{8,11},{9,10},{10,... | collective-permute-start | bytes 196616 | tf_op jit(solution)/shard_map/ppermute | solution.py:258
  13.2 4.5 %collective-permute-start.3 = (f32[192,256]{1,0:T(8,128)S(1)}, f32[192,256]{1,0:T(8,128)S(1)}, u32[]{:S(2)}, u32[]{:S(2)}) collective-permute-start(f32[192,256]{1,0:T(8,128)S(1)} %shard_map.58.mine_ref), channel_id=1, source_target_pairs={{0,4},{4,0},{8,12},{12,8},{16,20},{20,16},{24,28},{28,24},{1,5},{5... | collective-permute-start | bytes 589832 | tf_op jit(solution)/shard_map/ppermute | solution.py:258
  13.3 40.4 %collective-permute-start.4 = (f32[64,256]{1,0:T(8,128)S(1)}, f32[64,256]{1,0:T(8,128)S(1)}, u32[]{:S(2)}, u32[]{:S(2)}) collective-permute-start(f32[64,256]{1,0:T(8,128)S(1)} %get-tuple-element.28.after_ref.refs_0_), channel_id=1, source_target_pairs={{0,1},{1,0},{2,3},{3,2},{4,5},{5,4},{6,7},{7,6},{8,9},{9,8},{10,11... | collective-permute-start | bytes 196616 | tf_op jit(solution)/shard_map/ppermute | solution.py:258
  13.4 40.3 %collective-permute-start.5 = (f32[64,256]{1,0:T(8,128)S(1)}, f32[64,256]{1,0:T(8,128)S(1)}, u32[]{:S(2)}, u32[]{:S(2)}) collective-permute-start(f32[64,256]{1,0:T(8,128)S(1)} %get-tuple-element.28.after_ref.refs_0_), channel_id=1, source_target_pairs={{0,2},{1,3},{2,0},{3,1},{4,6},{5,7},{6,4},{7,5},{8,10},{9,11},{10,... | collective-permute-start | bytes 196616 | tf_op jit(solution)/shard_map/ppermute | solution.py:258
  16.3 37.4 %collective-permute-start.6 = (f32[64,256]{1,0:T(8,128)S(1)}, f32[64,256]{1,0:T(8,128)S(1)}, u32[]{:S(2)}, u32[]{:S(2)}) collective-permute-start(f32[64,256]{1,0:T(8,128)S(1)} %get-tuple-element.28.after_ref.refs_0_), channel_id=1, source_target_pairs={{0,3},{1,2},{2,1},{3,0},{4,7},{5,6},{6,5},{7,4},{8,11},{9,10},{10,... | collective-permute-start | bytes 196616 | tf_op jit(solution)/shard_map/ppermute | solution.py:258
  54.8 4.3 %collective-permute-start.7 = (f32[64,256]{1,0:T(8,128)S(1)}, f32[64,256]{1,0:T(8,128)S(1)}, u32[]{:S(2)}, u32[]{:S(2)}) collective-permute-start(f32[64,256]{1,0:T(8,128)S(1)} %get-tuple-element.34.refs_0_), channel_id=1, source_target_pairs={{0,8},{4,12},{8,0},{12,4},{16,24},{20,28},{24,16},{28,20},{1,9},{5... | collective-permute-start | bytes 196616 | tf_op jit(solution)/shard_map/ppermute | solution.py:258
  56.4 5.0 %collective-permute-start.8 = (f32[64,256]{1,0:T(8,128)S(1)}, f32[64,256]{1,0:T(8,128)S(1)}, u32[]{:S(2)}, u32[]{:S(2)}) collective-permute-start(f32[64,256]{1,0:T(8,128)S(1)} %get-tuple-element.34.refs_0_), channel_id=1, source_target_pairs={{0,16},{4,20},{8,24},{12,28},{16,0},{20,4},{24,8},{28,12},{1,17},{... | collective-permute-start | bytes 196616 | tf_op jit(solution)/shard_map/ppermute | solution.py:258
  57.9 5.2 %collective-permute-start.9 = (f32[64,256]{1,0:T(8,128)S(1)}, f32[64,256]{1,0:T(8,128)S(1)}, u32[]{:S(2)}, u32[]{:S(2)}) collective-permute-start(f32[64,256]{1,0:T(8,128)S(1)} %get-tuple-element.34.refs_0_), channel_id=1, source_target_pairs={{0,24},{4,28},{8,16},{12,20},{16,8},{20,12},{24,0},{28,4},{1,25},{... | collective-permute-start | bytes 196616 | tf_op jit(solution)/shard_map/ppermute | solution.py:258
  63.1 15.5 %collective-permute-start.10 = (f32[256,256]{1,0:T(8,128)S(1)}, f32[256,256]{1,0:T(8,128)S(1)}, u32[]{:S(2)}, u32[]{:S(2)}) collective-permute-start(f32[256,256]{1,0:T(8,128)S(1)} %shard_map.61.refs_1_), channel_id=1, source_target_pairs={{0,4},{4,0},{8,12},{12,8},{16,20},{20,16},{24,28},{28,24},{1,5},{5... | collective-permute-start | bytes 786440 | tf_op jit(solution)/shard_map/ppermute | solution.py:258
  63.2 5.7 %collective-permute-start.11 = (f32[64,256]{1,0:T(8,128)S(1)}, f32[64,256]{1,0:T(8,128)S(1)}, u32[]{:S(2)}, u32[]{:S(2)}) collective-permute-start(f32[64,256]{1,0:T(8,128)S(1)} %get-tuple-element.33.after_ref.refs_0_), channel_id=1, source_target_pairs={{0,1},{1,0},{2,3},{3,2},{4,5},{5,4},{6,7},{7,6},{8,9},{9,8},{10,11... | collective-permute-start | bytes 196616 | tf_op jit(solution)/shard_map/ppermute | solution.py:258
  63.3 7.0 %collective-permute-start.12 = (f32[64,256]{1,0:T(8,128)S(1)}, f32[64,256]{1,0:T(8,128)S(1)}, u32[]{:S(2)}, u32[]{:S(2)}) collective-permute-start(f32[64,256]{1,0:T(8,128)S(1)} %get-tuple-element.33.after_ref.refs_0_), channel_id=1, source_target_pairs={{0,2},{1,3},{2,0},{3,1},{4,6},{5,7},{6,4},{7,5},{8,10},{9,11},{10,... | collective-permute-start | bytes 196616 | tf_op jit(solution)/shard_map/ppermute | solution.py:258
  66.2 6.1 %collective-permute-start.13 = (f32[64,256]{1,0:T(8,128)S(1)}, f32[64,256]{1,0:T(8,128)S(1)}, u32[]{:S(2)}, u32[]{:S(2)}) collective-permute-start(f32[64,256]{1,0:T(8,128)S(1)} %get-tuple-element.33.after_ref.refs_0_), channel_id=1, source_target_pairs={{0,3},{1,2},{2,1},{3,0},{4,7},{5,6},{6,5},{7,4},{8,11},{9,10},{10,... | collective-permute-start | bytes 196616 | tf_op jit(solution)/shard_map/ppermute | solution.py:258
  72.3 4.3 %collective-permute-start.14 = (f32[64,256]{1,0:T(8,128)S(1)}, f32[64,256]{1,0:T(8,128)S(1)}, u32[]{:S(2)}, u32[]{:S(2)}) collective-permute-start(f32[64,256]{1,0:T(8,128)S(1)} %shard_map.63.refs_0_), channel_id=1, source_target_pairs={{0,8},{4,12},{8,0},{12,4},{16,24},{20,28},{24,16},{28,20},{1,9},{5... | collective-permute-start | bytes 196616 | tf_op jit(solution)/shard_map/ppermute | solution.py:258
  72.9 4.3 %collective-permute-start.15 = (f32[64,256]{1,0:T(8,128)S(1)}, f32[64,256]{1,0:T(8,128)S(1)}, u32[]{:S(2)}, u32[]{:S(2)}) collective-permute-start(f32[64,256]{1,0:T(8,128)S(1)} %shard_map.63.refs_0_), channel_id=1, source_target_pairs={{0,16},{4,20},{8,24},{12,28},{16,0},{20,4},{24,8},{28,12},{1,17},{... | collective-permute-start | bytes 196616 | tf_op jit(solution)/shard_map/ppermute | solution.py:258
  73.4 5.2 %collective-permute-start.16 = (f32[64,256]{1,0:T(8,128)S(1)}, f32[64,256]{1,0:T(8,128)S(1)}, u32[]{:S(2)}, u32[]{:S(2)}) collective-permute-start(f32[64,256]{1,0:T(8,128)S(1)} %shard_map.63.refs_0_), channel_id=1, source_target_pairs={{0,24},{4,28},{8,16},{12,20},{16,8},{20,12},{24,0},{28,4},{1,25},{... | collective-permute-start | bytes 196616 | tf_op jit(solution)/shard_map/ppermute | solution.py:258
  78.6 2.2 %collective-permute-start.17 = (f32[64,256]{1,0:T(8,128)S(1)}, f32[64,256]{1,0:T(8,128)S(1)}, u32[]{:S(2)}, u32[]{:S(2)}) collective-permute-start(f32[64,256]{1,0:T(8,128)S(1)} %shard_map.64.mine_ref), channel_id=1, source_target_pairs={{0,4},{4,0},{8,12},{12,8},{16,20},{20,16},{24,28},{28,24},{1,5},{5... | collective-permute-start | bytes 196616 | tf_op jit(solution)/shard_map/ppermute | solution.py:258
  83.6 1.4 %collective-permute-start.18 = (f32[64,256]{1,0:T(8,128)S(1)}, f32[64,256]{1,0:T(8,128)S(1)}, u32[]{:S(2)}, u32[]{:S(2)}) collective-permute-start(f32[64,256]{1,0:T(8,128)S(1)} %get-tuple-element.46), channel_id=1, source_target_pairs={{0,4},{4,0},{8,12},{12,8},{16,20},{20,16},{24,28},{28,24},{1,5},{5... | collective-permute-start | bytes 196616 | tf_op jit(solution)/shard_map/ppermute | solution.py:258
  85.0 4.4 %collective-permute-start.19 = (f32[64,256]{1,0:T(8,128)S(1)}, f32[64,256]{1,0:T(8,128)S(1)}, u32[]{:S(2)}, u32[]{:S(2)}) collective-permute-start(f32[64,256]{1,0:T(8,128)S(1)} %shard_map.70.refs_0_), channel_id=1, source_target_pairs={{0,8},{4,12},{8,0},{12,4},{16,24},{20,28},{24,16},{28,20},{1,9},{5... | collective-permute-start | bytes 196616 | tf_op jit(solution)/shard_map/ppermute | solution.py:258
  86.6 4.3 %collective-permute-start.20 = (f32[64,256]{1,0:T(8,128)S(1)}, f32[64,256]{1,0:T(8,128)S(1)}, u32[]{:S(2)}, u32[]{:S(2)}) collective-permute-start(f32[64,256]{1,0:T(8,128)S(1)} %shard_map.70.refs_0_), channel_id=1, source_target_pairs={{0,16},{4,20},{8,24},{12,28},{16,0},{20,4},{24,8},{28,12},{1,17},{... | collective-permute-start | bytes 196616 | tf_op jit(solution)/shard_map/ppermute | solution.py:258
  88.1 5.2 %collective-permute-start.21 = (f32[64,256]{1,0:T(8,128)S(1)}, f32[64,256]{1,0:T(8,128)S(1)}, u32[]{:S(2)}, u32[]{:S(2)}) collective-permute-start(f32[64,256]{1,0:T(8,128)S(1)} %shard_map.70.refs_0_), channel_id=1, source_target_pairs={{0,24},{4,28},{8,16},{12,20},{16,8},{20,12},{24,0},{28,4},{1,25},{... | collective-permute-start | bytes 196616 | tf_op jit(solution)/shard_map/ppermute | solution.py:258
  93.3 1.3 %collective-permute-start.22 = (f32[64,256]{1,0:T(8,128)S(1)}, f32[64,256]{1,0:T(8,128)S(1)}, u32[]{:S(2)}, u32[]{:S(2)}) collective-permute-start(f32[64,256]{1,0:T(8,128)S(1)} %shard_map.71.mine_ref), channel_id=1, source_target_pairs={{0,4},{4,0},{8,12},{12,8},{16,20},{20,16},{24,28},{28,24},{1,5},{5... | collective-permute-start | bytes 196616 | tf_op jit(solution)/shard_map/ppermute | solution.py:258
  95.5 4.5 %collective-permute-start.23 = (f32[8,256]{1,0:T(8,128)S(1)}, f32[8,256]{1,0:T(8,128)S(1)}, u32[]{:S(2)}, u32[]{:S(2)}) collective-permute-start(f32[8,256]{1,0:T(8,128)S(1)} %get-tuple-element.48.refs_1_), channel_id=1, source_target_pairs={{0,1},{1,0},{2,3},{3,2},{4,5},{5,4},{6,7},{7,6},{8,9},{9,8},{10,11... | collective-permute-start | bytes 24584 | tf_op jit(solution)/shard_map/ppermute | solution.py:258
  96.8 4.6 %collective-permute-start.24 = (f32[8,256]{1,0:T(8,128)S(1)}, f32[8,256]{1,0:T(8,128)S(1)}, u32[]{:S(2)}, u32[]{:S(2)}) collective-permute-start(f32[8,256]{1,0:T(8,128)S(1)} %get-tuple-element.48.refs_1_), channel_id=1, source_target_pairs={{0,2},{1,3},{2,0},{3,1},{4,6},{5,7},{6,4},{7,5},{8,10},{9,11},{10,... | collective-permute-start | bytes 24584 | tf_op jit(solution)/shard_map/ppermute | solution.py:258
  98.3 5.4 %collective-permute-start.25 = (f32[8,256]{1,0:T(8,128)S(1)}, f32[8,256]{1,0:T(8,128)S(1)}, u32[]{:S(2)}, u32[]{:S(2)}) collective-permute-start(f32[8,256]{1,0:T(8,128)S(1)} %get-tuple-element.48.refs_1_), channel_id=1, source_target_pairs={{0,3},{1,2},{2,1},{3,0},{4,7},{5,6},{6,5},{7,4},{8,11},{9,10},{10,... | collective-permute-start | bytes 24584 | tf_op jit(solution)/shard_map/ppermute | solution.py:258
where the time goes:
time: 105 us; the launch traced here: 104 us
  Pallas kernels  50.1 us (48%)
  starting transfers between devices  30.4 us (29%)
  waiting for transfers between devices  22.2 us (21%)
    pallas_call x16, Pallas kernels, placed(): call(*[pltpu.with_memory_space_constraint(x, pltpu.VMEM) for x in operands])  45.5 us
    ppermute x26, starting transfers between devices, exchange(): return lax.ppermute(value, axis, [(i, i ^ step) for i in range(count)])  30.4 us
    ppermute x26, waiting for transfers between devices, exchange(): return lax.ppermute(value, axis, [(i, i ^ step) for i in range(count)])  22.2 us
    pallas_call x1, Pallas kernels, on_device(): pl.pallas_call(lambda *refs: space_kernel(chunk, *refs), in_specs=[outsid...  4.57 us
  transfers between devices with their start and end apart: 26, of which 18 were waited for; matrix products, arithmetic and copies ran while one was open for 0% of the time, Pallas kernels for 43%

commit v1 on v0

v1 whole, which is shorter than its diff:
```python
import jax
import jax.numpy as jnp
from jax import lax
from jax.experimental import pallas as pl
from jax.experimental.pallas import tpu as pltpu
from jax.sharding import PartitionSpec as P


TIME_PAIR = True
RAW_PAIR = True
MB_HALF = True
ridge_share = 0.1
epsilon = 1e-06
contraction_bound = 1e-3
highest = lax.Precision.HIGHEST
f32 = jnp.float32
bf16 = jnp.bfloat16

vmem = pl.BlockSpec(memory_space=pltpu.VMEM)
flops_per_micro = 1e9
vmem_limit = 24 * 1024 * 1024


def dot(a, b, dims=((1,), (0,))):
    return lax.dot_general(a, b, (dims, ((), ())), precision=highest, preferred_element_type=f32)


def dot_fast(a, b, dims=((1,), (0,))):
    return lax.dot_general(a, b, (dims, ((), ())), preferred_element_type=f32)


def gram(factor):
    return dot(factor, factor, ((0,), (0,)))


def split(x):
    high = x.astype(bf16)
    return high, (x - high.astype(f32)).astype(bf16)


def tree_sum(values):
    values = list(values)
    while len(values) > 1:
        values = [a + b for a, b in zip(values[0::2], values[1::2])]
    return values[0]


def eye_mask(n):
    return lax.broadcasted_iota(jnp.int32, (n, n), 0) == lax.broadcasted_iota(jnp.int32, (n, n), 1)


def regularized(matrix):
    n = matrix.shape[0]
    eye = eye_mask(n)
    diagonal = jnp.where(eye, matrix, 0.0)
    ridge = ridge_share * jnp.sum(diagonal) / n
    return matrix + jnp.where(eye, ridge, 0.0)


def invert(matrix, x_ref, work_ref):
    n = matrix.shape[0]
    eye = eye_mask(n)
    diagonal = jnp.where(eye, matrix, 0.0)
    by_column = lax.rsqrt(jnp.sum(diagonal, axis=0, keepdims=True))
    by_row = lax.rsqrt(jnp.sum(diagonal, axis=1, keepdims=True))
    e1 = jnp.where(eye, 0.0, -(matrix * by_column) * by_row)
    e1_half = e1.astype(bf16)
    e2 = dot_fast(e1_half, e1_half)
    e2_half = e2.astype(bf16)
    e4 = dot_fast(e2_half, e2_half)
    e4_half = e4.astype(bf16)
    part = e1 + e2 + dot_fast(e1_half, e2_half)
    part = part + e4 + dot_fast(part.astype(bf16), e4_half)
    left = jnp.sum(e4 * e4)
    x_ref[...] = (part + jnp.where(eye, 1.0, 0.0)) * by_column * by_row

    @pl.when(jnp.logical_not(left < contraction_bound))
    def _():
        work_ref[...] = jnp.where(eye, 1.0, 0.0) - e1
        lane = lax.broadcasted_iota(jnp.int32, (n, n), 1)
        sublane = lax.broadcasted_iota(jnp.int32, (n, n), 0)
        lane_row = lax.broadcasted_iota(jnp.int32, (1, n), 1)

        def step(k, carry):
            work = work_ref[...]
            row = work_ref[pl.ds(k, 1), :]
            pivot = jnp.sum(jnp.where(lane_row == k, row, 0.0), axis=1, keepdims=True)
            column = jnp.sum(jnp.where(lane == k, work, 0.0), axis=1, keepdims=True)
            inverse = 1.0 / pivot
            new_row = jnp.where(lane_row == k, inverse, row * inverse)
            others = jnp.where(lane == k, 0.0, work) - column * new_row
            work_ref[...] = jnp.where(sublane == k, new_row, others)
            return carry

        lax.fori_loop(0, n, step, 0)
        x_ref[...] = work_ref[...] * by_column * by_row


def solve(right, matrix, inverse):
    first = dot(right, inverse)
    return first + dot(right - dot(first, matrix), inverse)


def place_of(axis):
    return lax.axis_index(axis)


def at_rows(block, rows):
    return pl.ds(pl.multiple_of(block * rows, rows), rows)


def load_kernel(time_hbm, species_hbm, half_ref, time_ref, species_ref, arrived):
    half = half_ref.shape[0]
    copies = [
        pltpu.make_async_copy(time_hbm.at[at_rows(place_of("space") % 2, half)], half_ref, arrived.at[0]),
        pltpu.make_async_copy(time_hbm, time_ref, arrived.at[1]),
        pltpu.make_async_copy(species_hbm, species_ref, arrived.at[2]),
    ]
    for copy in copies:
        copy.start()
    for copy in copies:
        copy.wait()


def space_kernel(tensor_ref, time_ref, species_ref, m_a_ref, side_ref):
    species = species_ref[...]
    species_count = species.shape[0]
    time_high, time_low = split(time_ref[...])
    weights = jnp.concatenate([time_high, time_low, time_low, time_high], axis=0)
    chunk = 8
    height = chunk * species_count
    for start in range(0, tensor_ref.shape[0], height):
        high, low = split(tensor_ref[start:start + height, :])
        side = dot_fast(jnp.concatenate([high, low, high, low], axis=1), weights)
        side = side.reshape(chunk, species_count, side.shape[1])
        at = start // species_count
        side_ref[at:at + chunk] = side
        m_a_ref[at:at + chunk, :] = jnp.sum(side * species[None], axis=1)


def pack_kernel(after_ref, *refs):
    *parts, out_ref = refs
    at = 0
    for part in parts:
        out_ref[at:at + part.shape[0], :] = part[...]
        at += part.shape[0]


def peers(count, paired):
    if not paired:
        return [], list(range(1, count))
    return [(j, j + 1) for j in range(1, count - 1, 2)], [count - 1]


def place_blocks(factor_ref, place, core, own_ref, mine_ref, partner_ref, paired):
    rows = own_ref.shape[0]
    half = rows // 2
    factor_ref[at_rows(place, rows), :] = own_ref[...]
    pairs, shared = peers(factor_ref.shape[0] // rows, paired)
    for i, (first, second) in enumerate(pairs):
        step = second - first
        taken = slice(i * rows, (i + 1) * rows)
        factor_ref[at_rows(jnp.bitwise_xor(place, first + core * step), rows), :] = mine_ref[taken, :]
        factor_ref[at_rows(jnp.bitwise_xor(place, second - core * step), rows), :] = partner_ref[taken, :]
    for i, step in enumerate(shared):
        start = len(pairs) * rows + i * half
        taken = slice(start, start + half)
        at = jnp.bitwise_xor(place, step) * 2
        factor_ref[at_rows(at + core, half), :] = mine_ref[taken, :]
        factor_ref[at_rows(at + 1 - core, half), :] = partner_ref[taken, :]


def sum_kernel(*refs):
    *parts, out_ref = refs
    out_ref[...] = tree_sum([part[...] for part in parts])


def time_side_kernel(species_count, raw_ref, tensor_ref, side_ref):
    rows = raw_ref.shape[0]
    raw_high, raw_low = split(raw_ref[...])
    weights = jnp.concatenate([raw_high, raw_high, raw_low, raw_low], axis=0)
    for p in range(species_count):
        high, low = split(tensor_ref[pl.ds(p, rows, stride=species_count), :])
        side_ref[p] = dot_fast(jnp.concatenate([high, low, high, low], axis=0), weights, ((0,), (0,)))


def first_inverse_kernel(species_ref, own_ref, mine_ref, partner_ref,
                         c_gram_ref, matrix_ref, inverse_ref, factor_ref, work_ref):
    place_blocks(factor_ref, place_of("tm"), place_of("space") % 2, own_ref, mine_ref, partner_ref, TIME_PAIR)
    c_gram = gram(factor_ref[...])
    c_gram_ref[...] = c_gram
    matrix = regularized(gram(species_ref[...]) * c_gram)
    matrix_ref[...] = matrix
    invert(matrix, inverse_ref, work_ref)


def space_solve_kernel(matrix_ref, inverse_ref, side_ref, *refs):
    *parts, raw_ref, keep_ref, send_ref, m_b_ref = refs
    core = place_of("space") % 2
    m_a = tree_sum([part[...] for part in parts])
    raw = solve(m_a, matrix_ref[...], inverse_ref[...])
    raw_ref[...] = raw
    rows = raw.shape[0]
    send_ref[:rows, :] = raw
    total = jnp.zeros(m_b_ref.shape, f32)
    for s in range(rows):
        total = total + side_ref[s] * raw_ref[pl.ds(s, 1), :]
    m_b_ref[...] = total
    half = keep_ref.shape[0]
    if MB_HALF:
        keep_ref[...] = m_b_ref[at_rows(core, half), :]
        send_ref[rows:, :] = m_b_ref[at_rows(1 - core, half), :]
    else:
        keep_ref[...] = total
        send_ref[rows:, :] = total


def chip_kernel(raw_ref, keep_ref, received_ref, block_ref, m_b_ref):
    core = place_of("space") % 2
    rows = raw_ref.shape[0]
    block_ref[at_rows(core, rows), :] = raw_ref[...]
    block_ref[at_rows(1 - core, rows), :] = received_ref[:rows, :]
    m_b_ref[...] = keep_ref[...] + received_ref[rows:, :]


def space_gram_kernel(c_gram_ref, own_ref, mine_ref, partner_ref,
                      a_gram_ref, matrix_ref, scale_ref, out_ref, factor_ref):
    place = place_of("space")
    place_blocks(factor_ref, place // 2, place % 2, own_ref, mine_ref, partner_ref, RAW_PAIR)
    raw_gram = gram(factor_ref[...])
    eye = eye_mask(raw_gram.shape[0])
    diagonal = jnp.where(eye, raw_gram, 0.0)
    total_rows = factor_ref.shape[0]
    by_column = lax.rsqrt(jnp.sum(diagonal, axis=0, keepdims=True) / total_rows + epsilon)
    by_row = lax.rsqrt(jnp.sum(diagonal, axis=1, keepdims=True) / total_rows + epsilon)
    scale_ref[...] = jnp.broadcast_to(by_column, scale_ref.shape)
    out_ref[...] = own_ref[at_rows(place % 2, out_ref.shape[0]), :] * by_column
    a_gram = raw_gram * by_column * by_row
    a_gram_ref[...] = a_gram
    matrix_ref[...] = regularized(a_gram * c_gram_ref[...])


def inverse_kernel(matrix_ref, inverse_ref, work_ref):
    invert(matrix_ref[...], inverse_ref, work_ref)


def species_kernel(scale_ref, matrix_ref, inverse_ref, side_ref, *refs):
    *parts, species_ref, out_ref, keep_ref, send_ref, scaled_ref = refs
    core = place_of("space") % 2
    scale = scale_ref[0:1, :]
    if MB_HALF:
        mine_ref, partner_ref = parts
        half = mine_ref.shape[0]
        scaled_ref[at_rows(core, half), :] = mine_ref[...]
        scaled_ref[at_rows(1 - core, half), :] = partner_ref[...]
        m_b = scaled_ref[...] * scale
    else:
        m_b = tree_sum([part[...] for part in parts]) * scale
    raw = solve(m_b, matrix_ref[...], inverse_ref[...])
    species = raw * lax.rsqrt(jnp.mean(raw * raw, axis=0, keepdims=True) + epsilon)
    species_ref[...] = species
    out_ref[...] = species
    scaled_ref[...] = species * scale
    half = keep_ref.shape[0]
    for ref, block in ((send_ref, 1 - core), (keep_ref, core)):
        total = jnp.zeros(ref.shape, f32)
        for p in range(side_ref.shape[0]):
            total = total + side_ref[p, at_rows(block, half), :] * scaled_ref[p:p + 1, :]
        ref[...] = total


def species_gram_kernel(a_gram_ref, species_ref, matrix_ref):
    matrix_ref[...] = regularized(a_gram_ref[...] * gram(species_ref[...]))


def time_solve_kernel(matrix_ref, inverse_ref, mine_ref, partner_ref, raw_ref, squares_ref, m_c_ref):
    core = place_of("space") % 2
    half = mine_ref.shape[0]
    m_c_ref[at_rows(core, half), :] = mine_ref[...]
    m_c_ref[at_rows(1 - core, half), :] = partner_ref[...]
    raw = solve(m_c_ref[...], matrix_ref[...], inverse_ref[...])
    raw_ref[...] = raw
    squares_ref[...] = jnp.broadcast_to(jnp.sum(raw * raw, axis=0, keepdims=True), squares_ref.shape)


def time_scale_kernel(total_steps, raw_ref, *refs):
    *parts, out_ref = refs
    squares = tree_sum([part[0:1, :] for part in parts])
    out_ref[...] = raw_ref[...] * lax.rsqrt(squares / total_steps + epsilon)


def exchange(value, axis, step, count):
    return lax.ppermute(value, axis, [(i, i ^ step) for i in range(count)])


def run(kernel, outs, micros, scratch=()):
    call = pl.pallas_call(
        kernel,
        out_shape=outs,
        out_specs=[vmem] * len(outs),
        scratch_shapes=list(scratch),
        cost_estimate=pl.CostEstimate(flops=int(micros * flops_per_micro), bytes_accessed=0, transcendentals=0),
        compiler_params=pltpu.CompilerParams(vmem_limit_bytes=vmem_limit),
    )

    def placed(*operands):
        return call(*[pltpu.with_memory_space_constraint(x, pltpu.VMEM) for x in operands])

    return placed


def on_device(tensor, species_factor, time_factor):
    row_count, species_count, step_count = tensor.shape
    rank = species_factor.shape[1]
    devices = lax.axis_size("space")
    blocks = lax.axis_size("tm")
    chips = devices // 2
    total_rows = row_count * devices
    total_steps = step_count * blocks

    def local(*dims):
        return pltpu.VMEM(dims, f32)

    def result(*dims):
        return jax.ShapeDtypeStruct(dims, f32)

    square = local(rank, rank)

    def over_time(value):
        return [value] + [exchange(value, "tm", j, blocks) for j in range(1, blocks)]

    def over_chips(value):
        return [value] + [exchange(value, "space", 2 * j, devices) for j in range(1, chips)]

    def to_partner(value):
        return exchange(value, "space", 1, devices)

    def block_from(block, half, axis):
        pairs, shared = peers(blocks, TIME_PAIR) if axis == "tm" else peers(chips, RAW_PAIR)
        received = []
        for steps in pairs:
            if axis == "tm":
                turns = [
                    (s * blocks + t, s * blocks + (t ^ steps[s % 2])) for s in range(devices) for t in range(blocks)
                ]
                received.append(lax.ppermute(block, ("space", "tm"), turns))
            else:
                turns = [(s, s ^ (2 * steps[s % 2])) for s in range(devices)]
                received.append(lax.ppermute(block, "space", turns))
        for j in shared:
            step, count = (j, blocks) if axis == "tm" else (2 * j, devices)
            received.append(exchange(half, axis, step, count))
        return received

    def pack(after, parts):
        return run(pack_kernel, [local(sum(part.shape[0] for part in parts), rank)], 0.3)(after, *parts)[0]

    def add(parts):
        return run(sum_kernel, [local(*parts[0].shape)], 0.3)(*parts)[0]

    half_steps = step_count // 2
    half_species = species_count // 2 if MB_HALF else species_count

    outside = pl.BlockSpec(memory_space=pltpu.HBM)
    time_half, time_here, species_here = pl.pallas_call(
        load_kernel,
        in_specs=[outside] * 2,
        out_specs=[vmem] * 3,
        out_shape=[local(half_steps, rank), local(step_count, rank), local(species_count, rank)],
        scratch_shapes=[pltpu.SemaphoreType.DMA((3,))],
        cost_estimate=pl.CostEstimate(flops=int(10 * flops_per_micro), bytes_accessed=10**8, transcendentals=0),
        compiler_params=pltpu.CompilerParams(vmem_limit_bytes=vmem_limit),
        name="load_factors",
    )(*[pltpu.with_memory_space_constraint(x, pltpu.HBM) for x in (time_factor, species_factor)])
    received = block_from(time_here, time_half, "tm")
    m_a, side = run(
        space_kernel, [local(row_count, rank), local(row_count, species_count, rank)], 2
    )(tensor.reshape(row_count * species_count, step_count), time_here, species_here)
    m_a_parts = over_time(m_a)

    mine = pack(m_a, received)
    partner = to_partner(mine)
    c_gram, matrix, inverse = run(
        first_inverse_kernel, [square] * 3, 2, [local(total_steps, rank), square]
    )(species_here, time_here, mine, partner)

    raw, keep, send = run(
        space_solve_kernel,
        [local(row_count, rank), local(half_species, rank), local(row_count + half_species, rank)],
        1,
        [local(species_count, rank)],
    )(matrix, inverse, side, *m_a_parts)
    received = to_partner(send)
    (time_side,) = run(
        lambda *refs: time_side_kernel(species_count, *refs), [local(species_count, step_count, rank)], 2
    )(raw, tensor.reshape(row_count * species_count, step_count))
    chip_block, m_b = run(chip_kernel, [local(2 * row_count, rank), local(half_species, rank)], 0.3)(
        raw, keep, received
    )
    m_b_parts = over_time(m_b)
    raw_blocks = block_from(chip_block, raw, "space")
    m_b_parts = over_chips(add(m_b_parts))
    mine = pack(m_b, raw_blocks)
    partner = to_partner(mine)
    if MB_HALF:
        m_b = add(m_b_parts)
        m_b_parts = [m_b, to_partner(m_b)]
    a_gram, matrix, scale, space_out = run(
        space_gram_kernel, [square, square, local(8, rank), result(row_count, rank)], 1.5, [local(total_rows, rank)]
    )(c_gram, chip_block, mine, partner)
    (inverse,) = run(inverse_kernel, [square], 1, [square])(matrix)

    species, species_out, m_c_keep, m_c_send = run(
        species_kernel,
        [local(species_count, rank), result(species_count, rank), local(half_steps, rank), local(half_steps, rank)],
        1.5,
        [local(species_count, rank)],
    )(scale, matrix, inverse, time_side, *m_b_parts)

    m_c_received = to_partner(m_c_send)
    (matrix,) = run(species_gram_kernel, [square], 0.5)(a_gram, species)
    m_c_parts = over_chips(add([m_c_keep, m_c_received]))
    (inverse,) = run(inverse_kernel, [square], 1, [square])(matrix)
    m_c = add(m_c_parts)
    m_c_partner = to_partner(m_c)
    raw_time, squares = run(
        time_solve_kernel, [local(step_count, rank), local(8, rank)], 1, [local(step_count, rank)]
    )(matrix, inverse, m_c, m_c_partner)

    squares = over_time(squares)
    (time_out,) = run(
        lambda *refs: time_scale_kernel(total_steps, *refs), [result(step_count, rank)], 0.5
    )(raw_time, *squares)
    return (space_out, species_out, time_out)


def solution(mesh):
    placed = (P("space", None, "tm"), P(), P("tm", None))
    return jax.shard_map(
        on_device,
        mesh=mesh,
        in_specs=placed,
        out_specs=(P("space", None), P(), P("tm", None)),
        check_vma=False,
    )
```

time: 105 us -> 94.8 us (0.903)
  waiting for transfers between devices: 22.2 us -> 16 us
  Pallas kernels: 50.1 us -> 48.4 us
    ppermute x26 -> x23, waiting for transfers between devices: 22.2 us -> 12.2 us  [exchange(): return lax.ppermute(value, axis, [(i, i ^ step) for i in range(count)])]
    ppermute x0 -> x2, waiting for transfers between devices: none -> 3.76 us  [the longest x1 3.76 us: block_from(): received.append(lax.ppermute(block, ('space', 'tm'), turns))]
    pallas_call x1, Pallas kernels: 4.57 us -> 1.12 us  [on_device(): pl.pallas_call(load_kernel, in_specs=[outside] * 2, out_specs=[vmem] * 3,...]
    ppermute x26 -> x23, starting transfers between devices: 30.4 us -> 27.9 us  [exchange(): return lax.ppermute(value, axis, [(i, i ^ step) for i in range(count)])]
    pallas_call x16 -> x18, Pallas kernels: 45.5 us -> 47.3 us  [placed(): call(*[pltpu.with_memory_space_constraint(x, pltpu.VMEM) for x in operands])]
    ppermute x0 -> x2, starting transfers between devices: none -> 1.57 us  [the longest x1 1.56 us: block_from(): received.append(lax.ppermute(block, 'space', turns))]
  transfers between devices with their start and end apart: 26 -> 25, of which waited for: 18 -> 13; matrix products, arithmetic and copies ran while one was open for 0% -> 0% of each run, Pallas kernels for 43% -> 45%
where the time goes in v1:
time: 94.8 us; the launch traced here: 94.7 us
  Pallas kernels  48.4 us (51%)
  starting transfers between devices  29.4 us (31%)
  waiting for transfers between devices  16 us (17%)
    pallas_call x18, Pallas kernels, placed(): call(*[pltpu.with_memory_space_constraint(x, pltpu.VMEM) for x in operands])  47.3 us
    ppermute x23, starting transfers between devices, exchange(): return lax.ppermute(value, axis, [(i, i ^ step) for i in range(count)])  27.9 us
    ppermute x23, waiting for transfers between devices, exchange(): return lax.ppermute(value, axis, [(i, i ^ step) for i in range(count)])  12.2 us
    ppermute x1, waiting for transfers between devices, block_from(): received.append(lax.ppermute(block, ('space', 'tm'), turns))  3.76 us
  transfers between devices with their start and end apart: 25, of which 13 were waited for; matrix products, arithmetic and copies ran while one was open for 0% of the time, Pallas kernels for 45%

profile of v1, /device:TPU:0, one launch (start us, length us, event | category | flops | bytes accessed | tf_op | source)
XLA Modules:
  0.0 94.7 jit_solution(7834975363143583399)
XLA Ops:
  0.6 1.1 %load_factors.1 = (f32[64,256]{1,0:T(8,128)S(1)}, f32[128,256]{1,0:T(8,128)S(1)}, f32[64,256]{1,0:T(8,128)S(1)}) custom-call(f32[128,256]{1,0:T(8,128)} %time_hbm.1, f32[64,256]{1,0:T(8,128)} %species_hbm.1), custom_call_target="tpu_custom_call" | custom-call | flops 10000000000 | bytes 100000000 | tf_op jit(solution)/shard_map/load_factors/pallas_call | solution.py:365
  1.8 5.1 %collective-permute-start.1 = (f32[64,256]{1,0:T(8,128)S(1)}, f32[64,256]{1,0:T(8,128)S(1)}, u32[]{:S(2)}, u32[]{:S(2)}) collective-permute-start(f32[64,256]{1,0:T(8,128)S(1)} %get-tuple-element.29), channel_id=1, source_target_pairs={{0,3},{1,2},{2,1},{3,0},{4,7},{5,6},{6,5},{7,4},{8,11},{9,10},{10,... | collective-permute-start | bytes 196616 | tf_op jit(solution)/shard_map/ppermute | solution.py:293
  6.9 1.3 %shard_map.58 = (f32[64,256]{1,0:T(8,128)S(1)}, f32[64,64,256]{2,1,0:T(8,128)S(1)}) custom-call(f32[4096,128]{1,0:T(8,128)S(1)} %bitcast.1, f32[128,256]{1,0:T(8,128)S(1)} %get-tuple-element.27.time_ref.own_ref, f32[64,256]{1,0:T(8,128)S(1)} %get-tuple-element.26.species_ref), custom_call_target="tpu_custom_call" | custom-call | flops 2000000000 | tf_op jit(solution)/shard_map/pallas_call | solution.py:307
  8.3 1.1 %collective-permute-done.1.refs_1_ = f32[64,256]{1,0:T(8,128)S(1)} collective-permute-done((f32[64,256]{1,0:T(8,128)S(1)}, f32[64,256]{1,0:T(8,128)S(1)}, u32[]{:S(2)}, u32[]{:S(2)}) %collective-permute-start.1) | collective-permute-done | bytes 65568 | tf_op jit(solution)/shard_map/ppermute | solution.py:293
  9.4 3.8 %collective-permute-done.refs_0_ = f32[128,256]{1,0:T(8,128)S(1)} collective-permute-done((f32[128,256]{1,0:T(8,128)S(1)}, f32[128,256]{1,0:T(8,128)S(1)}, u32[]{:S(2)}, u32[]{:S(2)}) %collective-permute-start) | collective-permute-done | bytes 131104 | tf_op jit(solution)/shard_map/ppermute | solution.py:346
  13.2 0.1 collective-permute-start.2
  13.3 1.9 %collective-permute-start.5 = (f32[64,256]{1,0:T(8,128)S(1)}, f32[64,256]{1,0:T(8,128)S(1)}, u32[]{:S(2)}, u32[]{:S(2)}) collective-permute-start(f32[64,256]{1,0:T(8,128)S(1)} %get-tuple-element.28.after_ref.refs_0_), channel_id=1, source_target_pairs={{0,3},{1,2},{2,1},{3,0},{4,7},{5,6},{6,5},{7,4},{8,11},{9,10},{10,... | collective-permute-start | bytes 196616 | tf_op jit(solution)/shard_map/ppermute | solution.py:293
  15.1 0.1 collective-permute-start.4
  15.2 2.5 %collective-permute-start.3 = (f32[64,256]{1,0:T(8,128)S(1)}, f32[64,256]{1,0:T(8,128)S(1)}, u32[]{:S(2)}, u32[]{:S(2)}) collective-permute-start(f32[64,256]{1,0:T(8,128)S(1)} %get-tuple-element.28.after_ref.refs_0_), channel_id=1, source_target_pairs={{0,1},{1,0},{2,3},{3,2},{4,5},{5,4},{6,7},{7,6},{8,9},{9,8},{10,11... | collective-permute-start | bytes 196616 | tf_op jit(solution)/shard_map/ppermute | solution.py:293
  17.7 35.9 %shard_map.60 = (f32[256,256]{1,0:T(8,128)S(1)}, f32[256,256]{1,0:T(8,128)S(1)}, f32[256,256]{1,0:T(8,128)S(1)}) custom-call(f32[64,256]{1,0:T(8,128)S(1)} %get-tuple-element.26.species_ref, f32[128,256]{1,0:T(8,128)S(1)} %get-tuple-element.27.time_ref.own_ref, f32[192,256]{1,0:T(8,128)S(1)} %shard_map.59.mine_ref, ...), custom_call_target="tpu_custom_call" | custom-call | flops 2000000000 | tf_op jit(solution)/shard_map/pallas_call | solution.py:307
  53.6 1.1 %shard_map.61 = (f32[64,256]{1,0:T(8,128)S(1)}, f32[32,256]{1,0:T(8,128)S(1)}, f32[96,256]{1,0:T(8,128)S(1)}) custom-call(f32[256,256]{1,0:T(8,128)S(1)} %get-tuple-element.31.matrix_ref, f32[256,256]{1,0:T(8,128)S(1)} %get-tuple-element.32.inverse_ref, f32[64,64,256]{2,1,0:T(8,128)S(1)} %get-tuple-element.33.side_ref, ...), custom_call_target="tpu_custom_call" | custom-call | flops 1000000000 | tf_op jit(solution)/shard_map/pallas_call | solution.py:307
  54.8 0.1 collective-permute-start.6
  54.9 1.3 %collective-permute-done.6.received_ref = f32[96,256]{1,0:T(8,128)S(1)} collective-permute-done((f32[96,256]{1,0:T(8,128)S(1)}, f32[96,256]{1,0:T(8,128)S(1)}, u32[]{:S(2)}, u32[]{:S(2)}) %collective-permute-start.6) | collective-permute-done | bytes 98336 | tf_op jit(solution)/shard_map/ppermute | solution.py:293
  56.2 1.6 %collective-permute-start.7 = (f32[128,256]{1,0:T(8,128)S(1)}, f32[128,256]{1,0:T(8,128)S(1)}, u32[]{:S(2)}, u32[]{:S(2)}) collective-permute-start(f32[128,256]{1,0:T(8,128)S(1)} %get-tuple-element.37.own_ref), channel_id=1, source_target_pairs={{0,8},{4,20},{8,0},{12,28},{16,24},{20,4},{24,16},{28,12},{1,9},{5... | collective-permute-start | bytes 393224 | tf_op jit(solution)/shard_map/ppermute | solution.py:349
  57.8 1.5 %collective-permute-start.8 = (f32[64,256]{1,0:T(8,128)S(1)}, f32[64,256]{1,0:T(8,128)S(1)}, u32[]{:S(2)}, u32[]{:S(2)}) collective-permute-start(f32[64,256]{1,0:T(8,128)S(1)} %get-tuple-element.34.raw_ref.refs_0_), channel_id=1, source_target_pairs={{0,24},{4,28},{8,16},{12,20},{16,8},{20,12},{24,0},{28,4},{1,25},{... | collective-permute-start | bytes 196616 | tf_op jit(solution)/shard_map/ppermute | solution.py:293
  59.2 1.8 %collective-permute-start.12 = (f32[32,256]{1,0:T(8,128)S(1)}, f32[32,256]{1,0:T(8,128)S(1)}, u32[]{:S(2)}, u32[]{:S(2)}) collective-permute-start(f32[32,256]{1,0:T(8,128)S(1)} %get-tuple-element.38.after_ref.refs_0_), channel_id=1, source_target_pairs={{0,3},{1,2},{2,1},{3,0},{4,7},{5,6},{6,5},{7,4},{8,11},{9,10},{10,... | collective-permute-start | bytes 98312 | tf_op jit(solution)/shard_map/ppermute | solution.py:293
  61.1 2.6 %collective-permute-start.10 = (f32[32,256]{1,0:T(8,128)S(1)}, f32[32,256]{1,0:T(8,128)S(1)}, u32[]{:S(2)}, u32[]{:S(2)}) collective-permute-start(f32[32,256]{1,0:T(8,128)S(1)} %get-tuple-element.38.after_ref.refs_0_), channel_id=1, source_target_pairs={{0,1},{1,0},{2,3},{3,2},{4,5},{5,4},{6,7},{7,6},{8,9},{9,8},{10,11... | collective-permute-start | bytes 98312 | tf_op jit(solution)/shard_map/ppermute | solution.py:293
  63.6 1.3 %collective-permute-done.12.refs_3_ = f32[32,256]{1,0:T(8,128)S(1)} collective-permute-done((f32[32,256]{1,0:T(8,128)S(1)}, f32[32,256]{1,0:T(8,128)S(1)}, u32[]{:S(2)}, u32[]{:S(2)}) %collective-permute-start.12) | collective-permute-done | bytes 32800 | tf_op jit(solution)/shard_map/ppermute | solution.py:293
  65.0 1.0 %collective-permute-done.11.refs_2_ = f32[32,256]{1,0:T(8,128)S(1)} collective-permute-done((f32[32,256]{1,0:T(8,128)S(1)}, f32[32,256]{1,0:T(8,128)S(1)}, u32[]{:S(2)}, u32[]{:S(2)}) %collective-permute-start.11) | collective-permute-done | bytes 32800 | tf_op jit(solution)/shard_map/ppermute | solution.py:293
  65.9 1.5 %collective-permute-start.15 = (f32[32,256]{1,0:T(8,128)S(1)}, f32[32,256]{1,0:T(8,128)S(1)}, u32[]{:S(2)}, u32[]{:S(2)}) collective-permute-start(f32[32,256]{1,0:T(8,128)S(1)} %shard_map.67.refs_0_), channel_id=1, source_target_pairs={{0,24},{4,28},{8,16},{12,20},{16,8},{20,12},{24,0},{28,4},{1,25},{... | collective-permute-start | bytes 98312 | tf_op jit(solution)/shard_map/ppermute | solution.py:293
  67.4 1.5 %collective-permute-start.14 = (f32[32,256]{1,0:T(8,128)S(1)}, f32[32,256]{1,0:T(8,128)S(1)}, u32[]{:S(2)}, u32[]{:S(2)}) collective-permute-start(f32[32,256]{1,0:T(8,128)S(1)} %shard_map.67.refs_0_), channel_id=1, source_target_pairs={{0,16},{4,20},{8,24},{12,28},{16,0},{20,4},{24,8},{28,12},{1,17},{... | collective-permute-start | bytes 98312 | tf_op jit(solution)/shard_map/ppermute | solution.py:293
  68.9 0.6 collective-permute-start.13
  69.5 0.1 collective-permute-start.9
  69.6 1.8 %shard_map.66.side_ref = f32[64,128,256]{2,1,0:T(8,128)S(1)} custom-call(f32[64,256]{1,0:T(8,128)S(1)} %get-tuple-element.34.raw_ref.refs_0_, f32[4096,128]{1,0:T(8,128)S(1)} %bitcast.2), custom_call_target="tpu_custom_call" | custom-call | flops 2000000000 | tf_op jit(solution)/shard_map/pallas_call | solution.py:307
  71.4 1.5 %collective-permute-done.13.refs_1_ = f32[32,256]{1,0:T(8,128)S(1)} collective-permute-done((f32[32,256]{1,0:T(8,128)S(1)}, f32[32,256]{1,0:T(8,128)S(1)}, u32[]{:S(2)}, u32[]{:S(2)}) %collective-permute-start.13) | collective-permute-done | bytes 32800 | tf_op jit(solution)/shard_map/ppermute | solution.py:293
  72.8 0.1 collective-permute-start.16
  72.9 1.4 %shard_map.64 = (f32[256,256]{1,0:T(8,128)S(1)}, f32[256,256]{1,0:T(8,128)S(1)}, f32[8,256]{1,0:T(8,128)S(1)}, f32[64,256]{1,0:T(8,128)}) custom-call(f32[256,256]{1,0:T(8,128)S(1)} %get-tuple-element.30.c_gram_ref, f32[128,256]{1,0:T(8,128)S(1)} %get-tuple-element.37.own_ref, f32[192,256]{1,0:T(8,128)S(1)} %shard_map.63.mine_ref, ...), custom_call_target="tpu_custom_call" | custom-call | flops 1500000000 | tf_op jit(solution)/shard_map/pallas_call | solution.py:307
  74.4 0.7 shard_map.65.inverse_ref
  75.1 2.1 %shard_map.69 = (f32[64,256]{1,0:T(8,128)S(1)}, f32[64,256]{1,0:T(8,128)}, f32[64,256]{1,0:T(8,128)S(1)}, f32[64,256]{1,0:T(8,128)S(1)}) custom-call(f32[8,256]{1,0:T(8,128)S(1)} %get-tuple-element.40.scale_ref, f32[256,256]{1,0:T(8,128)S(1)} %get-tuple-element.41.matrix_ref, f32[256,256]{1,0:T(8,128)S(1)} %shard_map.65.inverse_ref, ...), custom_call_target="tpu_custom_call" | custom-call | flops 1500000000 | tf_op jit(solution)/shard_map/pallas_call | solution.py:307
  77.2 0.5 collective-permute-start.17
  77.6 0.9 collective-permute-done.17.refs_1_
  78.6 1.0 %collective-permute-start.20 = (f32[64,256]{1,0:T(8,128)S(1)}, f32[64,256]{1,0:T(8,128)S(1)}, u32[]{:S(2)}, u32[]{:S(2)}) collective-permute-start(f32[64,256]{1,0:T(8,128)S(1)} %shard_map.72.refs_0_), channel_id=1, source_target_pairs={{0,24},{4,28},{8,16},{12,20},{16,8},{20,12},{24,0},{28,4},{1,25},{... | collective-permute-start | bytes 196616 | tf_op jit(solution)/shard_map/ppermute | solution.py:293
  79.5 1.1 %collective-permute-start.19 = (f32[64,256]{1,0:T(8,128)S(1)}, f32[64,256]{1,0:T(8,128)S(1)}, u32[]{:S(2)}, u32[]{:S(2)}) collective-permute-start(f32[64,256]{1,0:T(8,128)S(1)} %shard_map.72.refs_0_), channel_id=1, source_target_pairs={{0,16},{4,20},{8,24},{12,28},{16,0},{20,4},{24,8},{28,12},{1,17},{... | collective-permute-start | bytes 196616 | tf_op jit(solution)/shard_map/ppermute | solution.py:293
  80.6 1.5 %collective-permute-start.18 = (f32[64,256]{1,0:T(8,128)S(1)}, f32[64,256]{1,0:T(8,128)S(1)}, u32[]{:S(2)}, u32[]{:S(2)}) collective-permute-start(f32[64,256]{1,0:T(8,128)S(1)} %shard_map.72.refs_0_), channel_id=1, source_target_pairs={{0,8},{4,12},{8,0},{12,4},{16,24},{20,28},{24,16},{28,20},{1,9},{5... | collective-permute-start | bytes 196616 | tf_op jit(solution)/shard_map/ppermute | solution.py:293
  82.1 0.6 shard_map.70.matrix_ref
  82.7 1.7 %collective-permute-done.20.refs_3_ = f32[64,256]{1,0:T(8,128)S(1)} collective-permute-done((f32[64,256]{1,0:T(8,128)S(1)}, f32[64,256]{1,0:T(8,128)S(1)}, u32[]{:S(2)}, u32[]{:S(2)}) %collective-permute-start.20) | collective-permute-done | bytes 65568 | tf_op jit(solution)/shard_map/ppermute | solution.py:293
  84.4 0.6 collective-permute-done.19.refs_2_
  85.0 0.1 collective-permute-start.21
  85.1 0.7 shard_map.71.inverse_ref
  85.8 0.5 collective-permute-done.21.partner_ref
  86.4 0.9 shard_map.74
  87.3 1.9 %collective-permute-start.24 = (f32[8,256]{1,0:T(8,128)S(1)}, f32[8,256]{1,0:T(8,128)S(1)}, u32[]{:S(2)}, u32[]{:S(2)}) collective-permute-start(f32[8,256]{1,0:T(8,128)S(1)} %get-tuple-element.48.refs_1_), channel_id=1, source_target_pairs={{0,3},{1,2},{2,1},{3,0},{4,7},{5,6},{6,5},{7,4},{8,11},{9,10},{10,... | collective-permute-start | bytes 24584 | tf_op jit(solution)/shard_map/ppermute | solution.py:293
  89.2 1.1 %collective-permute-start.23 = (f32[8,256]{1,0:T(8,128)S(1)}, f32[8,256]{1,0:T(8,128)S(1)}, u32[]{:S(2)}, u32[]{:S(2)}) collective-permute-start(f32[8,256]{1,0:T(8,128)S(1)} %get-tuple-element.48.refs_1_), channel_id=1, source_target_pairs={{0,2},{1,3},{2,0},{3,1},{4,6},{5,7},{6,4},{7,5},{8,10},{9,11},{10,... | collective-permute-start | bytes 24584 | tf_op jit(solution)/shard_map/ppermute | solution.py:293
  90.3 1.4 %collective-permute-start.22 = (f32[8,256]{1,0:T(8,128)S(1)}, f32[8,256]{1,0:T(8,128)S(1)}, u32[]{:S(2)}, u32[]{:S(2)}) collective-permute-start(f32[8,256]{1,0:T(8,128)S(1)} %get-tuple-element.48.refs_1_), channel_id=1, source_target_pairs={{0,1},{1,0},{2,3},{3,2},{4,5},{5,4},{6,7},{7,6},{8,9},{9,8},{10,11... | collective-permute-start | bytes 24584 | tf_op jit(solution)/shard_map/ppermute | solution.py:293
  91.7 1.1 %collective-permute-done.24.refs_4_ = f32[8,256]{1,0:T(8,128)S(1)} collective-permute-done((f32[8,256]{1,0:T(8,128)S(1)}, f32[8,256]{1,0:T(8,128)S(1)}, u32[]{:S(2)}, u32[]{:S(2)}) %collective-permute-start.24) | collective-permute-done | bytes 8224 | tf_op jit(solution)/shard_map/ppermute | solution.py:293
  92.8 0.9 collective-permute-done.23.refs_3_
  93.8 0.2 collective-permute-done.22.refs_2_
  94.0 0.7 shard_map.75
  (23 shorter events, 0.1 us)
Async XLA Ops:
  0.6 6.3 %copy-start = (f32[64,64,128]{2,1,0:T(8,128)S(1)}, f32[64,64,128]{2,1,0:T(8,128)}, u32[]{:S(2)}) copy-start(f32[64,64,128]{2,1,0:T(8,128)} %param.3) | copy-start | bytes 6291460
  1.8 7.6 %collective-permute-start.1 = (f32[64,256]{1,0:T(8,128)S(1)}, f32[64,256]{1,0:T(8,128)S(1)}, u32[]{:S(2)}, u32[]{:S(2)}) collective-permute-start(f32[64,256]{1,0:T(8,128)S(1)} %get-tuple-element.29), channel_id=1, source_target_pairs={{0,3},{1,2},{2,1},{3,0},{4,7},{5,6},{6,5},{7,4},{8,11},{9,10},{10,... | collective-permute-start | bytes 196616 | tf_op jit(solution)/shard_map/ppermute | solution.py:293
  6.9 6.2 %collective-permute-start = (f32[128,256]{1,0:T(8,128)S(1)}, f32[128,256]{1,0:T(8,128)S(1)}, u32[]{:S(2)}, u32[]{:S(2)}) collective-permute-start(f32[128,256]{1,0:T(8,128)S(1)} %get-tuple-element.27.time_ref.own_ref), channel_id=1, source_target_pairs={{0,1},{1,0},{2,3},{3,2},{4,6},{5,7},{6,4},{7,5},{8,9},{9,8},{10,11... | collective-permute-start | bytes 393224 | tf_op jit(solution)/shard_map/ppermute | solution.py:346
  13.2 4.5 %collective-permute-start.2 = (f32[192,256]{1,0:T(8,128)S(1)}, f32[192,256]{1,0:T(8,128)S(1)}, u32[]{:S(2)}, u32[]{:S(2)}) collective-permute-start(f32[192,256]{1,0:T(8,128)S(1)} %shard_map.59.mine_ref), channel_id=1, source_target_pairs={{0,4},{4,0},{8,12},{12,8},{16,20},{20,16},{24,28},{28,24},{1,5},{5... | collective-permute-start | bytes 589832 | tf_op jit(solution)/shard_map/ppermute | solution.py:293
  13.3 40.4 %collective-permute-start.5 = (f32[64,256]{1,0:T(8,128)S(1)}, f32[64,256]{1,0:T(8,128)S(1)}, u32[]{:S(2)}, u32[]{:S(2)}) collective-permute-start(f32[64,256]{1,0:T(8,128)S(1)} %get-tuple-element.28.after_ref.refs_0_), channel_id=1, source_target_pairs={{0,3},{1,2},{2,1},{3,0},{4,7},{5,6},{6,5},{7,4},{8,11},{9,10},{10,... | collective-permute-start | bytes 196616 | tf_op jit(solution)/shard_map/ppermute | solution.py:293
  15.1 38.5 %collective-permute-start.4 = (f32[64,256]{1,0:T(8,128)S(1)}, f32[64,256]{1,0:T(8,128)S(1)}, u32[]{:S(2)}, u32[]{:S(2)}) collective-permute-start(f32[64,256]{1,0:T(8,128)S(1)} %get-tuple-element.28.after_ref.refs_0_), channel_id=1, source_target_pairs={{0,2},{1,3},{2,0},{3,1},{4,6},{5,7},{6,4},{7,5},{8,10},{9,11},{10,... | collective-permute-start | bytes 196616 | tf_op jit(solution)/shard_map/ppermute | solution.py:293
  15.2 38.4 %collective-permute-start.3 = (f32[64,256]{1,0:T(8,128)S(1)}, f32[64,256]{1,0:T(8,128)S(1)}, u32[]{:S(2)}, u32[]{:S(2)}) collective-permute-start(f32[64,256]{1,0:T(8,128)S(1)} %get-tuple-element.28.after_ref.refs_0_), channel_id=1, source_target_pairs={{0,1},{1,0},{2,3},{3,2},{4,5},{5,4},{6,7},{7,6},{8,9},{9,8},{10,11... | collective-permute-start | bytes 196616 | tf_op jit(solution)/shard_map/ppermute | solution.py:293
  54.8 1.4 %collective-permute-start.6 = (f32[96,256]{1,0:T(8,128)S(1)}, f32[96,256]{1,0:T(8,128)S(1)}, u32[]{:S(2)}, u32[]{:S(2)}) collective-permute-start(f32[96,256]{1,0:T(8,128)S(1)} %get-tuple-element.36), channel_id=1, source_target_pairs={{0,4},{4,0},{8,12},{12,8},{16,20},{20,16},{24,28},{28,24},{1,5},{5... | collective-permute-start | bytes 294920 | tf_op jit(solution)/shard_map/ppermute | solution.py:293
  56.2 13.3 %collective-permute-start.7 = (f32[128,256]{1,0:T(8,128)S(1)}, f32[128,256]{1,0:T(8,128)S(1)}, u32[]{:S(2)}, u32[]{:S(2)}) collective-permute-start(f32[128,256]{1,0:T(8,128)S(1)} %get-tuple-element.37.own_ref), channel_id=1, source_target_pairs={{0,8},{4,20},{8,0},{12,28},{16,24},{20,4},{24,16},{28,12},{1,9},{5... | collective-permute-start | bytes 393224 | tf_op jit(solution)/shard_map/ppermute | solution.py:349
  57.8 11.7 %collective-permute-start.8 = (f32[64,256]{1,0:T(8,128)S(1)}, f32[64,256]{1,0:T(8,128)S(1)}, u32[]{:S(2)}, u32[]{:S(2)}) collective-permute-start(f32[64,256]{1,0:T(8,128)S(1)} %get-tuple-element.34.raw_ref.refs_0_), channel_id=1, source_target_pairs={{0,24},{4,28},{8,16},{12,20},{16,8},{20,12},{24,0},{28,4},{1,25},{... | collective-permute-start | bytes 196616 | tf_op jit(solution)/shard_map/ppermute | solution.py:293
  59.2 5.7 %collective-permute-start.12 = (f32[32,256]{1,0:T(8,128)S(1)}, f32[32,256]{1,0:T(8,128)S(1)}, u32[]{:S(2)}, u32[]{:S(2)}) collective-permute-start(f32[32,256]{1,0:T(8,128)S(1)} %get-tuple-element.38.after_ref.refs_0_), channel_id=1, source_target_pairs={{0,3},{1,2},{2,1},{3,0},{4,7},{5,6},{6,5},{7,4},{8,11},{9,10},{10,... | collective-permute-start | bytes 98312 | tf_op jit(solution)/shard_map/ppermute | solution.py:293
  61.1 4.8 %collective-permute-start.11 = (f32[32,256]{1,0:T(8,128)S(1)}, f32[32,256]{1,0:T(8,128)S(1)}, u32[]{:S(2)}, u32[]{:S(2)}) collective-permute-start(f32[32,256]{1,0:T(8,128)S(1)} %get-tuple-element.38.after_ref.refs_0_), channel_id=1, source_target_pairs={{0,2},{1,3},{2,0},{3,1},{4,6},{5,7},{6,4},{7,5},{8,10},{9,11},{10,... | collective-permute-start | bytes 98312 | tf_op jit(solution)/shard_map/ppermute | solution.py:293
  61.1 4.8 %collective-permute-start.10 = (f32[32,256]{1,0:T(8,128)S(1)}, f32[32,256]{1,0:T(8,128)S(1)}, u32[]{:S(2)}, u32[]{:S(2)}) collective-permute-start(f32[32,256]{1,0:T(8,128)S(1)} %get-tuple-element.38.after_ref.refs_0_), channel_id=1, source_target_pairs={{0,1},{1,0},{2,3},{3,2},{4,5},{5,4},{6,7},{7,6},{8,9},{9,8},{10,11... | collective-permute-start | bytes 98312 | tf_op jit(solution)/shard_map/ppermute | solution.py:293
  65.9 5.4 %collective-permute-start.15 = (f32[32,256]{1,0:T(8,128)S(1)}, f32[32,256]{1,0:T(8,128)S(1)}, u32[]{:S(2)}, u32[]{:S(2)}) collective-permute-start(f32[32,256]{1,0:T(8,128)S(1)} %shard_map.67.refs_0_), channel_id=1, source_target_pairs={{0,24},{4,28},{8,16},{12,20},{16,8},{20,12},{24,0},{28,4},{1,25},{... | collective-permute-start | bytes 98312 | tf_op jit(solution)/shard_map/ppermute | solution.py:293
  67.4 4.0 %collective-permute-start.14 = (f32[32,256]{1,0:T(8,128)S(1)}, f32[32,256]{1,0:T(8,128)S(1)}, u32[]{:S(2)}, u32[]{:S(2)}) collective-permute-start(f32[32,256]{1,0:T(8,128)S(1)} %shard_map.67.refs_0_), channel_id=1, source_target_pairs={{0,16},{4,20},{8,24},{12,28},{16,0},{20,4},{24,8},{28,12},{1,17},{... | collective-permute-start | bytes 98312 | tf_op jit(solution)/shard_map/ppermute | solution.py:293
  68.9 3.9 %collective-permute-start.13 = (f32[32,256]{1,0:T(8,128)S(1)}, f32[32,256]{1,0:T(8,128)S(1)}, u32[]{:S(2)}, u32[]{:S(2)}) collective-permute-start(f32[32,256]{1,0:T(8,128)S(1)} %shard_map.67.refs_0_), channel_id=1, source_target_pairs={{0,8},{4,12},{8,0},{12,4},{16,24},{20,28},{24,16},{28,20},{1,9},{5... | collective-permute-start | bytes 98312 | tf_op jit(solution)/shard_map/ppermute | solution.py:293
  69.5 3.4 %collective-permute-start.9 = (f32[192,256]{1,0:T(8,128)S(1)}, f32[192,256]{1,0:T(8,128)S(1)}, u32[]{:S(2)}, u32[]{:S(2)}) collective-permute-start(f32[192,256]{1,0:T(8,128)S(1)} %shard_map.63.mine_ref), channel_id=1, source_target_pairs={{0,4},{4,0},{8,12},{12,8},{16,20},{20,16},{24,28},{28,24},{1,5},{5... | collective-permute-start | bytes 589832 | tf_op jit(solution)/shard_map/ppermute | solution.py:293
  72.8 2.2 %collective-permute-start.16 = (f32[32,256]{1,0:T(8,128)S(1)}, f32[32,256]{1,0:T(8,128)S(1)}, u32[]{:S(2)}, u32[]{:S(2)}) collective-permute-start(f32[32,256]{1,0:T(8,128)S(1)} %shard_map.68.refs_0_), channel_id=1, source_target_pairs={{0,4},{4,0},{8,12},{12,8},{16,20},{20,16},{24,28},{28,24},{1,5},{5... | collective-permute-start | bytes 98312 | tf_op jit(solution)/shard_map/ppermute | solution.py:293
  77.2 1.4 %collective-permute-start.17 = (f32[64,256]{1,0:T(8,128)S(1)}, f32[64,256]{1,0:T(8,128)S(1)}, u32[]{:S(2)}, u32[]{:S(2)}) collective-permute-start(f32[64,256]{1,0:T(8,128)S(1)} %get-tuple-element.46), channel_id=1, source_target_pairs={{0,4},{4,0},{8,12},{12,8},{16,20},{20,16},{24,28},{28,24},{1,5},{5... | collective-permute-start | bytes 196616 | tf_op jit(solution)/shard_map/ppermute | solution.py:293
  78.6 5.8 %collective-permute-start.20 = (f32[64,256]{1,0:T(8,128)S(1)}, f32[64,256]{1,0:T(8,128)S(1)}, u32[]{:S(2)}, u32[]{:S(2)}) collective-permute-start(f32[64,256]{1,0:T(8,128)S(1)} %shard_map.72.refs_0_), channel_id=1, source_target_pairs={{0,24},{4,28},{8,16},{12,20},{16,8},{20,12},{24,0},{28,4},{1,25},{... | collective-permute-start | bytes 196616 | tf_op jit(solution)/shard_map/ppermute | solution.py:293
  79.5 5.5 %collective-permute-start.19 = (f32[64,256]{1,0:T(8,128)S(1)}, f32[64,256]{1,0:T(8,128)S(1)}, u32[]{:S(2)}, u32[]{:S(2)}) collective-permute-start(f32[64,256]{1,0:T(8,128)S(1)} %shard_map.72.refs_0_), channel_id=1, source_target_pairs={{0,16},{4,20},{8,24},{12,28},{16,0},{20,4},{24,8},{28,12},{1,17},{... | collective-permute-start | bytes 196616 | tf_op jit(solution)/shard_map/ppermute | solution.py:293
  80.6 4.4 %collective-permute-start.18 = (f32[64,256]{1,0:T(8,128)S(1)}, f32[64,256]{1,0:T(8,128)S(1)}, u32[]{:S(2)}, u32[]{:S(2)}) collective-permute-start(f32[64,256]{1,0:T(8,128)S(1)} %shard_map.72.refs_0_), channel_id=1, source_target_pairs={{0,8},{4,12},{8,0},{12,4},{16,24},{20,28},{24,16},{28,20},{1,9},{5... | collective-permute-start | bytes 196616 | tf_op jit(solution)/shard_map/ppermute | solution.py:293
  85.0 1.3 %collective-permute-start.21 = (f32[64,256]{1,0:T(8,128)S(1)}, f32[64,256]{1,0:T(8,128)S(1)}, u32[]{:S(2)}, u32[]{:S(2)}) collective-permute-start(f32[64,256]{1,0:T(8,128)S(1)} %shard_map.73.mine_ref), channel_id=1, source_target_pairs={{0,4},{4,0},{8,12},{12,8},{16,20},{20,16},{24,28},{28,24},{1,5},{5... | collective-permute-start | bytes 196616 | tf_op jit(solution)/shard_map/ppermute | solution.py:293
  87.3 5.6 %collective-permute-start.24 = (f32[8,256]{1,0:T(8,128)S(1)}, f32[8,256]{1,0:T(8,128)S(1)}, u32[]{:S(2)}, u32[]{:S(2)}) collective-permute-start(f32[8,256]{1,0:T(8,128)S(1)} %get-tuple-element.48.refs_1_), channel_id=1, source_target_pairs={{0,3},{1,2},{2,1},{3,0},{4,7},{5,6},{6,5},{7,4},{8,11},{9,10},{10,... | collective-permute-start | bytes 24584 | tf_op jit(solution)/shard_map/ppermute | solution.py:293
  89.2 4.6 %collective-permute-start.23 = (f32[8,256]{1,0:T(8,128)S(1)}, f32[8,256]{1,0:T(8,128)S(1)}, u32[]{:S(2)}, u32[]{:S(2)}) collective-permute-start(f32[8,256]{1,0:T(8,128)S(1)} %get-tuple-element.48.refs_1_), channel_id=1, source_target_pairs={{0,2},{1,3},{2,0},{3,1},{4,6},{5,7},{6,4},{7,5},{8,10},{9,11},{10,... | collective-permute-start | bytes 24584 | tf_op jit(solution)/shard_map/ppermute | solution.py:293
  90.3 3.7 %collective-permute-start.22 = (f32[8,256]{1,0:T(8,128)S(1)}, f32[8,256]{1,0:T(8,128)S(1)}, u32[]{:S(2)}, u32[]{:S(2)}) collective-permute-start(f32[8,256]{1,0:T(8,128)S(1)} %get-tuple-element.48.refs_1_), channel_id=1, source_target_pairs={{0,1},{1,0},{2,3},{3,2},{4,5},{5,4},{6,7},{7,6},{8,9},{9,8},{10,11... | collective-permute-start | bytes 24584 | tf_op jit(solution)/shard_map/ppermute | solution.py:293

commit v2 on v1

--- a/solution.py
+++ b/solution.py
@@ -9,6 +9,8 @@
 TIME_PAIR = True
 RAW_PAIR = True
 MB_HALF = True
+MB_TREE = False
+EARLY = 5
 ridge_share = 0.1
 epsilon = 1e-06
 contraction_bound = 1e-3
@@ -175,12 +177,12 @@
     out_ref[...] = tree_sum([part[...] for part in parts])
 
 
-def time_side_kernel(species_count, raw_ref, tensor_ref, side_ref):
+def time_side_kernel(species_count, first, raw_ref, tensor_ref, side_ref):
     rows = raw_ref.shape[0]
     raw_high, raw_low = split(raw_ref[...])
     weights = jnp.concatenate([raw_high, raw_high, raw_low, raw_low], axis=0)
-    for p in range(species_count):
-        high, low = split(tensor_ref[pl.ds(p, rows, stride=species_count), :])
+    for p in range(side_ref.shape[0]):
+        high, low = split(tensor_ref[pl.ds(first + p, rows, stride=species_count), :])
         side_ref[p] = dot_fast(jnp.concatenate([high, low, high, low], axis=0), weights, ((0,), (0,)))
 
 
@@ -244,8 +246,16 @@
     invert(matrix_ref[...], inverse_ref, work_ref)
 
 
-def species_kernel(scale_ref, matrix_ref, inverse_ref, side_ref, *refs):
-    *parts, species_ref, out_ref, keep_ref, send_ref, scaled_ref = refs
+def refined_inverse_kernel(matrix_ref, inverse_ref, work_ref):
+    matrix = matrix_ref[...]
+    invert(matrix, inverse_ref, work_ref)
+    inverse = inverse_ref[...]
+    left = jnp.where(eye_mask(matrix.shape[0]), 1.0, 0.0) - dot(matrix, inverse)
+    inverse_ref[...] = inverse + dot(inverse, left)
+
+
+def species_kernel(scale_ref, matrix_ref, inverse_ref, side_ref, rest_ref, *refs):
+    *parts, species_ref, scaled_ref, send_ref = refs
     core = place_of("space") % 2
     scale = scale_ref[0:1, :]
     if MB_HALF:
@@ -259,26 +269,35 @@
     raw = solve(m_b, matrix_ref[...], inverse_ref[...])
     species = raw * lax.rsqrt(jnp.mean(raw * raw, axis=0, keepdims=True) + epsilon)
     species_ref[...] = species
-    out_ref[...] = species
     scaled_ref[...] = species * scale
-    half = keep_ref.shape[0]
-    for ref, block in ((send_ref, 1 - core), (keep_ref, core)):
-        total = jnp.zeros(ref.shape, f32)
+    time_half(1 - core, (side_ref, rest_ref), scaled_ref, send_ref)
+
+
+def time_half(block, side_refs, scaled_ref, out_ref):
+    half = out_ref.shape[0]
+    total = jnp.zeros(out_ref.shape, f32)
+    at = 0
+    for side_ref in side_refs:
         for p in range(side_ref.shape[0]):
-            total = total + side_ref[p, at_rows(block, half), :] * scaled_ref[p:p + 1, :]
-        ref[...] = total
+            total = total + side_ref[p, at_rows(block, half), :] * scaled_ref[at:at + 1, :]
+            at += 1
+    out_ref[...] = total
+
+
+def time_half_kernel(side_ref, rest_ref, scaled_ref, out_ref):
+    time_half(place_of("space") % 2, (side_ref, rest_ref), scaled_ref, out_ref)
 
 
 def species_gram_kernel(a_gram_ref, species_ref, matrix_ref):
     matrix_ref[...] = regularized(a_gram_ref[...] * gram(species_ref[...]))
 
 
-def time_solve_kernel(matrix_ref, inverse_ref, mine_ref, partner_ref, raw_ref, squares_ref, m_c_ref):
+def time_solve_kernel(inverse_ref, mine_ref, partner_ref, raw_ref, squares_ref, m_c_ref):
     core = place_of("space") % 2
     half = mine_ref.shape[0]
     m_c_ref[at_rows(core, half), :] = mine_ref[...]
     m_c_ref[at_rows(1 - core, half), :] = partner_ref[...]
-    raw = solve(m_c_ref[...], matrix_ref[...], inverse_ref[...])
+    raw = dot(m_c_ref[...], inverse_ref[...])
     raw_ref[...] = raw
     squares_ref[...] = jnp.broadcast_to(jnp.sum(raw * raw, axis=0, keepdims=True), squares_ref.shape)
 
@@ -372,7 +391,7 @@
         compiler_params=pltpu.CompilerParams(vmem_limit_bytes=vmem_limit),
         name="load_factors",
     )(*[pltpu.with_memory_space_constraint(x, pltpu.HBM) for x in (time_factor, species_factor)])
-    received = block_from(time_here, time_half, "tm")
+    received = block_from(time_factor, time_half, "tm")
     m_a, side = run(
         space_kernel, [local(row_count, rank), local(row_count, species_count, rank)], 2
     )(tensor.reshape(row_count * species_count, step_count), time_here, species_here)
@@ -391,47 +410,56 @@
         [local(species_count, rank)],
     )(matrix, inverse, side, *m_a_parts)
     received = to_partner(send)
-    (time_side,) = run(
-        lambda *refs: time_side_kernel(species_count, *refs), [local(species_count, step_count, rank)], 2
-    )(raw, tensor.reshape(row_count * species_count, step_count))
+    time_sides = []
+    for first, count in (
+        (0, EARLY * species_count // 8), (EARLY * species_count // 8, species_count - EARLY * species_count // 8)
+    ):
+        time_sides += run(
+            lambda *refs, first=first: time_side_kernel(species_count, first, *refs),
+            [local(count, step_count, rank)],
+            2 * count / species_count,
+        )(raw, tensor.reshape(row_count * species_count, step_count))
     chip_block, m_b = run(chip_kernel, [local(2 * row_count, rank), local(half_species, rank)], 0.3)(
         raw, keep, received
     )
-    m_b_parts = over_time(m_b)
+    if not MB_TREE:
+        m_b = add(over_time(m_b))
+    step = 1
+    while MB_TREE and step < blocks:
+        m_b = add([m_b, exchange(m_b, "tm", step, blocks)])
+        step *= 2
     raw_blocks = block_from(chip_block, raw, "space")
-    m_b_parts = over_chips(add(m_b_parts))
+    m_b_parts = over_chips(m_b)
     mine = pack(m_b, raw_blocks)
     partner = to_partner(mine)
     if MB_HALF:
         m_b = add(m_b_parts)
         m_b_parts = [m_b, to_partner(m_b)]
     a_gram, matrix, scale, space_out = run(
-        space_gram_kernel, [square, square, local(8, rank), result(row_count, rank)], 1.5, [local(total_rows, rank)]
+        space_gram_kernel, [square, square, local(8, rank), local(row_count, rank)], 1.5, [local(total_rows, rank)]
     )(c_gram, chip_block, mine, partner)
     (inverse,) = run(inverse_kernel, [square], 1, [square])(matrix)
 
-    species, species_out, m_c_keep, m_c_send = run(
-        species_kernel,
-        [local(species_count, rank), result(species_count, rank), local(half_steps, rank), local(half_steps, rank)],
-        1.5,
-        [local(species_count, rank)],
-    )(scale, matrix, inverse, time_side, *m_b_parts)
+    species, scaled, m_c_send = run(
+        species_kernel, [local(species_count, rank), local(species_count, rank), local(half_steps, rank)], 1.5
+    )(scale, matrix, inverse, *time_sides, *m_b_parts)
 
     m_c_received = to_partner(m_c_send)
+    (m_c_keep,) = run(time_half_kernel, [local(half_steps, rank)], 1)(*time_sides, scaled)
     (matrix,) = run(species_gram_kernel, [square], 0.5)(a_gram, species)
     m_c_parts = over_chips(add([m_c_keep, m_c_received]))
-    (inverse,) = run(inverse_kernel, [square], 1, [square])(matrix)
+    (inverse,) = run(refined_inverse_kernel, [square], 1, [square])(matrix)
     m_c = add(m_c_parts)
     m_c_partner = to_partner(m_c)
     raw_time, squares = run(
         time_solve_kernel, [local(step_count, rank), local(8, rank)], 1, [local(step_count, rank)]
-    )(matrix, inverse, m_c, m_c_partner)
+    )(inverse, m_c, m_c_partner)
 
     squares = over_time(squares)
     (time_out,) = run(
         lambda *refs: time_scale_kernel(total_steps, *refs), [result(step_count, rank)], 0.5
     )(raw_time, *squares)
-    return (space_out, species_out, time_out)
+    return (space_out, species, time_out)
 
 
 def solution(mesh):

time: 94.8 us -> 93.2 us (0.983)
  waiting for transfers between devices: 16 us -> 12.9 us
  local copies, waits for them, and re-layouts: 0.01 us -> 1.26 us
    ppermute x1, waiting for transfers between devices: 3.76 us -> 0.01 us  [block_from(): received.append(lax.ppermute(block, ('space', 'tm'), turns))]
    ppermute x1, starting transfers between devices: 0.01 us -> 3.12 us  [block_from(): received.append(lax.ppermute(block, ('space', 'tm'), turns))]
    ppermute x23, starting transfers between devices: 27.9 us -> 25.4 us  [exchange(): return lax.ppermute(value, axis, [(i, i ^ step) for i in range(count)])]
    unnamed x2 -> x4, local copies, waits for them, and re-layouts: 0.01 us -> 1.26 us
    pallas_call x18 -> x20, Pallas kernels: 47.3 us -> 47 us  [placed(): call(*[pltpu.with_memory_space_constraint(x, pltpu.VMEM) for x in operands])]
  transfers between devices with their start and end apart: 25 -> 25, of which waited for: 13 -> 12; matrix products, arithmetic and copies ran while one was open for 0% -> 1% of each run, Pallas kernels for 45% -> 48%
where the time goes in v2:
time: 93.2 us; the launch traced here: 93.1 us
  Pallas kernels  48 us (52%)
  starting transfers between devices  30.1 us (32%)
  waiting for transfers between devices  12.9 us (14%)
  local copies, waits for them, and re-layouts  1.26 us (1%)
    pallas_call x20, Pallas kernels, placed(): call(*[pltpu.with_memory_space_constraint(x, pltpu.VMEM) for x in operands])  47 us
    ppermute x23, starting transfers between devices, exchange(): return lax.ppermute(value, axis, [(i, i ^ step) for i in range(count)])  25.4 us
    ppermute x23, waiting for transfers between devices, exchange(): return lax.ppermute(value, axis, [(i, i ^ step) for i in range(count)])  12.9 us
    ppermute x1, starting transfers between devices, block_from(): received.append(lax.ppermute(block, ('space', 'tm'), turns))  3.12 us
  transfers between devices with their start and end apart: 25, of which 12 were waited for; matrix products, arithmetic and copies ran while one was open for 1% of the time, Pallas kernels for 48%

profile of v2, /device:TPU:0, one launch (start us, length us, event | category | flops | bytes accessed | tf_op | source)
XLA Modules:
  0.0 93.1 jit_solution(15566696484900346444)
XLA Ops:
  0.6 3.1 %collective-permute-start = (f32[128,256]{1,0:T(8,128)}, f32[128,256]{1,0:T(8,128)S(1)}, u32[]{:S(2)}, u32[]{:S(2)}) collective-permute-start(f32[128,256]{1,0:T(8,128)} %time_hbm.1), channel_id=1, source_target_pairs={{0,1},{1,0},{2,3},{3,2},{4,6},{5,7},{6,4},{7,5},{8,9},{9,8},{10,11... | collective-permute-start | bytes 393224 | tf_op jit(solution)/shard_map/ppermute | solution.py:365
  3.8 1.0 %load_factors.1 = (f32[64,256]{1,0:T(8,128)S(1)}, f32[128,256]{1,0:T(8,128)S(1)}, f32[64,256]{1,0:T(8,128)S(1)}) custom-call(f32[128,256]{1,0:T(8,128)} %time_hbm.1, f32[64,256]{1,0:T(8,128)} %species_hbm.1), custom_call_target="tpu_custom_call" | custom-call | flops 10000000000 | bytes 100000000 | tf_op jit(solution)/shard_map/load_factors/pallas_call | solution.py:384
  4.8 2.6 %collective-permute-start.1 = (f32[64,256]{1,0:T(8,128)S(1)}, f32[64,256]{1,0:T(8,128)S(1)}, u32[]{:S(2)}, u32[]{:S(2)}) collective-permute-start(f32[64,256]{1,0:T(8,128)S(1)} %get-tuple-element.28), channel_id=1, source_target_pairs={{0,3},{1,2},{2,1},{3,0},{4,7},{5,6},{6,5},{7,4},{8,11},{9,10},{10,... | collective-permute-start | bytes 196616 | tf_op jit(solution)/shard_map/ppermute | solution.py:312
  7.4 1.3 %shard_map.58 = (f32[64,256]{1,0:T(8,128)S(1)}, f32[64,64,256]{2,1,0:T(8,128)S(1)}) custom-call(f32[4096,128]{1,0:T(8,128)S(1)} %bitcast.1, f32[128,256]{1,0:T(8,128)S(1)} %get-tuple-element.26.time_ref.own_ref, f32[64,256]{1,0:T(8,128)S(1)} %get-tuple-element.25.species_ref), custom_call_target="tpu_custom_call" | custom-call | flops 2000000000 | tf_op jit(solution)/shard_map/pallas_call | solution.py:326
  8.7 2.6 %collective-permute-done.1.refs_1_ = f32[64,256]{1,0:T(8,128)S(1)} collective-permute-done((f32[64,256]{1,0:T(8,128)S(1)}, f32[64,256]{1,0:T(8,128)S(1)}, u32[]{:S(2)}, u32[]{:S(2)}) %collective-permute-start.1) | collective-permute-done | bytes 65568 | tf_op jit(solution)/shard_map/ppermute | solution.py:312
  11.4 2.4 %collective-permute-start.5 = (f32[64,256]{1,0:T(8,128)S(1)}, f32[64,256]{1,0:T(8,128)S(1)}, u32[]{:S(2)}, u32[]{:S(2)}) collective-permute-start(f32[64,256]{1,0:T(8,128)S(1)} %get-tuple-element.27.after_ref.refs_0_), channel_id=1, source_target_pairs={{0,3},{1,2},{2,1},{3,0},{4,7},{5,6},{6,5},{7,4},{8,11},{9,10},{10,... | collective-permute-start | bytes 196616 | tf_op jit(solution)/shard_map/ppermute | solution.py:312
  13.8 0.2 collective-permute-start.4
  14.0 1.8 %collective-permute-start.3 = (f32[64,256]{1,0:T(8,128)S(1)}, f32[64,256]{1,0:T(8,128)S(1)}, u32[]{:S(2)}, u32[]{:S(2)}) collective-permute-start(f32[64,256]{1,0:T(8,128)S(1)} %get-tuple-element.27.after_ref.refs_0_), channel_id=1, source_target_pairs={{0,1},{1,0},{2,3},{3,2},{4,5},{5,4},{6,7},{7,6},{8,9},{9,8},{10,11... | collective-permute-start | bytes 196616 | tf_op jit(solution)/shard_map/ppermute | solution.py:312
  15.9 35.9 %shard_map.60 = (f32[256,256]{1,0:T(8,128)S(1)}, f32[256,256]{1,0:T(8,128)S(1)}, f32[256,256]{1,0:T(8,128)S(1)}) custom-call(f32[64,256]{1,0:T(8,128)S(1)} %get-tuple-element.25.species_ref, f32[128,256]{1,0:T(8,128)S(1)} %get-tuple-element.26.time_ref.own_ref, f32[192,256]{1,0:T(8,128)S(1)} %shard_map.59.mine_ref, ...), custom_call_target="tpu_custom_call" | custom-call | flops 2000000000 | tf_op jit(solution)/shard_map/pallas_call | solution.py:326
  51.8 1.1 %shard_map.61 = (f32[64,256]{1,0:T(8,128)S(1)}, f32[32,256]{1,0:T(8,128)S(1)}, f32[96,256]{1,0:T(8,128)S(1)}) custom-call(f32[256,256]{1,0:T(8,128)S(1)} %get-tuple-element.30.matrix_ref, f32[256,256]{1,0:T(8,128)S(1)} %get-tuple-element.31.inverse_ref, f32[64,64,256]{2,1,0:T(8,128)S(1)} %get-tuple-element.32.side_ref, ...), custom_call_target="tpu_custom_call" | custom-call | flops 1000000000 | tf_op jit(solution)/shard_map/pallas_call | solution.py:326
  52.9 0.1 collective-permute-start.6
  53.0 1.3 %collective-permute-done.6.received_ref = f32[96,256]{1,0:T(8,128)S(1)} collective-permute-done((f32[96,256]{1,0:T(8,128)S(1)}, f32[96,256]{1,0:T(8,128)S(1)}, u32[]{:S(2)}, u32[]{:S(2)}) %collective-permute-start.6) | collective-permute-done | bytes 98336 | tf_op jit(solution)/shard_map/ppermute | solution.py:312
  54.3 1.6 %collective-permute-start.10 = (f32[128,256]{1,0:T(8,128)S(1)}, f32[128,256]{1,0:T(8,128)S(1)}, u32[]{:S(2)}, u32[]{:S(2)}) collective-permute-start(f32[128,256]{1,0:T(8,128)S(1)} %get-tuple-element.36.own_ref), channel_id=1, source_target_pairs={{0,8},{4,20},{8,0},{12,28},{16,24},{20,4},{24,16},{28,12},{1,9},{5... | collective-permute-start | bytes 393224 | tf_op jit(solution)/shard_map/ppermute | solution.py:368
  55.9 1.5 %collective-permute-start.11 = (f32[64,256]{1,0:T(8,128)S(1)}, f32[64,256]{1,0:T(8,128)S(1)}, u32[]{:S(2)}, u32[]{:S(2)}) collective-permute-start(f32[64,256]{1,0:T(8,128)S(1)} %get-tuple-element.33.raw_ref.refs_0_), channel_id=1, source_target_pairs={{0,24},{4,28},{8,16},{12,20},{16,8},{20,12},{24,0},{28,4},{1,25},{... | collective-permute-start | bytes 196616 | tf_op jit(solution)/shard_map/ppermute | solution.py:312
  57.4 2.4 %collective-permute-start.9 = (f32[32,256]{1,0:T(8,128)S(1)}, f32[32,256]{1,0:T(8,128)S(1)}, u32[]{:S(2)}, u32[]{:S(2)}) collective-permute-start(f32[32,256]{1,0:T(8,128)S(1)} %get-tuple-element.37.refs_0_), channel_id=1, source_target_pairs={{0,3},{1,2},{2,1},{3,0},{4,7},{5,6},{6,5},{7,4},{8,11},{9,10},{10,... | collective-permute-start | bytes 98312 | tf_op jit(solution)/shard_map/ppermute | solution.py:312
  59.7 2.0 %collective-permute-start.7 = (f32[32,256]{1,0:T(8,128)S(1)}, f32[32,256]{1,0:T(8,128)S(1)}, u32[]{:S(2)}, u32[]{:S(2)}) collective-permute-start(f32[32,256]{1,0:T(8,128)S(1)} %get-tuple-element.37.refs_0_), channel_id=1, source_target_pairs={{0,1},{1,0},{2,3},{3,2},{4,5},{5,4},{6,7},{7,6},{8,9},{9,8},{10,11... | collective-permute-start | bytes 98312 | tf_op jit(solution)/shard_map/ppermute | solution.py:312
  61.8 1.4 %collective-permute-done.9.refs_3_ = f32[32,256]{1,0:T(8,128)S(1)} collective-permute-done((f32[32,256]{1,0:T(8,128)S(1)}, f32[32,256]{1,0:T(8,128)S(1)}, u32[]{:S(2)}, u32[]{:S(2)}) %collective-permute-start.9) | collective-permute-done | bytes 32800 | tf_op jit(solution)/shard_map/ppermute | solution.py:312
  63.2 1.4 %collective-permute-done.8.refs_2_ = f32[32,256]{1,0:T(8,128)S(1)} collective-permute-done((f32[32,256]{1,0:T(8,128)S(1)}, f32[32,256]{1,0:T(8,128)S(1)}, u32[]{:S(2)}, u32[]{:S(2)}) %collective-permute-start.8) | collective-permute-done | bytes 32800 | tf_op jit(solution)/shard_map/ppermute | solution.py:312
  64.7 1.1 %shard_map.67.side_ref = f32[40,128,256]{2,1,0:T(8,128)S(1)} custom-call(f32[64,256]{1,0:T(8,128)S(1)} %get-tuple-element.33.raw_ref.refs_0_, f32[4096,128]{1,0:T(8,128)S(1)} %bitcast.2), custom_call_target="tpu_custom_call" | custom-call | flops 1250000000 | tf_op jit(solution)/shard_map/pallas_call | solution.py:326
  65.8 1.5 %collective-permute-start.15 = (f32[32,256]{1,0:T(8,128)S(1)}, f32[32,256]{1,0:T(8,128)S(1)}, u32[]{:S(2)}, u32[]{:S(2)}) collective-permute-start(f32[32,256]{1,0:T(8,128)S(1)} %shard_map.63.after_ref.refs_0_), channel_id=1, source_target_pairs={{0,24},{4,28},{8,16},{12,20},{16,8},{20,12},{24,0},{28,4},{1,25},{... | collective-permute-start | bytes 98312 | tf_op jit(solution)/shard_map/ppermute | solution.py:312
  67.3 1.5 %collective-permute-start.14 = (f32[32,256]{1,0:T(8,128)S(1)}, f32[32,256]{1,0:T(8,128)S(1)}, u32[]{:S(2)}, u32[]{:S(2)}) collective-permute-start(f32[32,256]{1,0:T(8,128)S(1)} %shard_map.63.after_ref.refs_0_), channel_id=1, source_target_pairs={{0,16},{4,20},{8,24},{12,28},{16,0},{20,4},{24,8},{28,12},{1,17},{... | collective-permute-start | bytes 98312 | tf_op jit(solution)/shard_map/ppermute | solution.py:312
  68.9 0.5 collective-permute-start.13
  69.4 0.7 shard_map.68.rest_ref
  70.1 0.6 collective-permute-done.15.refs_3_
  70.7 0.6 collective-permute-done.14.refs_2_
  71.3 1.5 %collective-permute-done.13.refs_1_ = f32[32,256]{1,0:T(8,128)S(1)} collective-permute-done((f32[32,256]{1,0:T(8,128)S(1)}, f32[32,256]{1,0:T(8,128)S(1)}, u32[]{:S(2)}, u32[]{:S(2)}) %collective-permute-start.13) | collective-permute-done | bytes 32800 | tf_op jit(solution)/shard_map/ppermute | solution.py:312
  72.9 1.0 %shard_map.65 = (f32[256,256]{1,0:T(8,128)S(1)}, f32[256,256]{1,0:T(8,128)S(1)}, f32[8,256]{1,0:T(8,128)S(1)}, f32[64,256]{1,0:T(8,128)S(1)}) custom-call(f32[256,256]{1,0:T(8,128)S(1)} %get-tuple-element.29.c_gram_ref, f32[128,256]{1,0:T(8,128)S(1)} %get-tuple-element.36.own_ref, f32[192,256]{1,0:T(8,128)S(1)} %shard_map.64.mine_ref, ...), custom_call_target="tpu_custom_call" | custom-call | flops 1500000000 | tf_op jit(solution)/shard_map/pallas_call | solution.py:326
  73.9 0.7 shard_map.66.inverse_ref
  74.6 1.2 %shard_map.70 = (f32[64,256]{1,0:T(8,128)S(1)}, f32[64,256]{1,0:T(8,128)S(1)}, f32[64,256]{1,0:T(8,128)S(1)}) custom-call(f32[8,256]{1,0:T(8,128)S(1)} %get-tuple-element.39.scale_ref, f32[256,256]{1,0:T(8,128)S(1)} %get-tuple-element.40.matrix_ref, f32[256,256]{1,0:T(8,128)S(1)} %shard_map.66.inverse_ref, f32[40,128,256]{2,1,0:T(8,128)S(1)} %shard_map.67.side_ref, ...), custom_call_target="tpu_custom_call" | custom-call | flops 1500000000 | tf_op jit(solution)/shard_map/pallas_call | solution.py:326
  75.8 0.6 collective-permute-start.17
  76.3 0.4 shard_map.73.refs_0_
  76.8 0.5 collective-permute-done.17.refs_1_
  77.2 0.5 collective-permute-start.20
  77.8 1.5 %collective-permute-start.19 = (f32[64,256]{1,0:T(8,128)S(1)}, f32[64,256]{1,0:T(8,128)S(1)}, u32[]{:S(2)}, u32[]{:S(2)}) collective-permute-start(f32[64,256]{1,0:T(8,128)S(1)} %shard_map.74.refs_0_), channel_id=1, source_target_pairs={{0,16},{4,20},{8,24},{12,28},{16,0},{20,4},{24,8},{28,12},{1,17},{... | collective-permute-start | bytes 196616 | tf_op jit(solution)/shard_map/ppermute | solution.py:312
  79.3 1.5 %collective-permute-start.18 = (f32[64,256]{1,0:T(8,128)S(1)}, f32[64,256]{1,0:T(8,128)S(1)}, u32[]{:S(2)}, u32[]{:S(2)}) collective-permute-start(f32[64,256]{1,0:T(8,128)S(1)} %shard_map.74.refs_0_), channel_id=1, source_target_pairs={{0,8},{4,12},{8,0},{12,4},{16,24},{20,28},{24,16},{28,20},{1,9},{5... | collective-permute-start | bytes 196616 | tf_op jit(solution)/shard_map/ppermute | solution.py:312
  80.8 0.6 shard_map.71.matrix_ref
  81.4 1.8 %collective-permute-done.20.refs_3_ = f32[64,256]{1,0:T(8,128)S(1)} collective-permute-done((f32[64,256]{1,0:T(8,128)S(1)}, f32[64,256]{1,0:T(8,128)S(1)}, u32[]{:S(2)}, u32[]{:S(2)}) %collective-permute-start.20) | collective-permute-done | bytes 65568 | tf_op jit(solution)/shard_map/ppermute | solution.py:312
  83.2 0.1 collective-permute-done.19.refs_2_
  83.3 0.3 collective-permute-done.18.refs_1_
  83.7 1.8 %shard_map.72.inverse_ref = f32[256,256]{1,0:T(8,128)S(1)} custom-call(f32[256,256]{1,0:T(8,128)S(1)} %shard_map.71.matrix_ref), custom_call_target="tpu_custom_call" | custom-call | flops 1000000000 | tf_op jit(solution)/shard_map/pallas_call | solution.py:326
  85.5 0.3 shard_map.76
  85.8 2.0 %collective-permute-start.24 = (f32[8,256]{1,0:T(8,128)S(1)}, f32[8,256]{1,0:T(8,128)S(1)}, u32[]{:S(2)}, u32[]{:S(2)}) collective-permute-start(f32[8,256]{1,0:T(8,128)S(1)} %get-tuple-element.46.refs_1_), channel_id=1, source_target_pairs={{0,3},{1,2},{2,1},{3,0},{4,7},{5,6},{6,5},{7,4},{8,11},{9,10},{10,... | collective-permute-start | bytes 24584 | tf_op jit(solution)/shard_map/ppermute | solution.py:312
  87.8 0.6 collective-permute-start.23
  88.4 1.8 %collective-permute-start.22 = (f32[8,256]{1,0:T(8,128)S(1)}, f32[8,256]{1,0:T(8,128)S(1)}, u32[]{:S(2)}, u32[]{:S(2)}) collective-permute-start(f32[8,256]{1,0:T(8,128)S(1)} %get-tuple-element.46.refs_1_), channel_id=1, source_target_pairs={{0,1},{1,0},{2,3},{3,2},{4,5},{5,4},{6,7},{7,6},{8,9},{9,8},{10,11... | collective-permute-start | bytes 24584 | tf_op jit(solution)/shard_map/ppermute | solution.py:312
  90.2 0.6 copy.7
  90.9 0.6 copy.6
  91.5 0.9 collective-permute-done.23.refs_3_
  92.4 0.7 shard_map.77
  (27 shorter events, 0.4 us)
Async XLA Ops:
  0.6 6.8 %copy-start = (f32[64,64,128]{2,1,0:T(8,128)S(1)}, f32[64,64,128]{2,1,0:T(8,128)}, u32[]{:S(2)}) copy-start(f32[64,64,128]{2,1,0:T(8,128)} %param.3) | copy-start | bytes 6291460
  0.6 10.7 %collective-permute-start = (f32[128,256]{1,0:T(8,128)}, f32[128,256]{1,0:T(8,128)S(1)}, u32[]{:S(2)}, u32[]{:S(2)}) collective-permute-start(f32[128,256]{1,0:T(8,128)} %time_hbm.1), channel_id=1, source_target_pairs={{0,1},{1,0},{2,3},{3,2},{4,6},{5,7},{6,4},{7,5},{8,9},{9,8},{10,11... | collective-permute-start | bytes 393224 | tf_op jit(solution)/shard_map/ppermute | solution.py:365
  4.8 6.5 %collective-permute-start.1 = (f32[64,256]{1,0:T(8,128)S(1)}, f32[64,256]{1,0:T(8,128)S(1)}, u32[]{:S(2)}, u32[]{:S(2)}) collective-permute-start(f32[64,256]{1,0:T(8,128)S(1)} %get-tuple-element.28), channel_id=1, source_target_pairs={{0,3},{1,2},{2,1},{3,0},{4,7},{5,6},{6,5},{7,4},{8,11},{9,10},{10,... | collective-permute-start | bytes 196616 | tf_op jit(solution)/shard_map/ppermute | solution.py:312
  11.3 4.5 %collective-permute-start.2 = (f32[192,256]{1,0:T(8,128)S(1)}, f32[192,256]{1,0:T(8,128)S(1)}, u32[]{:S(2)}, u32[]{:S(2)}) collective-permute-start(f32[192,256]{1,0:T(8,128)S(1)} %shard_map.59.mine_ref), channel_id=1, source_target_pairs={{0,4},{4,0},{8,12},{12,8},{16,20},{20,16},{24,28},{28,24},{1,5},{5... | collective-permute-start | bytes 589832 | tf_op jit(solution)/shard_map/ppermute | solution.py:312
  11.4 40.4 %collective-permute-start.5 = (f32[64,256]{1,0:T(8,128)S(1)}, f32[64,256]{1,0:T(8,128)S(1)}, u32[]{:S(2)}, u32[]{:S(2)}) collective-permute-start(f32[64,256]{1,0:T(8,128)S(1)} %get-tuple-element.27.after_ref.refs_0_), channel_id=1, source_target_pairs={{0,3},{1,2},{2,1},{3,0},{4,7},{5,6},{6,5},{7,4},{8,11},{9,10},{10,... | collective-permute-start | bytes 196616 | tf_op jit(solution)/shard_map/ppermute | solution.py:312
  13.8 38.0 %collective-permute-start.4 = (f32[64,256]{1,0:T(8,128)S(1)}, f32[64,256]{1,0:T(8,128)S(1)}, u32[]{:S(2)}, u32[]{:S(2)}) collective-permute-start(f32[64,256]{1,0:T(8,128)S(1)} %get-tuple-element.27.after_ref.refs_0_), channel_id=1, source_target_pairs={{0,2},{1,3},{2,0},{3,1},{4,6},{5,7},{6,4},{7,5},{8,10},{9,11},{10,... | collective-permute-start | bytes 196616 | tf_op jit(solution)/shard_map/ppermute | solution.py:312
  14.0 37.7 %collective-permute-start.3 = (f32[64,256]{1,0:T(8,128)S(1)}, f32[64,256]{1,0:T(8,128)S(1)}, u32[]{:S(2)}, u32[]{:S(2)}) collective-permute-start(f32[64,256]{1,0:T(8,128)S(1)} %get-tuple-element.27.after_ref.refs_0_), channel_id=1, source_target_pairs={{0,1},{1,0},{2,3},{3,2},{4,5},{5,4},{6,7},{7,6},{8,9},{9,8},{10,11... | collective-permute-start | bytes 196616 | tf_op jit(solution)/shard_map/ppermute | solution.py:312
  52.9 1.4 %collective-permute-start.6 = (f32[96,256]{1,0:T(8,128)S(1)}, f32[96,256]{1,0:T(8,128)S(1)}, u32[]{:S(2)}, u32[]{:S(2)}) collective-permute-start(f32[96,256]{1,0:T(8,128)S(1)} %get-tuple-element.35), channel_id=1, source_target_pairs={{0,4},{4,0},{8,12},{12,8},{16,20},{20,16},{24,28},{28,24},{1,5},{5... | collective-permute-start | bytes 294920 | tf_op jit(solution)/shard_map/ppermute | solution.py:312
  54.3 10.2 %collective-permute-start.10 = (f32[128,256]{1,0:T(8,128)S(1)}, f32[128,256]{1,0:T(8,128)S(1)}, u32[]{:S(2)}, u32[]{:S(2)}) collective-permute-start(f32[128,256]{1,0:T(8,128)S(1)} %get-tuple-element.36.own_ref), channel_id=1, source_target_pairs={{0,8},{4,20},{8,0},{12,28},{16,24},{20,4},{24,16},{28,12},{1,9},{5... | collective-permute-start | bytes 393224 | tf_op jit(solution)/shard_map/ppermute | solution.py:368
  55.9 8.7 %collective-permute-start.11 = (f32[64,256]{1,0:T(8,128)S(1)}, f32[64,256]{1,0:T(8,128)S(1)}, u32[]{:S(2)}, u32[]{:S(2)}) collective-permute-start(f32[64,256]{1,0:T(8,128)S(1)} %get-tuple-element.33.raw_ref.refs_0_), channel_id=1, source_target_pairs={{0,24},{4,28},{8,16},{12,20},{16,8},{20,12},{24,0},{28,4},{1,25},{... | collective-permute-start | bytes 196616 | tf_op jit(solution)/shard_map/ppermute | solution.py:312
  57.4 5.8 %collective-permute-start.9 = (f32[32,256]{1,0:T(8,128)S(1)}, f32[32,256]{1,0:T(8,128)S(1)}, u32[]{:S(2)}, u32[]{:S(2)}) collective-permute-start(f32[32,256]{1,0:T(8,128)S(1)} %get-tuple-element.37.refs_0_), channel_id=1, source_target_pairs={{0,3},{1,2},{2,1},{3,0},{4,7},{5,6},{6,5},{7,4},{8,11},{9,10},{10,... | collective-permute-start | bytes 98312 | tf_op jit(solution)/shard_map/ppermute | solution.py:312
  59.7 4.8 %collective-permute-start.8 = (f32[32,256]{1,0:T(8,128)S(1)}, f32[32,256]{1,0:T(8,128)S(1)}, u32[]{:S(2)}, u32[]{:S(2)}) collective-permute-start(f32[32,256]{1,0:T(8,128)S(1)} %get-tuple-element.37.refs_0_), channel_id=1, source_target_pairs={{0,2},{1,3},{2,0},{3,1},{4,6},{5,7},{6,4},{7,5},{8,10},{9,11},{10,... | collective-permute-start | bytes 98312 | tf_op jit(solution)/shard_map/ppermute | solution.py:312
  59.7 4.8 %collective-permute-start.7 = (f32[32,256]{1,0:T(8,128)S(1)}, f32[32,256]{1,0:T(8,128)S(1)}, u32[]{:S(2)}, u32[]{:S(2)}) collective-permute-start(f32[32,256]{1,0:T(8,128)S(1)} %get-tuple-element.37.refs_0_), channel_id=1, source_target_pairs={{0,1},{1,0},{2,3},{3,2},{4,5},{5,4},{6,7},{7,6},{8,9},{9,8},{10,11... | collective-permute-start | bytes 98312 | tf_op jit(solution)/shard_map/ppermute | solution.py:312
  64.6 8.3 %collective-permute-start.12 = (f32[192,256]{1,0:T(8,128)S(1)}, f32[192,256]{1,0:T(8,128)S(1)}, u32[]{:S(2)}, u32[]{:S(2)}) collective-permute-start(f32[192,256]{1,0:T(8,128)S(1)} %shard_map.64.mine_ref), channel_id=1, source_target_pairs={{0,4},{4,0},{8,12},{12,8},{16,20},{20,16},{24,28},{28,24},{1,5},{5... | collective-permute-start | bytes 589832 | tf_op jit(solution)/shard_map/ppermute | solution.py:312
  65.8 4.9 %collective-permute-start.15 = (f32[32,256]{1,0:T(8,128)S(1)}, f32[32,256]{1,0:T(8,128)S(1)}, u32[]{:S(2)}, u32[]{:S(2)}) collective-permute-start(f32[32,256]{1,0:T(8,128)S(1)} %shard_map.63.after_ref.refs_0_), channel_id=1, source_target_pairs={{0,24},{4,28},{8,16},{12,20},{16,8},{20,12},{24,0},{28,4},{1,25},{... | collective-permute-start | bytes 98312 | tf_op jit(solution)/shard_map/ppermute | solution.py:312
  67.3 4.0 %collective-permute-start.14 = (f32[32,256]{1,0:T(8,128)S(1)}, f32[32,256]{1,0:T(8,128)S(1)}, u32[]{:S(2)}, u32[]{:S(2)}) collective-permute-start(f32[32,256]{1,0:T(8,128)S(1)} %shard_map.63.after_ref.refs_0_), channel_id=1, source_target_pairs={{0,16},{4,20},{8,24},{12,28},{16,0},{20,4},{24,8},{28,12},{1,17},{... | collective-permute-start | bytes 98312 | tf_op jit(solution)/shard_map/ppermute | solution.py:312
  68.9 3.9 %collective-permute-start.13 = (f32[32,256]{1,0:T(8,128)S(1)}, f32[32,256]{1,0:T(8,128)S(1)}, u32[]{:S(2)}, u32[]{:S(2)}) collective-permute-start(f32[32,256]{1,0:T(8,128)S(1)} %shard_map.63.after_ref.refs_0_), channel_id=1, source_target_pairs={{0,8},{4,12},{8,0},{12,4},{16,24},{20,28},{24,16},{28,20},{1,9},{5... | collective-permute-start | bytes 98312 | tf_op jit(solution)/shard_map/ppermute | solution.py:312
  72.8 1.8 %collective-permute-start.16 = (f32[32,256]{1,0:T(8,128)S(1)}, f32[32,256]{1,0:T(8,128)S(1)}, u32[]{:S(2)}, u32[]{:S(2)}) collective-permute-start(f32[32,256]{1,0:T(8,128)S(1)} %shard_map.69.refs_0_), channel_id=1, source_target_pairs={{0,4},{4,0},{8,12},{12,8},{16,20},{20,16},{24,28},{28,24},{1,5},{5... | collective-permute-start | bytes 98312 | tf_op jit(solution)/shard_map/ppermute | solution.py:312
  75.8 1.5 %collective-permute-start.17 = (f32[64,256]{1,0:T(8,128)S(1)}, f32[64,256]{1,0:T(8,128)S(1)}, u32[]{:S(2)}, u32[]{:S(2)}) collective-permute-start(f32[64,256]{1,0:T(8,128)S(1)} %get-tuple-element.44), channel_id=1, source_target_pairs={{0,4},{4,0},{8,12},{12,8},{16,20},{20,16},{24,28},{28,24},{1,5},{5... | collective-permute-start | bytes 196616 | tf_op jit(solution)/shard_map/ppermute | solution.py:312
  77.2 5.9 %collective-permute-start.20 = (f32[64,256]{1,0:T(8,128)S(1)}, f32[64,256]{1,0:T(8,128)S(1)}, u32[]{:S(2)}, u32[]{:S(2)}) collective-permute-start(f32[64,256]{1,0:T(8,128)S(1)} %shard_map.74.refs_0_), channel_id=1, source_target_pairs={{0,24},{4,28},{8,16},{12,20},{16,8},{20,12},{24,0},{28,4},{1,25},{... | collective-permute-start | bytes 196616 | tf_op jit(solution)/shard_map/ppermute | solution.py:312
  77.8 5.5 %collective-permute-start.19 = (f32[64,256]{1,0:T(8,128)S(1)}, f32[64,256]{1,0:T(8,128)S(1)}, u32[]{:S(2)}, u32[]{:S(2)}) collective-permute-start(f32[64,256]{1,0:T(8,128)S(1)} %shard_map.74.refs_0_), channel_id=1, source_target_pairs={{0,16},{4,20},{8,24},{12,28},{16,0},{20,4},{24,8},{28,12},{1,17},{... | collective-permute-start | bytes 196616 | tf_op jit(solution)/shard_map/ppermute | solution.py:312
  79.3 4.3 %collective-permute-start.18 = (f32[64,256]{1,0:T(8,128)S(1)}, f32[64,256]{1,0:T(8,128)S(1)}, u32[]{:S(2)}, u32[]{:S(2)}) collective-permute-start(f32[64,256]{1,0:T(8,128)S(1)} %shard_map.74.refs_0_), channel_id=1, source_target_pairs={{0,8},{4,12},{8,0},{12,4},{16,24},{20,28},{24,16},{28,20},{1,9},{5... | collective-permute-start | bytes 196616 | tf_op jit(solution)/shard_map/ppermute | solution.py:312
  83.6 1.9 %collective-permute-start.21 = (f32[64,256]{1,0:T(8,128)S(1)}, f32[64,256]{1,0:T(8,128)S(1)}, u32[]{:S(2)}, u32[]{:S(2)}) collective-permute-start(f32[64,256]{1,0:T(8,128)S(1)} %shard_map.75.mine_ref), channel_id=1, source_target_pairs={{0,4},{4,0},{8,12},{12,8},{16,20},{20,16},{24,28},{28,24},{1,5},{5... | collective-permute-start | bytes 196616 | tf_op jit(solution)/shard_map/ppermute | solution.py:312
  85.8 5.7 %collective-permute-start.24 = (f32[8,256]{1,0:T(8,128)S(1)}, f32[8,256]{1,0:T(8,128)S(1)}, u32[]{:S(2)}, u32[]{:S(2)}) collective-permute-start(f32[8,256]{1,0:T(8,128)S(1)} %get-tuple-element.46.refs_1_), channel_id=1, source_target_pairs={{0,3},{1,2},{2,1},{3,0},{4,7},{5,6},{6,5},{7,4},{8,11},{9,10},{10,... | collective-permute-start | bytes 24584 | tf_op jit(solution)/shard_map/ppermute | solution.py:312
  87.8 4.6 %collective-permute-start.23 = (f32[8,256]{1,0:T(8,128)S(1)}, f32[8,256]{1,0:T(8,128)S(1)}, u32[]{:S(2)}, u32[]{:S(2)}) collective-permute-start(f32[8,256]{1,0:T(8,128)S(1)} %get-tuple-element.46.refs_1_), channel_id=1, source_target_pairs={{0,2},{1,3},{2,0},{3,1},{4,6},{5,7},{6,4},{7,5},{8,10},{9,11},{10,... | collective-permute-start | bytes 24584 | tf_op jit(solution)/shard_map/ppermute | solution.py:312
  88.4 4.0 %collective-permute-start.22 = (f32[8,256]{1,0:T(8,128)S(1)}, f32[8,256]{1,0:T(8,128)S(1)}, u32[]{:S(2)}, u32[]{:S(2)}) collective-permute-start(f32[8,256]{1,0:T(8,128)S(1)} %get-tuple-element.46.refs_1_), channel_id=1, source_target_pairs={{0,1},{1,0},{2,3},{3,2},{4,5},{5,4},{6,7},{7,6},{8,9},{9,8},{10,11... | collective-permute-start | bytes 24584 | tf_op jit(solution)/shard_map/ppermute | solution.py:312

commit v3 on v2

--- a/solution.py
+++ b/solution.py
@@ -6,11 +6,6 @@
 from jax.sharding import PartitionSpec as P
 
 
-TIME_PAIR = True
-RAW_PAIR = True
-MB_HALF = True
-MB_TREE = False
-EARLY = 5
 ridge_share = 0.1
 epsilon = 1e-06
 contraction_bound = 1e-3
@@ -148,28 +143,24 @@
         at += part.shape[0]
 
 
-def peers(count, paired):
-    if not paired:
-        return [], list(range(1, count))
-    return [(j, j + 1) for j in range(1, count - 1, 2)], [count - 1]
-
-
-def place_blocks(factor_ref, place, core, own_ref, mine_ref, partner_ref, paired):
+def peers(count):
+    return [(j, j + 1) for j in range(1, count - 1, 2)], count - 1
+
+
+def place_blocks(factor_ref, place, core, own_ref, mine_ref, partner_ref):
     rows = own_ref.shape[0]
     half = rows // 2
     factor_ref[at_rows(place, rows), :] = own_ref[...]
-    pairs, shared = peers(factor_ref.shape[0] // rows, paired)
+    pairs, last = peers(factor_ref.shape[0] // rows)
     for i, (first, second) in enumerate(pairs):
         step = second - first
         taken = slice(i * rows, (i + 1) * rows)
         factor_ref[at_rows(jnp.bitwise_xor(place, first + core * step), rows), :] = mine_ref[taken, :]
         factor_ref[at_rows(jnp.bitwise_xor(place, second - core * step), rows), :] = partner_ref[taken, :]
-    for i, step in enumerate(shared):
-        start = len(pairs) * rows + i * half
-        taken = slice(start, start + half)
-        at = jnp.bitwise_xor(place, step) * 2
-        factor_ref[at_rows(at + core, half), :] = mine_ref[taken, :]
-        factor_ref[at_rows(at + 1 - core, half), :] = partner_ref[taken, :]
+    taken = slice(len(pairs) * rows, len(pairs) * rows + half)
+    at = jnp.bitwise_xor(place, last) * 2
+    factor_ref[at_rows(at + core, half), :] = mine_ref[taken, :]
+    factor_ref[at_rows(at + 1 - core, half), :] = partner_ref[taken, :]
 
 
 def sum_kernel(*refs):
@@ -188,7 +179,7 @@
 
 def first_inverse_kernel(species_ref, own_ref, mine_ref, partner_ref,
                          c_gram_ref, matrix_ref, inverse_ref, factor_ref, work_ref):
-    place_blocks(factor_ref, place_of("tm"), place_of("space") % 2, own_ref, mine_ref, partner_ref, TIME_PAIR)
+    place_blocks(factor_ref, place_of("tm"), place_of("space") % 2, own_ref, mine_ref, partner_ref)
     c_gram = gram(factor_ref[...])
     c_gram_ref[...] = c_gram
     matrix = regularized(gram(species_ref[...]) * c_gram)
@@ -209,12 +200,8 @@
         total = total + side_ref[s] * raw_ref[pl.ds(s, 1), :]
     m_b_ref[...] = total
     half = keep_ref.shape[0]
-    if MB_HALF:
-        keep_ref[...] = m_b_ref[at_rows(core, half), :]
-        send_ref[rows:, :] = m_b_ref[at_rows(1 - core, half), :]
-    else:
-        keep_ref[...] = total
-        send_ref[rows:, :] = total
+    keep_ref[...] = m_b_ref[at_rows(core, half), :]
+    send_ref[rows:, :] = m_b_ref[at_rows(1 - core, half), :]
 
 
 def chip_kernel(raw_ref, keep_ref, received_ref, block_ref, m_b_ref):
@@ -228,7 +215,7 @@
 def space_gram_kernel(c_gram_ref, own_ref, mine_ref, partner_ref,
                       a_gram_ref, matrix_ref, scale_ref, out_ref, factor_ref):
     place = place_of("space")
-    place_blocks(factor_ref, place // 2, place % 2, own_ref, mine_ref, partner_ref, RAW_PAIR)
+    place_blocks(factor_ref, place // 2, place % 2, own_ref, mine_ref, partner_ref)
     raw_gram = gram(factor_ref[...])
     eye = eye_mask(raw_gram.shape[0])
     diagonal = jnp.where(eye, raw_gram, 0.0)
@@ -254,18 +241,14 @@
     inverse_ref[...] = inverse + dot(inverse, left)
 
 
-def species_kernel(scale_ref, matrix_ref, inverse_ref, side_ref, rest_ref, *refs):
-    *parts, species_ref, scaled_ref, send_ref = refs
+def species_kernel(scale_ref, matrix_ref, inverse_ref, side_ref, rest_ref, mine_ref, partner_ref,
+                   species_ref, scaled_ref, send_ref):
     core = place_of("space") % 2
     scale = scale_ref[0:1, :]
-    if MB_HALF:
-        mine_ref, partner_ref = parts
-        half = mine_ref.shape[0]
-        scaled_ref[at_rows(core, half), :] = mine_ref[...]
-        scaled_ref[at_rows(1 - core, half), :] = partner_ref[...]
-        m_b = scaled_ref[...] * scale
-    else:
-        m_b = tree_sum([part[...] for part in parts]) * scale
+    half = mine_ref.shape[0]
+    scaled_ref[at_rows(core, half), :] = mine_ref[...]
+    scaled_ref[at_rows(1 - core, half), :] = partner_ref[...]
+    m_b = scaled_ref[...] * scale
     raw = solve(m_b, matrix_ref[...], inverse_ref[...])
     species = raw * lax.rsqrt(jnp.mean(raw * raw, axis=0, keepdims=True) + epsilon)
     species_ref[...] = species
@@ -355,7 +338,7 @@
         return exchange(value, "space", 1, devices)
 
     def block_from(block, half, axis):
-        pairs, shared = peers(blocks, TIME_PAIR) if axis == "tm" else peers(chips, RAW_PAIR)
+        pairs, last = peers(blocks if axis == "tm" else chips)
         received = []
         for steps in pairs:
             if axis == "tm":
@@ -366,10 +349,8 @@
             else:
                 turns = [(s, s ^ (2 * steps[s % 2])) for s in range(devices)]
                 received.append(lax.ppermute(block, "space", turns))
-        for j in shared:
-            step, count = (j, blocks) if axis == "tm" else (2 * j, devices)
-            received.append(exchange(half, axis, step, count))
-        return received
+        step, count = (last, blocks) if axis == "tm" else (2 * last, devices)
+        return received + [exchange(half, axis, step, count)]
 
     def pack(after, parts):
         return run(pack_kernel, [local(sum(part.shape[0] for part in parts), rank)], 0.3)(after, *parts)[0]
@@ -378,7 +359,7 @@
         return run(sum_kernel, [local(*parts[0].shape)], 0.3)(*parts)[0]
 
     half_steps = step_count // 2
-    half_species = species_count // 2 if MB_HALF else species_count
+    half_species = species_count // 2
 
     outside = pl.BlockSpec(memory_space=pltpu.HBM)
     time_half, time_here, species_here = pl.pallas_call(
@@ -389,7 +370,7 @@
         scratch_shapes=[pltpu.SemaphoreType.DMA((3,))],
         cost_estimate=pl.CostEstimate(flops=int(10 * flops_per_micro), bytes_accessed=10**8, transcendentals=0),
         compiler_params=pltpu.CompilerParams(vmem_limit_bytes=vmem_limit),
-        name="load_factors",
+        name="load",
     )(*[pltpu.with_memory_space_constraint(x, pltpu.HBM) for x in (time_factor, species_factor)])
     received = block_from(time_factor, time_half, "tm")
     m_a, side = run(
@@ -410,10 +391,9 @@
         [local(species_count, rank)],
     )(matrix, inverse, side, *m_a_parts)
     received = to_partner(send)
+    early = 5 * species_count // 8
     time_sides = []
-    for first, count in (
-        (0, EARLY * species_count // 8), (EARLY * species_count // 8, species_count - EARLY * species_count // 8)
-    ):
+    for first, count in ((0, early), (early, species_count - early)):
         time_sides += run(
             lambda *refs, first=first: time_side_kernel(species_count, first, *refs),
             [local(count, step_count, rank)],
@@ -422,19 +402,13 @@
     chip_block, m_b = run(chip_kernel, [local(2 * row_count, rank), local(half_species, rank)], 0.3)(
         raw, keep, received
     )
-    if not MB_TREE:
-        m_b = add(over_time(m_b))
-    step = 1
-    while MB_TREE and step < blocks:
-        m_b = add([m_b, exchange(m_b, "tm", step, blocks)])
-        step *= 2
+    m_b = add(over_time(m_b))
     raw_blocks = block_from(chip_block, raw, "space")
     m_b_parts = over_chips(m_b)
     mine = pack(m_b, raw_blocks)
     partner = to_partner(mine)
-    if MB_HALF:
-        m_b = add(m_b_parts)
-        m_b_parts = [m_b, to_partner(m_b)]
+    m_b = add(m_b_parts)
+    m_b_partner = to_partner(m_b)
     a_gram, matrix, scale, space_out = run(
         space_gram_kernel, [square, square, local(8, rank), local(row_count, rank)], 1.5, [local(total_rows, rank)]
     )(c_gram, chip_block, mine, partner)
@@ -442,7 +416,7 @@
 
     species, scaled, m_c_send = run(
         species_kernel, [local(species_count, rank), local(species_count, rank), local(half_steps, rank)], 1.5
-    )(scale, matrix, inverse, *time_sides, *m_b_parts)
+    )(scale, matrix, inverse, *time_sides, m_b, m_b_partner)
 
     m_c_received = to_partner(m_c_send)
     (m_c_keep,) = run(time_half_kernel, [local(half_steps, rank)], 1)(*time_sides, scaled)

time: 93.2 us -> 93.2 us (level)
  no operation moved by 1% of the time
where the time goes in v3:
time: 93.2 us; the launch traced here: 93.1 us
  Pallas kernels  48 us (52%)
  starting transfers between devices  30.1 us (32%)
  waiting for transfers between devices  12.9 us (14%)
  local copies, waits for them, and re-layouts  1.26 us (1%)
    pallas_call x20, Pallas kernels, placed(): call(*[pltpu.with_memory_space_constraint(x, pltpu.VMEM) for x in operands])  47 us
    ppermute x23, starting transfers between devices, exchange(): return lax.ppermute(value, axis, [(i, i ^ step) for i in range(count)])  25.4 us
    ppermute x23, waiting for transfers between devices, exchange(): return lax.ppermute(value, axis, [(i, i ^ step) for i in range(count)])  12.9 us
    ppermute x1, starting transfers between devices, block_from(): received.append(lax.ppermute(block, ('space', 'tm'), turns))  3.12 us
  transfers between devices with their start and end apart: 25, of which 12 were waited for; matrix products, arithmetic and copies ran while one was open for 1% of the time, Pallas kernels for 48%

profile of v3, /device:TPU:0, one launch (start us, length us, event | category | flops | bytes accessed | tf_op | source)
XLA Modules:
  0.0 93.1 jit_solution(15566696484900346444)
XLA Ops:
  0.6 3.1 %collective-permute-start = (f32[128,256]{1,0:T(8,128)}, f32[128,256]{1,0:T(8,128)S(1)}, u32[]{:S(2)}, u32[]{:S(2)}) collective-permute-start(f32[128,256]{1,0:T(8,128)} %time_hbm.1), channel_id=1, source_target_pairs={{0,1},{1,0},{2,3},{3,2},{4,6},{5,7},{6,4},{7,5},{8,9},{9,8},{10,11... | collective-permute-start | bytes 393224 | tf_op jit(solution)/shard_map/ppermute | solution.py:348
  3.8 1.0 %load.1 = (f32[64,256]{1,0:T(8,128)S(1)}, f32[128,256]{1,0:T(8,128)S(1)}, f32[64,256]{1,0:T(8,128)S(1)}) custom-call(f32[128,256]{1,0:T(8,128)} %time_hbm.1, f32[64,256]{1,0:T(8,128)} %species_hbm.1), custom_call_target="tpu_custom_call" | custom-call | flops 10000000000 | bytes 100000000 | tf_op jit(solution)/shard_map/load/pallas_call | solution.py:365
  4.8 2.6 %collective-permute-start.1 = (f32[64,256]{1,0:T(8,128)S(1)}, f32[64,256]{1,0:T(8,128)S(1)}, u32[]{:S(2)}, u32[]{:S(2)}) collective-permute-start(f32[64,256]{1,0:T(8,128)S(1)} %get-tuple-element.28), channel_id=1, source_target_pairs={{0,3},{1,2},{2,1},{3,0},{4,7},{5,6},{6,5},{7,4},{8,11},{9,10},{10,... | collective-permute-start | bytes 196616 | tf_op jit(solution)/shard_map/ppermute | solution.py:295
  7.4 1.3 %shard_map.58 = (f32[64,256]{1,0:T(8,128)S(1)}, f32[64,64,256]{2,1,0:T(8,128)S(1)}) custom-call(f32[4096,128]{1,0:T(8,128)S(1)} %bitcast.1, f32[128,256]{1,0:T(8,128)S(1)} %get-tuple-element.26.time_ref.own_ref, f32[64,256]{1,0:T(8,128)S(1)} %get-tuple-element.25.species_ref), custom_call_target="tpu_custom_call" | custom-call | flops 2000000000 | tf_op jit(solution)/shard_map/pallas_call | solution.py:309
  8.7 2.6 %collective-permute-done.1.refs_1_ = f32[64,256]{1,0:T(8,128)S(1)} collective-permute-done((f32[64,256]{1,0:T(8,128)S(1)}, f32[64,256]{1,0:T(8,128)S(1)}, u32[]{:S(2)}, u32[]{:S(2)}) %collective-permute-start.1) | collective-permute-done | bytes 65568 | tf_op jit(solution)/shard_map/ppermute | solution.py:295
  11.4 2.4 %collective-permute-start.5 = (f32[64,256]{1,0:T(8,128)S(1)}, f32[64,256]{1,0:T(8,128)S(1)}, u32[]{:S(2)}, u32[]{:S(2)}) collective-permute-start(f32[64,256]{1,0:T(8,128)S(1)} %get-tuple-element.27.after_ref.refs_0_), channel_id=1, source_target_pairs={{0,3},{1,2},{2,1},{3,0},{4,7},{5,6},{6,5},{7,4},{8,11},{9,10},{10,... | collective-permute-start | bytes 196616 | tf_op jit(solution)/shard_map/ppermute | solution.py:295
  13.8 0.2 collective-permute-start.4
  14.0 1.8 %collective-permute-start.3 = (f32[64,256]{1,0:T(8,128)S(1)}, f32[64,256]{1,0:T(8,128)S(1)}, u32[]{:S(2)}, u32[]{:S(2)}) collective-permute-start(f32[64,256]{1,0:T(8,128)S(1)} %get-tuple-element.27.after_ref.refs_0_), channel_id=1, source_target_pairs={{0,1},{1,0},{2,3},{3,2},{4,5},{5,4},{6,7},{7,6},{8,9},{9,8},{10,11... | collective-permute-start | bytes 196616 | tf_op jit(solution)/shard_map/ppermute | solution.py:295
  15.9 35.9 %shard_map.60 = (f32[256,256]{1,0:T(8,128)S(1)}, f32[256,256]{1,0:T(8,128)S(1)}, f32[256,256]{1,0:T(8,128)S(1)}) custom-call(f32[64,256]{1,0:T(8,128)S(1)} %get-tuple-element.25.species_ref, f32[128,256]{1,0:T(8,128)S(1)} %get-tuple-element.26.time_ref.own_ref, f32[192,256]{1,0:T(8,128)S(1)} %shard_map.59.mine_ref, ...), custom_call_target="tpu_custom_call" | custom-call | flops 2000000000 | tf_op jit(solution)/shard_map/pallas_call | solution.py:309
  51.8 1.1 %shard_map.61 = (f32[64,256]{1,0:T(8,128)S(1)}, f32[32,256]{1,0:T(8,128)S(1)}, f32[96,256]{1,0:T(8,128)S(1)}) custom-call(f32[256,256]{1,0:T(8,128)S(1)} %get-tuple-element.30.matrix_ref, f32[256,256]{1,0:T(8,128)S(1)} %get-tuple-element.31.inverse_ref, f32[64,64,256]{2,1,0:T(8,128)S(1)} %get-tuple-element.32.side_ref, ...), custom_call_target="tpu_custom_call" | custom-call | flops 1000000000 | tf_op jit(solution)/shard_map/pallas_call | solution.py:309
  52.9 0.1 collective-permute-start.6
  53.0 1.3 %collective-permute-done.6.received_ref = f32[96,256]{1,0:T(8,128)S(1)} collective-permute-done((f32[96,256]{1,0:T(8,128)S(1)}, f32[96,256]{1,0:T(8,128)S(1)}, u32[]{:S(2)}, u32[]{:S(2)}) %collective-permute-start.6) | collective-permute-done | bytes 98336 | tf_op jit(solution)/shard_map/ppermute | solution.py:295
  54.3 1.6 %collective-permute-start.10 = (f32[128,256]{1,0:T(8,128)S(1)}, f32[128,256]{1,0:T(8,128)S(1)}, u32[]{:S(2)}, u32[]{:S(2)}) collective-permute-start(f32[128,256]{1,0:T(8,128)S(1)} %get-tuple-element.36.own_ref), channel_id=1, source_target_pairs={{0,8},{4,20},{8,0},{12,28},{16,24},{20,4},{24,16},{28,12},{1,9},{5... | collective-permute-start | bytes 393224 | tf_op jit(solution)/shard_map/ppermute | solution.py:351
  55.9 1.5 %collective-permute-start.11 = (f32[64,256]{1,0:T(8,128)S(1)}, f32[64,256]{1,0:T(8,128)S(1)}, u32[]{:S(2)}, u32[]{:S(2)}) collective-permute-start(f32[64,256]{1,0:T(8,128)S(1)} %get-tuple-element.33.raw_ref.refs_0_), channel_id=1, source_target_pairs={{0,24},{4,28},{8,16},{12,20},{16,8},{20,12},{24,0},{28,4},{1,25},{... | collective-permute-start | bytes 196616 | tf_op jit(solution)/shard_map/ppermute | solution.py:295
  57.4 2.4 %collective-permute-start.9 = (f32[32,256]{1,0:T(8,128)S(1)}, f32[32,256]{1,0:T(8,128)S(1)}, u32[]{:S(2)}, u32[]{:S(2)}) collective-permute-start(f32[32,256]{1,0:T(8,128)S(1)} %get-tuple-element.37.refs_0_), channel_id=1, source_target_pairs={{0,3},{1,2},{2,1},{3,0},{4,7},{5,6},{6,5},{7,4},{8,11},{9,10},{10,... | collective-permute-start | bytes 98312 | tf_op jit(solution)/shard_map/ppermute | solution.py:295
  59.7 2.0 %collective-permute-start.7 = (f32[32,256]{1,0:T(8,128)S(1)}, f32[32,256]{1,0:T(8,128)S(1)}, u32[]{:S(2)}, u32[]{:S(2)}) collective-permute-start(f32[32,256]{1,0:T(8,128)S(1)} %get-tuple-element.37.refs_0_), channel_id=1, source_target_pairs={{0,1},{1,0},{2,3},{3,2},{4,5},{5,4},{6,7},{7,6},{8,9},{9,8},{10,11... | collective-permute-start | bytes 98312 | tf_op jit(solution)/shard_map/ppermute | solution.py:295
  61.8 1.4 %collective-permute-done.9.refs_3_ = f32[32,256]{1,0:T(8,128)S(1)} collective-permute-done((f32[32,256]{1,0:T(8,128)S(1)}, f32[32,256]{1,0:T(8,128)S(1)}, u32[]{:S(2)}, u32[]{:S(2)}) %collective-permute-start.9) | collective-permute-done | bytes 32800 | tf_op jit(solution)/shard_map/ppermute | solution.py:295
  63.2 1.4 %collective-permute-done.8.refs_2_ = f32[32,256]{1,0:T(8,128)S(1)} collective-permute-done((f32[32,256]{1,0:T(8,128)S(1)}, f32[32,256]{1,0:T(8,128)S(1)}, u32[]{:S(2)}, u32[]{:S(2)}) %collective-permute-start.8) | collective-permute-done | bytes 32800 | tf_op jit(solution)/shard_map/ppermute | solution.py:295
  64.7 1.1 %shard_map.67.side_ref = f32[40,128,256]{2,1,0:T(8,128)S(1)} custom-call(f32[64,256]{1,0:T(8,128)S(1)} %get-tuple-element.33.raw_ref.refs_0_, f32[4096,128]{1,0:T(8,128)S(1)} %bitcast.2), custom_call_target="tpu_custom_call" | custom-call | flops 1250000000 | tf_op jit(solution)/shard_map/pallas_call | solution.py:309
  65.8 1.5 %collective-permute-start.15 = (f32[32,256]{1,0:T(8,128)S(1)}, f32[32,256]{1,0:T(8,128)S(1)}, u32[]{:S(2)}, u32[]{:S(2)}) collective-permute-start(f32[32,256]{1,0:T(8,128)S(1)} %shard_map.63.after_ref.refs_0_), channel_id=1, source_target_pairs={{0,24},{4,28},{8,16},{12,20},{16,8},{20,12},{24,0},{28,4},{1,25},{... | collective-permute-start | bytes 98312 | tf_op jit(solution)/shard_map/ppermute | solution.py:295
  67.3 1.5 %collective-permute-start.14 = (f32[32,256]{1,0:T(8,128)S(1)}, f32[32,256]{1,0:T(8,128)S(1)}, u32[]{:S(2)}, u32[]{:S(2)}) collective-permute-start(f32[32,256]{1,0:T(8,128)S(1)} %shard_map.63.after_ref.refs_0_), channel_id=1, source_target_pairs={{0,16},{4,20},{8,24},{12,28},{16,0},{20,4},{24,8},{28,12},{1,17},{... | collective-permute-start | bytes 98312 | tf_op jit(solution)/shard_map/ppermute | solution.py:295
  68.9 0.5 collective-permute-start.13
  69.4 0.7 shard_map.68.rest_ref
  70.1 0.6 collective-permute-done.15.refs_3_
  70.7 0.6 collective-permute-done.14.refs_2_
  71.3 1.5 %collective-permute-done.13.refs_1_ = f32[32,256]{1,0:T(8,128)S(1)} collective-permute-done((f32[32,256]{1,0:T(8,128)S(1)}, f32[32,256]{1,0:T(8,128)S(1)}, u32[]{:S(2)}, u32[]{:S(2)}) %collective-permute-start.13) | collective-permute-done | bytes 32800 | tf_op jit(solution)/shard_map/ppermute | solution.py:295
  72.9 1.0 %shard_map.65 = (f32[256,256]{1,0:T(8,128)S(1)}, f32[256,256]{1,0:T(8,128)S(1)}, f32[8,256]{1,0:T(8,128)S(1)}, f32[64,256]{1,0:T(8,128)S(1)}) custom-call(f32[256,256]{1,0:T(8,128)S(1)} %get-tuple-element.29.c_gram_ref, f32[128,256]{1,0:T(8,128)S(1)} %get-tuple-element.36.own_ref, f32[192,256]{1,0:T(8,128)S(1)} %shard_map.64.mine_ref, ...), custom_call_target="tpu_custom_call" | custom-call | flops 1500000000 | tf_op jit(solution)/shard_map/pallas_call | solution.py:309
  73.9 0.7 shard_map.66.inverse_ref
  74.6 1.2 %shard_map.70 = (f32[64,256]{1,0:T(8,128)S(1)}, f32[64,256]{1,0:T(8,128)S(1)}, f32[64,256]{1,0:T(8,128)S(1)}) custom-call(f32[8,256]{1,0:T(8,128)S(1)} %get-tuple-element.39.scale_ref, f32[256,256]{1,0:T(8,128)S(1)} %get-tuple-element.40.matrix_ref, f32[256,256]{1,0:T(8,128)S(1)} %shard_map.66.inverse_ref, f32[40,128,256]{2,1,0:T(8,128)S(1)} %shard_map.67.side_ref, ...), custom_call_target="tpu_custom_call" | custom-call | flops 1500000000 | tf_op jit(solution)/shard_map/pallas_call | solution.py:309
  75.8 0.6 collective-permute-start.17
  76.3 0.4 shard_map.73.refs_0_
  76.8 0.5 collective-permute-done.17.refs_1_
  77.2 0.5 collective-permute-start.20
  77.8 1.5 %collective-permute-start.19 = (f32[64,256]{1,0:T(8,128)S(1)}, f32[64,256]{1,0:T(8,128)S(1)}, u32[]{:S(2)}, u32[]{:S(2)}) collective-permute-start(f32[64,256]{1,0:T(8,128)S(1)} %shard_map.74.refs_0_), channel_id=1, source_target_pairs={{0,16},{4,20},{8,24},{12,28},{16,0},{20,4},{24,8},{28,12},{1,17},{... | collective-permute-start | bytes 196616 | tf_op jit(solution)/shard_map/ppermute | solution.py:295
  79.3 1.5 %collective-permute-start.18 = (f32[64,256]{1,0:T(8,128)S(1)}, f32[64,256]{1,0:T(8,128)S(1)}, u32[]{:S(2)}, u32[]{:S(2)}) collective-permute-start(f32[64,256]{1,0:T(8,128)S(1)} %shard_map.74.refs_0_), channel_id=1, source_target_pairs={{0,8},{4,12},{8,0},{12,4},{16,24},{20,28},{24,16},{28,20},{1,9},{5... | collective-permute-start | bytes 196616 | tf_op jit(solution)/shard_map/ppermute | solution.py:295
  80.8 0.6 shard_map.71.matrix_ref
  81.4 1.8 %collective-permute-done.20.refs_3_ = f32[64,256]{1,0:T(8,128)S(1)} collective-permute-done((f32[64,256]{1,0:T(8,128)S(1)}, f32[64,256]{1,0:T(8,128)S(1)}, u32[]{:S(2)}, u32[]{:S(2)}) %collective-permute-start.20) | collective-permute-done | bytes 65568 | tf_op jit(solution)/shard_map/ppermute | solution.py:295
  83.2 0.1 collective-permute-done.19.refs_2_
  83.3 0.3 collective-permute-done.18.refs_1_
  83.7 1.8 %shard_map.72.inverse_ref = f32[256,256]{1,0:T(8,128)S(1)} custom-call(f32[256,256]{1,0:T(8,128)S(1)} %shard_map.71.matrix_ref), custom_call_target="tpu_custom_call" | custom-call | flops 1000000000 | tf_op jit(solution)/shard_map/pallas_call | solution.py:309
  85.5 0.3 shard_map.76
  85.8 2.0 %collective-permute-start.24 = (f32[8,256]{1,0:T(8,128)S(1)}, f32[8,256]{1,0:T(8,128)S(1)}, u32[]{:S(2)}, u32[]{:S(2)}) collective-permute-start(f32[8,256]{1,0:T(8,128)S(1)} %get-tuple-element.46.refs_1_), channel_id=1, source_target_pairs={{0,3},{1,2},{2,1},{3,0},{4,7},{5,6},{6,5},{7,4},{8,11},{9,10},{10,... | collective-permute-start | bytes 24584 | tf_op jit(solution)/shard_map/ppermute | solution.py:295
  87.8 0.6 collective-permute-start.23
  88.4 1.8 %collective-permute-start.22 = (f32[8,256]{1,0:T(8,128)S(1)}, f32[8,256]{1,0:T(8,128)S(1)}, u32[]{:S(2)}, u32[]{:S(2)}) collective-permute-start(f32[8,256]{1,0:T(8,128)S(1)} %get-tuple-element.46.refs_1_), channel_id=1, source_target_pairs={{0,1},{1,0},{2,3},{3,2},{4,5},{5,4},{6,7},{7,6},{8,9},{9,8},{10,11... | collective-permute-start | bytes 24584 | tf_op jit(solution)/shard_map/ppermute | solution.py:295
  90.2 0.6 copy.7
  90.9 0.6 copy.6
  91.5 0.9 collective-permute-done.23.refs_3_
  92.4 0.7 shard_map.77
  (27 shorter events, 0.4 us)
Async XLA Ops:
  0.6 6.8 %copy-start = (f32[64,64,128]{2,1,0:T(8,128)S(1)}, f32[64,64,128]{2,1,0:T(8,128)}, u32[]{:S(2)}) copy-start(f32[64,64,128]{2,1,0:T(8,128)} %param.3) | copy-start | bytes 6291460
  0.6 10.7 %collective-permute-start = (f32[128,256]{1,0:T(8,128)}, f32[128,256]{1,0:T(8,128)S(1)}, u32[]{:S(2)}, u32[]{:S(2)}) collective-permute-start(f32[128,256]{1,0:T(8,128)} %time_hbm.1), channel_id=1, source_target_pairs={{0,1},{1,0},{2,3},{3,2},{4,6},{5,7},{6,4},{7,5},{8,9},{9,8},{10,11... | collective-permute-start | bytes 393224 | tf_op jit(solution)/shard_map/ppermute | solution.py:348
  4.8 6.5 %collective-permute-start.1 = (f32[64,256]{1,0:T(8,128)S(1)}, f32[64,256]{1,0:T(8,128)S(1)}, u32[]{:S(2)}, u32[]{:S(2)}) collective-permute-start(f32[64,256]{1,0:T(8,128)S(1)} %get-tuple-element.28), channel_id=1, source_target_pairs={{0,3},{1,2},{2,1},{3,0},{4,7},{5,6},{6,5},{7,4},{8,11},{9,10},{10,... | collective-permute-start | bytes 196616 | tf_op jit(solution)/shard_map/ppermute | solution.py:295
  11.3 4.5 %collective-permute-start.2 = (f32[192,256]{1,0:T(8,128)S(1)}, f32[192,256]{1,0:T(8,128)S(1)}, u32[]{:S(2)}, u32[]{:S(2)}) collective-permute-start(f32[192,256]{1,0:T(8,128)S(1)} %shard_map.59.mine_ref), channel_id=1, source_target_pairs={{0,4},{4,0},{8,12},{12,8},{16,20},{20,16},{24,28},{28,24},{1,5},{5... | collective-permute-start | bytes 589832 | tf_op jit(solution)/shard_map/ppermute | solution.py:295
  11.4 40.4 %collective-permute-start.5 = (f32[64,256]{1,0:T(8,128)S(1)}, f32[64,256]{1,0:T(8,128)S(1)}, u32[]{:S(2)}, u32[]{:S(2)}) collective-permute-start(f32[64,256]{1,0:T(8,128)S(1)} %get-tuple-element.27.after_ref.refs_0_), channel_id=1, source_target_pairs={{0,3},{1,2},{2,1},{3,0},{4,7},{5,6},{6,5},{7,4},{8,11},{9,10},{10,... | collective-permute-start | bytes 196616 | tf_op jit(solution)/shard_map/ppermute | solution.py:295
  13.8 38.0 %collective-permute-start.4 = (f32[64,256]{1,0:T(8,128)S(1)}, f32[64,256]{1,0:T(8,128)S(1)}, u32[]{:S(2)}, u32[]{:S(2)}) collective-permute-start(f32[64,256]{1,0:T(8,128)S(1)} %get-tuple-element.27.after_ref.refs_0_), channel_id=1, source_target_pairs={{0,2},{1,3},{2,0},{3,1},{4,6},{5,7},{6,4},{7,5},{8,10},{9,11},{10,... | collective-permute-start | bytes 196616 | tf_op jit(solution)/shard_map/ppermute | solution.py:295
  14.0 37.7 %collective-permute-start.3 = (f32[64,256]{1,0:T(8,128)S(1)}, f32[64,256]{1,0:T(8,128)S(1)}, u32[]{:S(2)}, u32[]{:S(2)}) collective-permute-start(f32[64,256]{1,0:T(8,128)S(1)} %get-tuple-element.27.after_ref.refs_0_), channel_id=1, source_target_pairs={{0,1},{1,0},{2,3},{3,2},{4,5},{5,4},{6,7},{7,6},{8,9},{9,8},{10,11... | collective-permute-start | bytes 196616 | tf_op jit(solution)/shard_map/ppermute | solution.py:295
  52.9 1.4 %collective-permute-start.6 = (f32[96,256]{1,0:T(8,128)S(1)}, f32[96,256]{1,0:T(8,128)S(1)}, u32[]{:S(2)}, u32[]{:S(2)}) collective-permute-start(f32[96,256]{1,0:T(8,128)S(1)} %get-tuple-element.35), channel_id=1, source_target_pairs={{0,4},{4,0},{8,12},{12,8},{16,20},{20,16},{24,28},{28,24},{1,5},{5... | collective-permute-start | bytes 294920 | tf_op jit(solution)/shard_map/ppermute | solution.py:295
  54.3 10.2 %collective-permute-start.10 = (f32[128,256]{1,0:T(8,128)S(1)}, f32[128,256]{1,0:T(8,128)S(1)}, u32[]{:S(2)}, u32[]{:S(2)}) collective-permute-start(f32[128,256]{1,0:T(8,128)S(1)} %get-tuple-element.36.own_ref), channel_id=1, source_target_pairs={{0,8},{4,20},{8,0},{12,28},{16,24},{20,4},{24,16},{28,12},{1,9},{5... | collective-permute-start | bytes 393224 | tf_op jit(solution)/shard_map/ppermute | solution.py:351
  55.9 8.7 %collective-permute-start.11 = (f32[64,256]{1,0:T(8,128)S(1)}, f32[64,256]{1,0:T(8,128)S(1)}, u32[]{:S(2)}, u32[]{:S(2)}) collective-permute-start(f32[64,256]{1,0:T(8,128)S(1)} %get-tuple-element.33.raw_ref.refs_0_), channel_id=1, source_target_pairs={{0,24},{4,28},{8,16},{12,20},{16,8},{20,12},{24,0},{28,4},{1,25},{... | collective-permute-start | bytes 196616 | tf_op jit(solution)/shard_map/ppermute | solution.py:295
  57.4 5.8 %collective-permute-start.9 = (f32[32,256]{1,0:T(8,128)S(1)}, f32[32,256]{1,0:T(8,128)S(1)}, u32[]{:S(2)}, u32[]{:S(2)}) collective-permute-start(f32[32,256]{1,0:T(8,128)S(1)} %get-tuple-element.37.refs_0_), channel_id=1, source_target_pairs={{0,3},{1,2},{2,1},{3,0},{4,7},{5,6},{6,5},{7,4},{8,11},{9,10},{10,... | collective-permute-start | bytes 98312 | tf_op jit(solution)/shard_map/ppermute | solution.py:295
  59.7 4.8 %collective-permute-start.8 = (f32[32,256]{1,0:T(8,128)S(1)}, f32[32,256]{1,0:T(8,128)S(1)}, u32[]{:S(2)}, u32[]{:S(2)}) collective-permute-start(f32[32,256]{1,0:T(8,128)S(1)} %get-tuple-element.37.refs_0_), channel_id=1, source_target_pairs={{0,2},{1,3},{2,0},{3,1},{4,6},{5,7},{6,4},{7,5},{8,10},{9,11},{10,... | collective-permute-start | bytes 98312 | tf_op jit(solution)/shard_map/ppermute | solution.py:295
  59.7 4.8 %collective-permute-start.7 = (f32[32,256]{1,0:T(8,128)S(1)}, f32[32,256]{1,0:T(8,128)S(1)}, u32[]{:S(2)}, u32[]{:S(2)}) collective-permute-start(f32[32,256]{1,0:T(8,128)S(1)} %get-tuple-element.37.refs_0_), channel_id=1, source_target_pairs={{0,1},{1,0},{2,3},{3,2},{4,5},{5,4},{6,7},{7,6},{8,9},{9,8},{10,11... | collective-permute-start | bytes 98312 | tf_op jit(solution)/shard_map/ppermute | solution.py:295
  64.6 8.3 %collective-permute-start.12 = (f32[192,256]{1,0:T(8,128)S(1)}, f32[192,256]{1,0:T(8,128)S(1)}, u32[]{:S(2)}, u32[]{:S(2)}) collective-permute-start(f32[192,256]{1,0:T(8,128)S(1)} %shard_map.64.mine_ref), channel_id=1, source_target_pairs={{0,4},{4,0},{8,12},{12,8},{16,20},{20,16},{24,28},{28,24},{1,5},{5... | collective-permute-start | bytes 589832 | tf_op jit(solution)/shard_map/ppermute | solution.py:295
  65.8 4.9 %collective-permute-start.15 = (f32[32,256]{1,0:T(8,128)S(1)}, f32[32,256]{1,0:T(8,128)S(1)}, u32[]{:S(2)}, u32[]{:S(2)}) collective-permute-start(f32[32,256]{1,0:T(8,128)S(1)} %shard_map.63.after_ref.refs_0_), channel_id=1, source_target_pairs={{0,24},{4,28},{8,16},{12,20},{16,8},{20,12},{24,0},{28,4},{1,25},{... | collective-permute-start | bytes 98312 | tf_op jit(solution)/shard_map/ppermute | solution.py:295
  67.3 4.0 %collective-permute-start.14 = (f32[32,256]{1,0:T(8,128)S(1)}, f32[32,256]{1,0:T(8,128)S(1)}, u32[]{:S(2)}, u32[]{:S(2)}) collective-permute-start(f32[32,256]{1,0:T(8,128)S(1)} %shard_map.63.after_ref.refs_0_), channel_id=1, source_target_pairs={{0,16},{4,20},{8,24},{12,28},{16,0},{20,4},{24,8},{28,12},{1,17},{... | collective-permute-start | bytes 98312 | tf_op jit(solution)/shard_map/ppermute | solution.py:295
  68.9 3.9 %collective-permute-start.13 = (f32[32,256]{1,0:T(8,128)S(1)}, f32[32,256]{1,0:T(8,128)S(1)}, u32[]{:S(2)}, u32[]{:S(2)}) collective-permute-start(f32[32,256]{1,0:T(8,128)S(1)} %shard_map.63.after_ref.refs_0_), channel_id=1, source_target_pairs={{0,8},{4,12},{8,0},{12,4},{16,24},{20,28},{24,16},{28,20},{1,9},{5... | collective-permute-start | bytes 98312 | tf_op jit(solution)/shard_map/ppermute | solution.py:295
  72.8 1.8 %collective-permute-start.16 = (f32[32,256]{1,0:T(8,128)S(1)}, f32[32,256]{1,0:T(8,128)S(1)}, u32[]{:S(2)}, u32[]{:S(2)}) collective-permute-start(f32[32,256]{1,0:T(8,128)S(1)} %shard_map.69.mine_ref), channel_id=1, source_target_pairs={{0,4},{4,0},{8,12},{12,8},{16,20},{20,16},{24,28},{28,24},{1,5},{5... | collective-permute-start | bytes 98312 | tf_op jit(solution)/shard_map/ppermute | solution.py:295
  75.8 1.5 %collective-permute-start.17 = (f32[64,256]{1,0:T(8,128)S(1)}, f32[64,256]{1,0:T(8,128)S(1)}, u32[]{:S(2)}, u32[]{:S(2)}) collective-permute-start(f32[64,256]{1,0:T(8,128)S(1)} %get-tuple-element.44), channel_id=1, source_target_pairs={{0,4},{4,0},{8,12},{12,8},{16,20},{20,16},{24,28},{28,24},{1,5},{5... | collective-permute-start | bytes 196616 | tf_op jit(solution)/shard_map/ppermute | solution.py:295
  77.2 5.9 %collective-permute-start.20 = (f32[64,256]{1,0:T(8,128)S(1)}, f32[64,256]{1,0:T(8,128)S(1)}, u32[]{:S(2)}, u32[]{:S(2)}) collective-permute-start(f32[64,256]{1,0:T(8,128)S(1)} %shard_map.74.refs_0_), channel_id=1, source_target_pairs={{0,24},{4,28},{8,16},{12,20},{16,8},{20,12},{24,0},{28,4},{1,25},{... | collective-permute-start | bytes 196616 | tf_op jit(solution)/shard_map/ppermute | solution.py:295
  77.8 5.5 %collective-permute-start.19 = (f32[64,256]{1,0:T(8,128)S(1)}, f32[64,256]{1,0:T(8,128)S(1)}, u32[]{:S(2)}, u32[]{:S(2)}) collective-permute-start(f32[64,256]{1,0:T(8,128)S(1)} %shard_map.74.refs_0_), channel_id=1, source_target_pairs={{0,16},{4,20},{8,24},{12,28},{16,0},{20,4},{24,8},{28,12},{1,17},{... | collective-permute-start | bytes 196616 | tf_op jit(solution)/shard_map/ppermute | solution.py:295
  79.3 4.3 %collective-permute-start.18 = (f32[64,256]{1,0:T(8,128)S(1)}, f32[64,256]{1,0:T(8,128)S(1)}, u32[]{:S(2)}, u32[]{:S(2)}) collective-permute-start(f32[64,256]{1,0:T(8,128)S(1)} %shard_map.74.refs_0_), channel_id=1, source_target_pairs={{0,8},{4,12},{8,0},{12,4},{16,24},{20,28},{24,16},{28,20},{1,9},{5... | collective-permute-start | bytes 196616 | tf_op jit(solution)/shard_map/ppermute | solution.py:295
  83.6 1.9 %collective-permute-start.21 = (f32[64,256]{1,0:T(8,128)S(1)}, f32[64,256]{1,0:T(8,128)S(1)}, u32[]{:S(2)}, u32[]{:S(2)}) collective-permute-start(f32[64,256]{1,0:T(8,128)S(1)} %shard_map.75.mine_ref), channel_id=1, source_target_pairs={{0,4},{4,0},{8,12},{12,8},{16,20},{20,16},{24,28},{28,24},{1,5},{5... | collective-permute-start | bytes 196616 | tf_op jit(solution)/shard_map/ppermute | solution.py:295
  85.8 5.7 %collective-permute-start.24 = (f32[8,256]{1,0:T(8,128)S(1)}, f32[8,256]{1,0:T(8,128)S(1)}, u32[]{:S(2)}, u32[]{:S(2)}) collective-permute-start(f32[8,256]{1,0:T(8,128)S(1)} %get-tuple-element.46.refs_1_), channel_id=1, source_target_pairs={{0,3},{1,2},{2,1},{3,0},{4,7},{5,6},{6,5},{7,4},{8,11},{9,10},{10,... | collective-permute-start | bytes 24584 | tf_op jit(solution)/shard_map/ppermute | solution.py:295
  87.8 4.6 %collective-permute-start.23 = (f32[8,256]{1,0:T(8,128)S(1)}, f32[8,256]{1,0:T(8,128)S(1)}, u32[]{:S(2)}, u32[]{:S(2)}) collective-permute-start(f32[8,256]{1,0:T(8,128)S(1)} %get-tuple-element.46.refs_1_), channel_id=1, source_target_pairs={{0,2},{1,3},{2,0},{3,1},{4,6},{5,7},{6,4},{7,5},{8,10},{9,11},{10,... | collective-permute-start | bytes 24584 | tf_op jit(solution)/shard_map/ppermute | solution.py:295
  88.4 4.0 %collective-permute-start.22 = (f32[8,256]{1,0:T(8,128)S(1)}, f32[8,256]{1,0:T(8,128)S(1)}, u32[]{:S(2)}, u32[]{:S(2)}) collective-permute-start(f32[8,256]{1,0:T(8,128)S(1)} %get-tuple-element.46.refs_1_), channel_id=1, source_target_pairs={{0,1},{1,0},{2,3},{3,2},{4,5},{5,4},{6,7},{7,6},{8,9},{9,8},{10,11... | collective-permute-start | bytes 24584 | tf_op jit(solution)/shard_map/ppermute | solution.py:295

commit v4 on v3

--- a/solution.py
+++ b/solution.py
@@ -9,7 +9,6 @@
 ridge_share = 0.1
 epsilon = 1e-06
 contraction_bound = 1e-3
-highest = lax.Precision.HIGHEST
 f32 = jnp.float32
 bf16 = jnp.bfloat16
 
@@ -18,8 +17,22 @@
 vmem_limit = 24 * 1024 * 1024
 
 
-def dot(a, b, dims=((1,), (0,))):
-    return lax.dot_general(a, b, (dims, ((), ())), precision=highest, preferred_element_type=f32)
+def split3(x):
+    high = x.astype(bf16)
+    rest = x - high.astype(f32)
+    middle = rest.astype(bf16)
+    return high, middle, (rest - middle.astype(f32)).astype(bf16)
+
+
+def dot(a, b):
+    rows = a.shape[0]
+    high, middle, low = split3(a)
+    b_high, b_middle, b_low = split3(b)
+    two = jnp.concatenate([high, middle], axis=0)
+    first = dot_fast(jnp.concatenate([two, low], axis=0), b_high)
+    second = dot_fast(two, b_middle)
+    small = first[2 * rows:] + second[rows:] + dot_fast(high, b_low)
+    return first[:rows] + (first[rows:2 * rows] + second[:rows] + small)
 
 
 def dot_fast(a, b, dims=((1,), (0,))):
@@ -27,7 +40,12 @@
 
 
 def gram(factor):
-    return dot(factor, factor, ((0,), (0,)))
+    n = factor.shape[1]
+    rows_first = ((0,), (0,))
+    high, middle, low = split3(factor)
+    products = dot_fast(high, jnp.concatenate([high, middle, low], axis=1), rows_first)
+    mixed = products[:, n:2 * n] + products[:, 2 * n:]
+    return products[:, :n] + (mixed + mixed.T + dot_fast(middle, middle, rows_first))
 
 
 def split(x):

time: 93.2 us -> 92.3 us (level)
  Pallas kernels: 48 us -> 47 us
    pallas_call x20, Pallas kernels: 47 us -> 46 us  [placed(): call(*[pltpu.with_memory_space_constraint(x, pltpu.VMEM) for x in operands])]
where the time goes in v4:
time: 92.3 us; the launch traced here: 92.2 us
  Pallas kernels  47 us (51%)
  starting transfers between devices  30.1 us (33%)
  waiting for transfers between devices  12.9 us (14%)
  local copies, waits for them, and re-layouts  1.26 us (1%)
    pallas_call x20, Pallas kernels, placed(): call(*[pltpu.with_memory_space_constraint(x, pltpu.VMEM) for x in operands])  46 us
    ppermute x23, starting transfers between devices, exchange(): return lax.ppermute(value, axis, [(i, i ^ step) for i in range(count)])  25.4 us
    ppermute x23, waiting for transfers between devices, exchange(): return lax.ppermute(value, axis, [(i, i ^ step) for i in range(count)])  12.9 us
    ppermute x1, starting transfers between devices, block_from(): received.append(lax.ppermute(block, ('space', 'tm'), turns))  3.12 us
  transfers between devices with their start and end apart: 25, of which 12 were waited for; matrix products, arithmetic and copies ran while one was open for 1% of the time, Pallas kernels for 48%

profile of v4, /device:TPU:0, one launch (start us, length us, event | category | flops | bytes accessed | tf_op | source)
XLA Modules:
  0.0 92.2 jit_solution(3333100769084410102)
XLA Ops:
  0.6 3.1 %collective-permute-start = (f32[128,256]{1,0:T(8,128)}, f32[128,256]{1,0:T(8,128)S(1)}, u32[]{:S(2)}, u32[]{:S(2)}) collective-permute-start(f32[128,256]{1,0:T(8,128)} %time_hbm.1), channel_id=1, source_target_pairs={{0,1},{1,0},{2,3},{3,2},{4,6},{5,7},{6,4},{7,5},{8,9},{9,8},{10,11... | collective-permute-start | bytes 393224 | tf_op jit(solution)/shard_map/ppermute | solution.py:366
  3.8 1.0 %load.1 = (f32[64,256]{1,0:T(8,128)S(1)}, f32[128,256]{1,0:T(8,128)S(1)}, f32[64,256]{1,0:T(8,128)S(1)}) custom-call(f32[128,256]{1,0:T(8,128)} %time_hbm.1, f32[64,256]{1,0:T(8,128)} %species_hbm.1), custom_call_target="tpu_custom_call" | custom-call | flops 10000000000 | bytes 100000000 | tf_op jit(solution)/shard_map/load/pallas_call | solution.py:383
  4.8 2.6 %collective-permute-start.1 = (f32[64,256]{1,0:T(8,128)S(1)}, f32[64,256]{1,0:T(8,128)S(1)}, u32[]{:S(2)}, u32[]{:S(2)}) collective-permute-start(f32[64,256]{1,0:T(8,128)S(1)} %get-tuple-element.28), channel_id=1, source_target_pairs={{0,3},{1,2},{2,1},{3,0},{4,7},{5,6},{6,5},{7,4},{8,11},{9,10},{10,... | collective-permute-start | bytes 196616 | tf_op jit(solution)/shard_map/ppermute | solution.py:313
  7.4 1.3 %shard_map.58 = (f32[64,256]{1,0:T(8,128)S(1)}, f32[64,64,256]{2,1,0:T(8,128)S(1)}) custom-call(f32[4096,128]{1,0:T(8,128)S(1)} %bitcast.1, f32[128,256]{1,0:T(8,128)S(1)} %get-tuple-element.26.time_ref.own_ref, f32[64,256]{1,0:T(8,128)S(1)} %get-tuple-element.25.species_ref), custom_call_target="tpu_custom_call" | custom-call | flops 2000000000 | tf_op jit(solution)/shard_map/pallas_call | solution.py:327
  8.7 2.6 %collective-permute-done.1.refs_1_ = f32[64,256]{1,0:T(8,128)S(1)} collective-permute-done((f32[64,256]{1,0:T(8,128)S(1)}, f32[64,256]{1,0:T(8,128)S(1)}, u32[]{:S(2)}, u32[]{:S(2)}) %collective-permute-start.1) | collective-permute-done | bytes 65568 | tf_op jit(solution)/shard_map/ppermute | solution.py:313
  11.4 2.4 %collective-permute-start.5 = (f32[64,256]{1,0:T(8,128)S(1)}, f32[64,256]{1,0:T(8,128)S(1)}, u32[]{:S(2)}, u32[]{:S(2)}) collective-permute-start(f32[64,256]{1,0:T(8,128)S(1)} %get-tuple-element.27.after_ref.refs_0_), channel_id=1, source_target_pairs={{0,3},{1,2},{2,1},{3,0},{4,7},{5,6},{6,5},{7,4},{8,11},{9,10},{10,... | collective-permute-start | bytes 196616 | tf_op jit(solution)/shard_map/ppermute | solution.py:313
  13.8 0.2 collective-permute-start.4
  14.0 1.8 %collective-permute-start.3 = (f32[64,256]{1,0:T(8,128)S(1)}, f32[64,256]{1,0:T(8,128)S(1)}, u32[]{:S(2)}, u32[]{:S(2)}) collective-permute-start(f32[64,256]{1,0:T(8,128)S(1)} %get-tuple-element.27.after_ref.refs_0_), channel_id=1, source_target_pairs={{0,1},{1,0},{2,3},{3,2},{4,5},{5,4},{6,7},{7,6},{8,9},{9,8},{10,11... | collective-permute-start | bytes 196616 | tf_op jit(solution)/shard_map/ppermute | solution.py:313
  15.9 35.7 %shard_map.60 = (f32[256,256]{1,0:T(8,128)S(1)}, f32[256,256]{1,0:T(8,128)S(1)}, f32[256,256]{1,0:T(8,128)S(1)}) custom-call(f32[64,256]{1,0:T(8,128)S(1)} %get-tuple-element.25.species_ref, f32[128,256]{1,0:T(8,128)S(1)} %get-tuple-element.26.time_ref.own_ref, f32[192,256]{1,0:T(8,128)S(1)} %shard_map.59.mine_ref, ...), custom_call_target="tpu_custom_call" | custom-call | flops 2000000000 | tf_op jit(solution)/shard_map/pallas_call | solution.py:327
  51.6 0.9 shard_map.61
  52.5 0.1 collective-permute-start.6
  52.6 1.3 %collective-permute-done.6.received_ref = f32[96,256]{1,0:T(8,128)S(1)} collective-permute-done((f32[96,256]{1,0:T(8,128)S(1)}, f32[96,256]{1,0:T(8,128)S(1)}, u32[]{:S(2)}, u32[]{:S(2)}) %collective-permute-start.6) | collective-permute-done | bytes 98336 | tf_op jit(solution)/shard_map/ppermute | solution.py:313
  53.9 1.6 %collective-permute-start.10 = (f32[128,256]{1,0:T(8,128)S(1)}, f32[128,256]{1,0:T(8,128)S(1)}, u32[]{:S(2)}, u32[]{:S(2)}) collective-permute-start(f32[128,256]{1,0:T(8,128)S(1)} %get-tuple-element.36.own_ref), channel_id=1, source_target_pairs={{0,8},{4,20},{8,0},{12,28},{16,24},{20,4},{24,16},{28,12},{1,9},{5... | collective-permute-start | bytes 393224 | tf_op jit(solution)/shard_map/ppermute | solution.py:369
  55.4 1.5 %collective-permute-start.11 = (f32[64,256]{1,0:T(8,128)S(1)}, f32[64,256]{1,0:T(8,128)S(1)}, u32[]{:S(2)}, u32[]{:S(2)}) collective-permute-start(f32[64,256]{1,0:T(8,128)S(1)} %get-tuple-element.33.raw_ref.refs_0_), channel_id=1, source_target_pairs={{0,24},{4,28},{8,16},{12,20},{16,8},{20,12},{24,0},{28,4},{1,25},{... | collective-permute-start | bytes 196616 | tf_op jit(solution)/shard_map/ppermute | solution.py:313
  56.9 2.3 %collective-permute-start.9 = (f32[32,256]{1,0:T(8,128)S(1)}, f32[32,256]{1,0:T(8,128)S(1)}, u32[]{:S(2)}, u32[]{:S(2)}) collective-permute-start(f32[32,256]{1,0:T(8,128)S(1)} %get-tuple-element.37.refs_0_), channel_id=1, source_target_pairs={{0,3},{1,2},{2,1},{3,0},{4,7},{5,6},{6,5},{7,4},{8,11},{9,10},{10,... | collective-permute-start | bytes 98312 | tf_op jit(solution)/shard_map/ppermute | solution.py:313
  59.3 2.0 %collective-permute-start.7 = (f32[32,256]{1,0:T(8,128)S(1)}, f32[32,256]{1,0:T(8,128)S(1)}, u32[]{:S(2)}, u32[]{:S(2)}) collective-permute-start(f32[32,256]{1,0:T(8,128)S(1)} %get-tuple-element.37.refs_0_), channel_id=1, source_target_pairs={{0,1},{1,0},{2,3},{3,2},{4,5},{5,4},{6,7},{7,6},{8,9},{9,8},{10,11... | collective-permute-start | bytes 98312 | tf_op jit(solution)/shard_map/ppermute | solution.py:313
  61.3 1.4 %collective-permute-done.9.refs_3_ = f32[32,256]{1,0:T(8,128)S(1)} collective-permute-done((f32[32,256]{1,0:T(8,128)S(1)}, f32[32,256]{1,0:T(8,128)S(1)}, u32[]{:S(2)}, u32[]{:S(2)}) %collective-permute-start.9) | collective-permute-done | bytes 32800 | tf_op jit(solution)/shard_map/ppermute | solution.py:313
  62.7 1.3 %collective-permute-done.8.refs_2_ = f32[32,256]{1,0:T(8,128)S(1)} collective-permute-done((f32[32,256]{1,0:T(8,128)S(1)}, f32[32,256]{1,0:T(8,128)S(1)}, u32[]{:S(2)}, u32[]{:S(2)}) %collective-permute-start.8) | collective-permute-done | bytes 32800 | tf_op jit(solution)/shard_map/ppermute | solution.py:313
  64.2 1.1 %shard_map.67.side_ref = f32[40,128,256]{2,1,0:T(8,128)S(1)} custom-call(f32[64,256]{1,0:T(8,128)S(1)} %get-tuple-element.33.raw_ref.refs_0_, f32[4096,128]{1,0:T(8,128)S(1)} %bitcast.2), custom_call_target="tpu_custom_call" | custom-call | flops 1250000000 | tf_op jit(solution)/shard_map/pallas_call | solution.py:327
  65.4 1.5 %collective-permute-start.15 = (f32[32,256]{1,0:T(8,128)S(1)}, f32[32,256]{1,0:T(8,128)S(1)}, u32[]{:S(2)}, u32[]{:S(2)}) collective-permute-start(f32[32,256]{1,0:T(8,128)S(1)} %shard_map.63.after_ref.refs_0_), channel_id=1, source_target_pairs={{0,24},{4,28},{8,16},{12,20},{16,8},{20,12},{24,0},{28,4},{1,25},{... | collective-permute-start | bytes 98312 | tf_op jit(solution)/shard_map/ppermute | solution.py:313
  66.9 1.5 %collective-permute-start.14 = (f32[32,256]{1,0:T(8,128)S(1)}, f32[32,256]{1,0:T(8,128)S(1)}, u32[]{:S(2)}, u32[]{:S(2)}) collective-permute-start(f32[32,256]{1,0:T(8,128)S(1)} %shard_map.63.after_ref.refs_0_), channel_id=1, source_target_pairs={{0,16},{4,20},{8,24},{12,28},{16,0},{20,4},{24,8},{28,12},{1,17},{... | collective-permute-start | bytes 98312 | tf_op jit(solution)/shard_map/ppermute | solution.py:313
  68.4 0.5 collective-permute-start.13
  68.9 0.7 shard_map.68.rest_ref
  69.7 0.6 collective-permute-done.15.refs_3_
  70.2 0.6 collective-permute-done.14.refs_2_
  70.8 1.5 %collective-permute-done.13.refs_1_ = f32[32,256]{1,0:T(8,128)S(1)} collective-permute-done((f32[32,256]{1,0:T(8,128)S(1)}, f32[32,256]{1,0:T(8,128)S(1)}, u32[]{:S(2)}, u32[]{:S(2)}) %collective-permute-start.13) | collective-permute-done | bytes 32800 | tf_op jit(solution)/shard_map/ppermute | solution.py:313
  72.4 0.8 shard_map.65
  73.2 0.7 shard_map.66.inverse_ref
  74.0 0.9 %shard_map.70 = (f32[64,256]{1,0:T(8,128)S(1)}, f32[64,256]{1,0:T(8,128)S(1)}, f32[64,256]{1,0:T(8,128)S(1)}) custom-call(f32[8,256]{1,0:T(8,128)S(1)} %get-tuple-element.39.scale_ref, f32[256,256]{1,0:T(8,128)S(1)} %get-tuple-element.40.matrix_ref, f32[256,256]{1,0:T(8,128)S(1)} %shard_map.66.inverse_ref, f32[40,128,256]{2,1,0:T(8,128)S(1)} %shard_map.67.side_ref, ...), custom_call_target="tpu_custom_call" | custom-call | flops 1500000000 | tf_op jit(solution)/shard_map/pallas_call | solution.py:327
  74.9 0.6 collective-permute-start.17
  75.5 0.4 shard_map.73.refs_0_
  75.9 0.5 collective-permute-done.17.refs_1_
  76.4 0.5 collective-permute-start.20
  76.9 1.5 %collective-permute-start.19 = (f32[64,256]{1,0:T(8,128)S(1)}, f32[64,256]{1,0:T(8,128)S(1)}, u32[]{:S(2)}, u32[]{:S(2)}) collective-permute-start(f32[64,256]{1,0:T(8,128)S(1)} %shard_map.74.refs_0_), channel_id=1, source_target_pairs={{0,16},{4,20},{8,24},{12,28},{16,0},{20,4},{24,8},{28,12},{1,17},{... | collective-permute-start | bytes 196616 | tf_op jit(solution)/shard_map/ppermute | solution.py:313
  78.4 1.5 %collective-permute-start.18 = (f32[64,256]{1,0:T(8,128)S(1)}, f32[64,256]{1,0:T(8,128)S(1)}, u32[]{:S(2)}, u32[]{:S(2)}) collective-permute-start(f32[64,256]{1,0:T(8,128)S(1)} %shard_map.74.refs_0_), channel_id=1, source_target_pairs={{0,8},{4,12},{8,0},{12,4},{16,24},{20,28},{24,16},{28,20},{1,9},{5... | collective-permute-start | bytes 196616 | tf_op jit(solution)/shard_map/ppermute | solution.py:313
  79.9 0.5 shard_map.71.matrix_ref
  80.5 1.8 %collective-permute-done.20.refs_3_ = f32[64,256]{1,0:T(8,128)S(1)} collective-permute-done((f32[64,256]{1,0:T(8,128)S(1)}, f32[64,256]{1,0:T(8,128)S(1)}, u32[]{:S(2)}, u32[]{:S(2)}) %collective-permute-start.20) | collective-permute-done | bytes 65568 | tf_op jit(solution)/shard_map/ppermute | solution.py:313
  82.3 0.1 collective-permute-done.19.refs_2_
  82.4 0.3 collective-permute-done.18.refs_1_
  82.8 1.8 %shard_map.72.inverse_ref = f32[256,256]{1,0:T(8,128)S(1)} custom-call(f32[256,256]{1,0:T(8,128)S(1)} %shard_map.71.matrix_ref), custom_call_target="tpu_custom_call" | custom-call | flops 1000000000 | tf_op jit(solution)/shard_map/pallas_call | solution.py:327
  84.6 0.3 shard_map.76
  84.9 2.1 %collective-permute-start.24 = (f32[8,256]{1,0:T(8,128)S(1)}, f32[8,256]{1,0:T(8,128)S(1)}, u32[]{:S(2)}, u32[]{:S(2)}) collective-permute-start(f32[8,256]{1,0:T(8,128)S(1)} %get-tuple-element.46.refs_1_), channel_id=1, source_target_pairs={{0,3},{1,2},{2,1},{3,0},{4,7},{5,6},{6,5},{7,4},{8,11},{9,10},{10,... | collective-permute-start | bytes 24584 | tf_op jit(solution)/shard_map/ppermute | solution.py:313
  86.9 0.6 collective-permute-start.23
  87.5 1.8 %collective-permute-start.22 = (f32[8,256]{1,0:T(8,128)S(1)}, f32[8,256]{1,0:T(8,128)S(1)}, u32[]{:S(2)}, u32[]{:S(2)}) collective-permute-start(f32[8,256]{1,0:T(8,128)S(1)} %get-tuple-element.46.refs_1_), channel_id=1, source_target_pairs={{0,1},{1,0},{2,3},{3,2},{4,5},{5,4},{6,7},{7,6},{8,9},{9,8},{10,11... | collective-permute-start | bytes 24584 | tf_op jit(solution)/shard_map/ppermute | solution.py:313
  89.3 0.6 copy.7
  90.0 0.6 copy.6
  90.6 0.9 collective-permute-done.23.refs_3_
  91.5 0.7 shard_map.77
  (27 shorter events, 0.4 us)
Async XLA Ops:
  0.6 6.8 %copy-start = (f32[64,64,128]{2,1,0:T(8,128)S(1)}, f32[64,64,128]{2,1,0:T(8,128)}, u32[]{:S(2)}) copy-start(f32[64,64,128]{2,1,0:T(8,128)} %param.3) | copy-start | bytes 6291460
  0.6 10.7 %collective-permute-start = (f32[128,256]{1,0:T(8,128)}, f32[128,256]{1,0:T(8,128)S(1)}, u32[]{:S(2)}, u32[]{:S(2)}) collective-permute-start(f32[128,256]{1,0:T(8,128)} %time_hbm.1), channel_id=1, source_target_pairs={{0,1},{1,0},{2,3},{3,2},{4,6},{5,7},{6,4},{7,5},{8,9},{9,8},{10,11... | collective-permute-start | bytes 393224 | tf_op jit(solution)/shard_map/ppermute | solution.py:366
  4.8 6.5 %collective-permute-start.1 = (f32[64,256]{1,0:T(8,128)S(1)}, f32[64,256]{1,0:T(8,128)S(1)}, u32[]{:S(2)}, u32[]{:S(2)}) collective-permute-start(f32[64,256]{1,0:T(8,128)S(1)} %get-tuple-element.28), channel_id=1, source_target_pairs={{0,3},{1,2},{2,1},{3,0},{4,7},{5,6},{6,5},{7,4},{8,11},{9,10},{10,... | collective-permute-start | bytes 196616 | tf_op jit(solution)/shard_map/ppermute | solution.py:313
  11.3 4.5 %collective-permute-start.2 = (f32[192,256]{1,0:T(8,128)S(1)}, f32[192,256]{1,0:T(8,128)S(1)}, u32[]{:S(2)}, u32[]{:S(2)}) collective-permute-start(f32[192,256]{1,0:T(8,128)S(1)} %shard_map.59.mine_ref), channel_id=1, source_target_pairs={{0,4},{4,0},{8,12},{12,8},{16,20},{20,16},{24,28},{28,24},{1,5},{5... | collective-permute-start | bytes 589832 | tf_op jit(solution)/shard_map/ppermute | solution.py:313
  11.4 40.1 %collective-permute-start.5 = (f32[64,256]{1,0:T(8,128)S(1)}, f32[64,256]{1,0:T(8,128)S(1)}, u32[]{:S(2)}, u32[]{:S(2)}) collective-permute-start(f32[64,256]{1,0:T(8,128)S(1)} %get-tuple-element.27.after_ref.refs_0_), channel_id=1, source_target_pairs={{0,3},{1,2},{2,1},{3,0},{4,7},{5,6},{6,5},{7,4},{8,11},{9,10},{10,... | collective-permute-start | bytes 196616 | tf_op jit(solution)/shard_map/ppermute | solution.py:313
  13.8 37.7 %collective-permute-start.4 = (f32[64,256]{1,0:T(8,128)S(1)}, f32[64,256]{1,0:T(8,128)S(1)}, u32[]{:S(2)}, u32[]{:S(2)}) collective-permute-start(f32[64,256]{1,0:T(8,128)S(1)} %get-tuple-element.27.after_ref.refs_0_), channel_id=1, source_target_pairs={{0,2},{1,3},{2,0},{3,1},{4,6},{5,7},{6,4},{7,5},{8,10},{9,11},{10,... | collective-permute-start | bytes 196616 | tf_op jit(solution)/shard_map/ppermute | solution.py:313
  14.0 37.5 %collective-permute-start.3 = (f32[64,256]{1,0:T(8,128)S(1)}, f32[64,256]{1,0:T(8,128)S(1)}, u32[]{:S(2)}, u32[]{:S(2)}) collective-permute-start(f32[64,256]{1,0:T(8,128)S(1)} %get-tuple-element.27.after_ref.refs_0_), channel_id=1, source_target_pairs={{0,1},{1,0},{2,3},{3,2},{4,5},{5,4},{6,7},{7,6},{8,9},{9,8},{10,11... | collective-permute-start | bytes 196616 | tf_op jit(solution)/shard_map/ppermute | solution.py:313
  52.5 1.4 %collective-permute-start.6 = (f32[96,256]{1,0:T(8,128)S(1)}, f32[96,256]{1,0:T(8,128)S(1)}, u32[]{:S(2)}, u32[]{:S(2)}) collective-permute-start(f32[96,256]{1,0:T(8,128)S(1)} %get-tuple-element.35), channel_id=1, source_target_pairs={{0,4},{4,0},{8,12},{12,8},{16,20},{20,16},{24,28},{28,24},{1,5},{5... | collective-permute-start | bytes 294920 | tf_op jit(solution)/shard_map/ppermute | solution.py:313
  53.9 10.2 %collective-permute-start.10 = (f32[128,256]{1,0:T(8,128)S(1)}, f32[128,256]{1,0:T(8,128)S(1)}, u32[]{:S(2)}, u32[]{:S(2)}) collective-permute-start(f32[128,256]{1,0:T(8,128)S(1)} %get-tuple-element.36.own_ref), channel_id=1, source_target_pairs={{0,8},{4,20},{8,0},{12,28},{16,24},{20,4},{24,16},{28,12},{1,9},{5... | collective-permute-start | bytes 393224 | tf_op jit(solution)/shard_map/ppermute | solution.py:369
  55.4 8.7 %collective-permute-start.11 = (f32[64,256]{1,0:T(8,128)S(1)}, f32[64,256]{1,0:T(8,128)S(1)}, u32[]{:S(2)}, u32[]{:S(2)}) collective-permute-start(f32[64,256]{1,0:T(8,128)S(1)} %get-tuple-element.33.raw_ref.refs_0_), channel_id=1, source_target_pairs={{0,24},{4,28},{8,16},{12,20},{16,8},{20,12},{24,0},{28,4},{1,25},{... | collective-permute-start | bytes 196616 | tf_op jit(solution)/shard_map/ppermute | solution.py:313
  56.9 5.8 %collective-permute-start.9 = (f32[32,256]{1,0:T(8,128)S(1)}, f32[32,256]{1,0:T(8,128)S(1)}, u32[]{:S(2)}, u32[]{:S(2)}) collective-permute-start(f32[32,256]{1,0:T(8,128)S(1)} %get-tuple-element.37.refs_0_), channel_id=1, source_target_pairs={{0,3},{1,2},{2,1},{3,0},{4,7},{5,6},{6,5},{7,4},{8,11},{9,10},{10,... | collective-permute-start | bytes 98312 | tf_op jit(solution)/shard_map/ppermute | solution.py:313
  59.3 4.8 %collective-permute-start.8 = (f32[32,256]{1,0:T(8,128)S(1)}, f32[32,256]{1,0:T(8,128)S(1)}, u32[]{:S(2)}, u32[]{:S(2)}) collective-permute-start(f32[32,256]{1,0:T(8,128)S(1)} %get-tuple-element.37.refs_0_), channel_id=1, source_target_pairs={{0,2},{1,3},{2,0},{3,1},{4,6},{5,7},{6,4},{7,5},{8,10},{9,11},{10,... | collective-permute-start | bytes 98312 | tf_op jit(solution)/shard_map/ppermute | solution.py:313
  59.3 4.8 %collective-permute-start.7 = (f32[32,256]{1,0:T(8,128)S(1)}, f32[32,256]{1,0:T(8,128)S(1)}, u32[]{:S(2)}, u32[]{:S(2)}) collective-permute-start(f32[32,256]{1,0:T(8,128)S(1)} %get-tuple-element.37.refs_0_), channel_id=1, source_target_pairs={{0,1},{1,0},{2,3},{3,2},{4,5},{5,4},{6,7},{7,6},{8,9},{9,8},{10,11... | collective-permute-start | bytes 98312 | tf_op jit(solution)/shard_map/ppermute | solution.py:313
  64.1 8.3 %collective-permute-start.12 = (f32[192,256]{1,0:T(8,128)S(1)}, f32[192,256]{1,0:T(8,128)S(1)}, u32[]{:S(2)}, u32[]{:S(2)}) collective-permute-start(f32[192,256]{1,0:T(8,128)S(1)} %shard_map.64.mine_ref), channel_id=1, source_target_pairs={{0,4},{4,0},{8,12},{12,8},{16,20},{20,16},{24,28},{28,24},{1,5},{5... | collective-permute-start | bytes 589832 | tf_op jit(solution)/shard_map/ppermute | solution.py:313
  65.4 4.9 %collective-permute-start.15 = (f32[32,256]{1,0:T(8,128)S(1)}, f32[32,256]{1,0:T(8,128)S(1)}, u32[]{:S(2)}, u32[]{:S(2)}) collective-permute-start(f32[32,256]{1,0:T(8,128)S(1)} %shard_map.63.after_ref.refs_0_), channel_id=1, source_target_pairs={{0,24},{4,28},{8,16},{12,20},{16,8},{20,12},{24,0},{28,4},{1,25},{... | collective-permute-start | bytes 98312 | tf_op jit(solution)/shard_map/ppermute | solution.py:313
  66.9 3.9 %collective-permute-start.14 = (f32[32,256]{1,0:T(8,128)S(1)}, f32[32,256]{1,0:T(8,128)S(1)}, u32[]{:S(2)}, u32[]{:S(2)}) collective-permute-start(f32[32,256]{1,0:T(8,128)S(1)} %shard_map.63.after_ref.refs_0_), channel_id=1, source_target_pairs={{0,16},{4,20},{8,24},{12,28},{16,0},{20,4},{24,8},{28,12},{1,17},{... | collective-permute-start | bytes 98312 | tf_op jit(solution)/shard_map/ppermute | solution.py:313
  68.4 3.9 %collective-permute-start.13 = (f32[32,256]{1,0:T(8,128)S(1)}, f32[32,256]{1,0:T(8,128)S(1)}, u32[]{:S(2)}, u32[]{:S(2)}) collective-permute-start(f32[32,256]{1,0:T(8,128)S(1)} %shard_map.63.after_ref.refs_0_), channel_id=1, source_target_pairs={{0,8},{4,12},{8,0},{12,4},{16,24},{20,28},{24,16},{28,20},{1,9},{5... | collective-permute-start | bytes 98312 | tf_op jit(solution)/shard_map/ppermute | solution.py:313
  72.3 1.6 %collective-permute-start.16 = (f32[32,256]{1,0:T(8,128)S(1)}, f32[32,256]{1,0:T(8,128)S(1)}, u32[]{:S(2)}, u32[]{:S(2)}) collective-permute-start(f32[32,256]{1,0:T(8,128)S(1)} %shard_map.69.mine_ref), channel_id=1, source_target_pairs={{0,4},{4,0},{8,12},{12,8},{16,20},{20,16},{24,28},{28,24},{1,5},{5... | collective-permute-start | bytes 98312 | tf_op jit(solution)/shard_map/ppermute | solution.py:313
  74.9 1.5 %collective-permute-start.17 = (f32[64,256]{1,0:T(8,128)S(1)}, f32[64,256]{1,0:T(8,128)S(1)}, u32[]{:S(2)}, u32[]{:S(2)}) collective-permute-start(f32[64,256]{1,0:T(8,128)S(1)} %get-tuple-element.44), channel_id=1, source_target_pairs={{0,4},{4,0},{8,12},{12,8},{16,20},{20,16},{24,28},{28,24},{1,5},{5... | collective-permute-start | bytes 196616 | tf_op jit(solution)/shard_map/ppermute | solution.py:313
  76.4 5.9 %collective-permute-start.20 = (f32[64,256]{1,0:T(8,128)S(1)}, f32[64,256]{1,0:T(8,128)S(1)}, u32[]{:S(2)}, u32[]{:S(2)}) collective-permute-start(f32[64,256]{1,0:T(8,128)S(1)} %shard_map.74.refs_0_), channel_id=1, source_target_pairs={{0,24},{4,28},{8,16},{12,20},{16,8},{20,12},{24,0},{28,4},{1,25},{... | collective-permute-start | bytes 196616 | tf_op jit(solution)/shard_map/ppermute | solution.py:313
  76.9 5.5 %collective-permute-start.19 = (f32[64,256]{1,0:T(8,128)S(1)}, f32[64,256]{1,0:T(8,128)S(1)}, u32[]{:S(2)}, u32[]{:S(2)}) collective-permute-start(f32[64,256]{1,0:T(8,128)S(1)} %shard_map.74.refs_0_), channel_id=1, source_target_pairs={{0,16},{4,20},{8,24},{12,28},{16,0},{20,4},{24,8},{28,12},{1,17},{... | collective-permute-start | bytes 196616 | tf_op jit(solution)/shard_map/ppermute | solution.py:313
  78.4 4.3 %collective-permute-start.18 = (f32[64,256]{1,0:T(8,128)S(1)}, f32[64,256]{1,0:T(8,128)S(1)}, u32[]{:S(2)}, u32[]{:S(2)}) collective-permute-start(f32[64,256]{1,0:T(8,128)S(1)} %shard_map.74.refs_0_), channel_id=1, source_target_pairs={{0,8},{4,12},{8,0},{12,4},{16,24},{20,28},{24,16},{28,20},{1,9},{5... | collective-permute-start | bytes 196616 | tf_op jit(solution)/shard_map/ppermute | solution.py:313
  82.7 1.9 %collective-permute-start.21 = (f32[64,256]{1,0:T(8,128)S(1)}, f32[64,256]{1,0:T(8,128)S(1)}, u32[]{:S(2)}, u32[]{:S(2)}) collective-permute-start(f32[64,256]{1,0:T(8,128)S(1)} %shard_map.75.mine_ref), channel_id=1, source_target_pairs={{0,4},{4,0},{8,12},{12,8},{16,20},{20,16},{24,28},{28,24},{1,5},{5... | collective-permute-start | bytes 196616 | tf_op jit(solution)/shard_map/ppermute | solution.py:313
  84.9 5.7 %collective-permute-start.24 = (f32[8,256]{1,0:T(8,128)S(1)}, f32[8,256]{1,0:T(8,128)S(1)}, u32[]{:S(2)}, u32[]{:S(2)}) collective-permute-start(f32[8,256]{1,0:T(8,128)S(1)} %get-tuple-element.46.refs_1_), channel_id=1, source_target_pairs={{0,3},{1,2},{2,1},{3,0},{4,7},{5,6},{6,5},{7,4},{8,11},{9,10},{10,... | collective-permute-start | bytes 24584 | tf_op jit(solution)/shard_map/ppermute | solution.py:313
  86.9 4.6 %collective-permute-start.23 = (f32[8,256]{1,0:T(8,128)S(1)}, f32[8,256]{1,0:T(8,128)S(1)}, u32[]{:S(2)}, u32[]{:S(2)}) collective-permute-start(f32[8,256]{1,0:T(8,128)S(1)} %get-tuple-element.46.refs_1_), channel_id=1, source_target_pairs={{0,2},{1,3},{2,0},{3,1},{4,6},{5,7},{6,4},{7,5},{8,10},{9,11},{10,... | collective-permute-start | bytes 24584 | tf_op jit(solution)/shard_map/ppermute | solution.py:313
  87.5 4.0 %collective-permute-start.22 = (f32[8,256]{1,0:T(8,128)S(1)}, f32[8,256]{1,0:T(8,128)S(1)}, u32[]{:S(2)}, u32[]{:S(2)}) collective-permute-start(f32[8,256]{1,0:T(8,128)S(1)} %get-tuple-element.46.refs_1_), channel_id=1, source_target_pairs={{0,1},{1,0},{2,3},{3,2},{4,5},{5,4},{6,7},{7,6},{8,9},{9,8},{10,11... | collective-permute-start | bytes 24584 | tf_op jit(solution)/shard_map/ppermute | solution.py:313

commit v5 on v4

--- a/solution.py
+++ b/solution.py
@@ -195,12 +195,16 @@
         side_ref[p] = dot_fast(jnp.concatenate([high, low, high, low], axis=0), weights, ((0,), (0,)))
 
 
-def first_inverse_kernel(species_ref, own_ref, mine_ref, partner_ref,
+def factor_gram_kernel(after_ref, species_ref, out_ref):
+    out_ref[...] = gram(species_ref[...])
+
+
+def first_inverse_kernel(b_gram_ref, own_ref, mine_ref, partner_ref,
                          c_gram_ref, matrix_ref, inverse_ref, factor_ref, work_ref):
     place_blocks(factor_ref, place_of("tm"), place_of("space") % 2, own_ref, mine_ref, partner_ref)
     c_gram = gram(factor_ref[...])
     c_gram_ref[...] = c_gram
-    matrix = regularized(gram(species_ref[...]) * c_gram)
+    matrix = regularized(b_gram_ref[...] * c_gram)
     matrix_ref[...] = matrix
     invert(matrix, inverse_ref, work_ref)
 
@@ -398,9 +402,10 @@
 
     mine = pack(m_a, received)
     partner = to_partner(mine)
+    (b_gram,) = run(factor_gram_kernel, [square], 0.5)(mine, species_here)
     c_gram, matrix, inverse = run(
         first_inverse_kernel, [square] * 3, 2, [local(total_steps, rank), square]
-    )(species_here, time_here, mine, partner)
+    )(b_gram, time_here, mine, partner)
 
     raw, keep, send = run(
         space_solve_kernel,

time: 92.3 us -> 92.6 us (level)
    pallas_call x20 -> x21, Pallas kernels: 46 us -> 46.3 us  [placed(): call(*[pltpu.with_memory_space_constraint(x, pltpu.VMEM) for x in operands])]
where the time goes in v5:
time: 92.6 us; the launch traced here: 92.5 us
  Pallas kernels  47.3 us (51%)
  starting transfers between devices  30.1 us (33%)
  waiting for transfers between devices  12.9 us (14%)
  local copies, waits for them, and re-layouts  1.26 us (1%)
    pallas_call x21, Pallas kernels, placed(): call(*[pltpu.with_memory_space_constraint(x, pltpu.VMEM) for x in operands])  46.3 us
    ppermute x23, starting transfers between devices, exchange(): return lax.ppermute(value, axis, [(i, i ^ step) for i in range(count)])  25.4 us
    ppermute x23, waiting for transfers between devices, exchange(): return lax.ppermute(value, axis, [(i, i ^ step) for i in range(count)])  12.9 us
    ppermute x1, starting transfers between devices, block_from(): received.append(lax.ppermute(block, ('space', 'tm'), turns))  3.12 us
  transfers between devices with their start and end apart: 25, of which 12 were waited for; matrix products, arithmetic and copies ran while one was open for 1% of the time, Pallas kernels for 48%

profile of v5, /device:TPU:0, one launch (start us, length us, event | category | flops | bytes accessed | tf_op | source)
XLA Modules:
  0.0 92.5 jit_solution(6516903388214343814)
XLA Ops:
  0.6 3.1 %collective-permute-start = (f32[128,256]{1,0:T(8,128)}, f32[128,256]{1,0:T(8,128)S(1)}, u32[]{:S(2)}, u32[]{:S(2)}) collective-permute-start(f32[128,256]{1,0:T(8,128)} %time_hbm.1), channel_id=1, source_target_pairs={{0,1},{1,0},{2,3},{3,2},{4,6},{5,7},{6,4},{7,5},{8,9},{9,8},{10,11... | collective-permute-start | bytes 393224 | tf_op jit(solution)/shard_map/ppermute | solution.py:370
  3.8 1.0 %load.1 = (f32[64,256]{1,0:T(8,128)S(1)}, f32[128,256]{1,0:T(8,128)S(1)}, f32[64,256]{1,0:T(8,128)S(1)}) custom-call(f32[128,256]{1,0:T(8,128)} %time_hbm.1, f32[64,256]{1,0:T(8,128)} %species_hbm.1), custom_call_target="tpu_custom_call" | custom-call | flops 10000000000 | bytes 100000000 | tf_op jit(solution)/shard_map/load/pallas_call | solution.py:387
  4.8 2.6 %collective-permute-start.1 = (f32[64,256]{1,0:T(8,128)S(1)}, f32[64,256]{1,0:T(8,128)S(1)}, u32[]{:S(2)}, u32[]{:S(2)}) collective-permute-start(f32[64,256]{1,0:T(8,128)S(1)} %get-tuple-element.28), channel_id=1, source_target_pairs={{0,3},{1,2},{2,1},{3,0},{4,7},{5,6},{6,5},{7,4},{8,11},{9,10},{10,... | collective-permute-start | bytes 196616 | tf_op jit(solution)/shard_map/ppermute | solution.py:317
  7.4 1.3 %shard_map.58 = (f32[64,256]{1,0:T(8,128)S(1)}, f32[64,64,256]{2,1,0:T(8,128)S(1)}) custom-call(f32[4096,128]{1,0:T(8,128)S(1)} %bitcast.1, f32[128,256]{1,0:T(8,128)S(1)} %get-tuple-element.25.time_ref.own_ref, f32[64,256]{1,0:T(8,128)S(1)} %get-tuple-element.26.species_ref), custom_call_target="tpu_custom_call" | custom-call | flops 2000000000 | tf_op jit(solution)/shard_map/pallas_call | solution.py:331
  8.7 2.6 %collective-permute-done.1.refs_1_ = f32[64,256]{1,0:T(8,128)S(1)} collective-permute-done((f32[64,256]{1,0:T(8,128)S(1)}, f32[64,256]{1,0:T(8,128)S(1)}, u32[]{:S(2)}, u32[]{:S(2)}) %collective-permute-start.1) | collective-permute-done | bytes 65568 | tf_op jit(solution)/shard_map/ppermute | solution.py:317
  11.4 2.4 %collective-permute-start.5 = (f32[64,256]{1,0:T(8,128)S(1)}, f32[64,256]{1,0:T(8,128)S(1)}, u32[]{:S(2)}, u32[]{:S(2)}) collective-permute-start(f32[64,256]{1,0:T(8,128)S(1)} %get-tuple-element.27.after_ref.refs_0_), channel_id=1, source_target_pairs={{0,3},{1,2},{2,1},{3,0},{4,7},{5,6},{6,5},{7,4},{8,11},{9,10},{10,... | collective-permute-start | bytes 196616 | tf_op jit(solution)/shard_map/ppermute | solution.py:317
  13.8 0.2 collective-permute-start.4
  14.0 1.8 %collective-permute-start.3 = (f32[64,256]{1,0:T(8,128)S(1)}, f32[64,256]{1,0:T(8,128)S(1)}, u32[]{:S(2)}, u32[]{:S(2)}) collective-permute-start(f32[64,256]{1,0:T(8,128)S(1)} %get-tuple-element.27.after_ref.refs_0_), channel_id=1, source_target_pairs={{0,1},{1,0},{2,3},{3,2},{4,5},{5,4},{6,7},{7,6},{8,9},{9,8},{10,11... | collective-permute-start | bytes 196616 | tf_op jit(solution)/shard_map/ppermute | solution.py:317
  15.9 0.4 shard_map.60.b_gram_ref
  16.3 35.5 %shard_map.61 = (f32[256,256]{1,0:T(8,128)S(1)}, f32[256,256]{1,0:T(8,128)S(1)}, f32[256,256]{1,0:T(8,128)S(1)}) custom-call(f32[256,256]{1,0:T(8,128)S(1)} %shard_map.60.b_gram_ref, f32[128,256]{1,0:T(8,128)S(1)} %get-tuple-element.25.time_ref.own_ref, f32[192,256]{1,0:T(8,128)S(1)} %shard_map.59.after_ref.mine_ref, ...), custom_call_target="tpu_custom_call" | custom-call | flops 2000000000 | tf_op jit(solution)/shard_map/pallas_call | solution.py:331
  51.8 0.9 shard_map.62
  52.8 1.3 %collective-permute-done.6.received_ref = f32[96,256]{1,0:T(8,128)S(1)} collective-permute-done((f32[96,256]{1,0:T(8,128)S(1)}, f32[96,256]{1,0:T(8,128)S(1)}, u32[]{:S(2)}, u32[]{:S(2)}) %collective-permute-start.6) | collective-permute-done | bytes 98336 | tf_op jit(solution)/shard_map/ppermute | solution.py:317
  54.1 1.6 %collective-permute-start.10 = (f32[128,256]{1,0:T(8,128)S(1)}, f32[128,256]{1,0:T(8,128)S(1)}, u32[]{:S(2)}, u32[]{:S(2)}) collective-permute-start(f32[128,256]{1,0:T(8,128)S(1)} %get-tuple-element.36.own_ref), channel_id=1, source_target_pairs={{0,8},{4,20},{8,0},{12,28},{16,24},{20,4},{24,16},{28,12},{1,9},{5... | collective-permute-start | bytes 393224 | tf_op jit(solution)/shard_map/ppermute | solution.py:373
  55.7 1.5 %collective-permute-start.11 = (f32[64,256]{1,0:T(8,128)S(1)}, f32[64,256]{1,0:T(8,128)S(1)}, u32[]{:S(2)}, u32[]{:S(2)}) collective-permute-start(f32[64,256]{1,0:T(8,128)S(1)} %get-tuple-element.33.raw_ref.refs_0_), channel_id=1, source_target_pairs={{0,24},{4,28},{8,16},{12,20},{16,8},{20,12},{24,0},{28,4},{1,25},{... | collective-permute-start | bytes 196616 | tf_op jit(solution)/shard_map/ppermute | solution.py:317
  57.2 2.4 %collective-permute-start.9 = (f32[32,256]{1,0:T(8,128)S(1)}, f32[32,256]{1,0:T(8,128)S(1)}, u32[]{:S(2)}, u32[]{:S(2)}) collective-permute-start(f32[32,256]{1,0:T(8,128)S(1)} %get-tuple-element.37.refs_0_), channel_id=1, source_target_pairs={{0,3},{1,2},{2,1},{3,0},{4,7},{5,6},{6,5},{7,4},{8,11},{9,10},{10,... | collective-permute-start | bytes 98312 | tf_op jit(solution)/shard_map/ppermute | solution.py:317
  59.5 2.0 %collective-permute-start.7 = (f32[32,256]{1,0:T(8,128)S(1)}, f32[32,256]{1,0:T(8,128)S(1)}, u32[]{:S(2)}, u32[]{:S(2)}) collective-permute-start(f32[32,256]{1,0:T(8,128)S(1)} %get-tuple-element.37.refs_0_), channel_id=1, source_target_pairs={{0,1},{1,0},{2,3},{3,2},{4,5},{5,4},{6,7},{7,6},{8,9},{9,8},{10,11... | collective-permute-start | bytes 98312 | tf_op jit(solution)/shard_map/ppermute | solution.py:317
  61.6 1.4 %collective-permute-done.9.refs_3_ = f32[32,256]{1,0:T(8,128)S(1)} collective-permute-done((f32[32,256]{1,0:T(8,128)S(1)}, f32[32,256]{1,0:T(8,128)S(1)}, u32[]{:S(2)}, u32[]{:S(2)}) %collective-permute-start.9) | collective-permute-done | bytes 32800 | tf_op jit(solution)/shard_map/ppermute | solution.py:317
  63.0 1.4 %collective-permute-done.8.refs_2_ = f32[32,256]{1,0:T(8,128)S(1)} collective-permute-done((f32[32,256]{1,0:T(8,128)S(1)}, f32[32,256]{1,0:T(8,128)S(1)}, u32[]{:S(2)}, u32[]{:S(2)}) %collective-permute-start.8) | collective-permute-done | bytes 32800 | tf_op jit(solution)/shard_map/ppermute | solution.py:317
  64.5 1.1 %shard_map.68.side_ref = f32[40,128,256]{2,1,0:T(8,128)S(1)} custom-call(f32[64,256]{1,0:T(8,128)S(1)} %get-tuple-element.33.raw_ref.refs_0_, f32[4096,128]{1,0:T(8,128)S(1)} %bitcast.2), custom_call_target="tpu_custom_call" | custom-call | flops 1250000000 | tf_op jit(solution)/shard_map/pallas_call | solution.py:331
  65.6 1.5 %collective-permute-start.15 = (f32[32,256]{1,0:T(8,128)S(1)}, f32[32,256]{1,0:T(8,128)S(1)}, u32[]{:S(2)}, u32[]{:S(2)}) collective-permute-start(f32[32,256]{1,0:T(8,128)S(1)} %shard_map.64.after_ref.refs_0_), channel_id=1, source_target_pairs={{0,24},{4,28},{8,16},{12,20},{16,8},{20,12},{24,0},{28,4},{1,25},{... | collective-permute-start | bytes 98312 | tf_op jit(solution)/shard_map/ppermute | solution.py:317
  67.1 1.5 %collective-permute-start.14 = (f32[32,256]{1,0:T(8,128)S(1)}, f32[32,256]{1,0:T(8,128)S(1)}, u32[]{:S(2)}, u32[]{:S(2)}) collective-permute-start(f32[32,256]{1,0:T(8,128)S(1)} %shard_map.64.after_ref.refs_0_), channel_id=1, source_target_pairs={{0,16},{4,20},{8,24},{12,28},{16,0},{20,4},{24,8},{28,12},{1,17},{... | collective-permute-start | bytes 98312 | tf_op jit(solution)/shard_map/ppermute | solution.py:317
  68.7 0.5 collective-permute-start.13
  69.2 0.7 shard_map.69.rest_ref
  69.9 0.6 collective-permute-done.15.refs_3_
  70.5 0.6 collective-permute-done.14.refs_2_
  71.1 1.5 %collective-permute-done.13.refs_1_ = f32[32,256]{1,0:T(8,128)S(1)} collective-permute-done((f32[32,256]{1,0:T(8,128)S(1)}, f32[32,256]{1,0:T(8,128)S(1)}, u32[]{:S(2)}, u32[]{:S(2)}) %collective-permute-start.13) | collective-permute-done | bytes 32800 | tf_op jit(solution)/shard_map/ppermute | solution.py:317
  72.7 0.8 shard_map.66
  73.5 0.7 shard_map.67.inverse_ref
  74.2 0.9 %shard_map.71 = (f32[64,256]{1,0:T(8,128)S(1)}, f32[64,256]{1,0:T(8,128)S(1)}, f32[64,256]{1,0:T(8,128)S(1)}) custom-call(f32[8,256]{1,0:T(8,128)S(1)} %get-tuple-element.39.scale_ref, f32[256,256]{1,0:T(8,128)S(1)} %get-tuple-element.40.matrix_ref, f32[256,256]{1,0:T(8,128)S(1)} %shard_map.67.inverse_ref, f32[40,128,256]{2,1,0:T(8,128)S(1)} %shard_map.68.side_ref, ...), custom_call_target="tpu_custom_call" | custom-call | flops 1500000000 | tf_op jit(solution)/shard_map/pallas_call | solution.py:331
  75.2 0.6 collective-permute-start.17
  75.7 0.4 shard_map.74.refs_0_
  76.2 0.5 collective-permute-done.17.refs_1_
  76.6 0.5 collective-permute-start.20
  77.2 1.5 %collective-permute-start.19 = (f32[64,256]{1,0:T(8,128)S(1)}, f32[64,256]{1,0:T(8,128)S(1)}, u32[]{:S(2)}, u32[]{:S(2)}) collective-permute-start(f32[64,256]{1,0:T(8,128)S(1)} %shard_map.75.refs_0_), channel_id=1, source_target_pairs={{0,16},{4,20},{8,24},{12,28},{16,0},{20,4},{24,8},{28,12},{1,17},{... | collective-permute-start | bytes 196616 | tf_op jit(solution)/shard_map/ppermute | solution.py:317
  78.7 1.5 %collective-permute-start.18 = (f32[64,256]{1,0:T(8,128)S(1)}, f32[64,256]{1,0:T(8,128)S(1)}, u32[]{:S(2)}, u32[]{:S(2)}) collective-permute-start(f32[64,256]{1,0:T(8,128)S(1)} %shard_map.75.refs_0_), channel_id=1, source_target_pairs={{0,8},{4,12},{8,0},{12,4},{16,24},{20,28},{24,16},{28,20},{1,9},{5... | collective-permute-start | bytes 196616 | tf_op jit(solution)/shard_map/ppermute | solution.py:317
  80.2 0.5 shard_map.72.matrix_ref
  80.7 1.8 %collective-permute-done.20.refs_3_ = f32[64,256]{1,0:T(8,128)S(1)} collective-permute-done((f32[64,256]{1,0:T(8,128)S(1)}, f32[64,256]{1,0:T(8,128)S(1)}, u32[]{:S(2)}, u32[]{:S(2)}) %collective-permute-start.20) | collective-permute-done | bytes 65568 | tf_op jit(solution)/shard_map/ppermute | solution.py:317
  82.6 0.1 collective-permute-done.19.refs_2_
  82.7 0.3 collective-permute-done.18.refs_1_
  83.1 1.8 %shard_map.73.inverse_ref = f32[256,256]{1,0:T(8,128)S(1)} custom-call(f32[256,256]{1,0:T(8,128)S(1)} %shard_map.72.matrix_ref), custom_call_target="tpu_custom_call" | custom-call | flops 1000000000 | tf_op jit(solution)/shard_map/pallas_call | solution.py:331
  84.8 0.3 shard_map.77
  85.1 2.1 %collective-permute-start.24 = (f32[8,256]{1,0:T(8,128)S(1)}, f32[8,256]{1,0:T(8,128)S(1)}, u32[]{:S(2)}, u32[]{:S(2)}) collective-permute-start(f32[8,256]{1,0:T(8,128)S(1)} %get-tuple-element.46.refs_1_), channel_id=1, source_target_pairs={{0,3},{1,2},{2,1},{3,0},{4,7},{5,6},{6,5},{7,4},{8,11},{9,10},{10,... | collective-permute-start | bytes 24584 | tf_op jit(solution)/shard_map/ppermute | solution.py:317
  87.2 0.6 collective-permute-start.23
  87.8 1.8 %collective-permute-start.22 = (f32[8,256]{1,0:T(8,128)S(1)}, f32[8,256]{1,0:T(8,128)S(1)}, u32[]{:S(2)}, u32[]{:S(2)}) collective-permute-start(f32[8,256]{1,0:T(8,128)S(1)} %get-tuple-element.46.refs_1_), channel_id=1, source_target_pairs={{0,1},{1,0},{2,3},{3,2},{4,5},{5,4},{6,7},{7,6},{8,9},{9,8},{10,11... | collective-permute-start | bytes 24584 | tf_op jit(solution)/shard_map/ppermute | solution.py:317
  89.6 0.6 copy.7
  90.2 0.6 copy.6
  90.9 0.9 collective-permute-done.23.refs_3_
  91.8 0.7 shard_map.78
  (28 shorter events, 0.5 us)
Async XLA Ops:
  0.6 6.8 %copy-start = (f32[64,64,128]{2,1,0:T(8,128)S(1)}, f32[64,64,128]{2,1,0:T(8,128)}, u32[]{:S(2)}) copy-start(f32[64,64,128]{2,1,0:T(8,128)} %param.3) | copy-start | bytes 6291460
  0.6 10.7 %collective-permute-start = (f32[128,256]{1,0:T(8,128)}, f32[128,256]{1,0:T(8,128)S(1)}, u32[]{:S(2)}, u32[]{:S(2)}) collective-permute-start(f32[128,256]{1,0:T(8,128)} %time_hbm.1), channel_id=1, source_target_pairs={{0,1},{1,0},{2,3},{3,2},{4,6},{5,7},{6,4},{7,5},{8,9},{9,8},{10,11... | collective-permute-start | bytes 393224 | tf_op jit(solution)/shard_map/ppermute | solution.py:370
  4.8 6.5 %collective-permute-start.1 = (f32[64,256]{1,0:T(8,128)S(1)}, f32[64,256]{1,0:T(8,128)S(1)}, u32[]{:S(2)}, u32[]{:S(2)}) collective-permute-start(f32[64,256]{1,0:T(8,128)S(1)} %get-tuple-element.28), channel_id=1, source_target_pairs={{0,3},{1,2},{2,1},{3,0},{4,7},{5,6},{6,5},{7,4},{8,11},{9,10},{10,... | collective-permute-start | bytes 196616 | tf_op jit(solution)/shard_map/ppermute | solution.py:317
  11.3 4.9 %collective-permute-start.2 = (f32[192,256]{1,0:T(8,128)S(1)}, f32[192,256]{1,0:T(8,128)S(1)}, u32[]{:S(2)}, u32[]{:S(2)}) collective-permute-start(f32[192,256]{1,0:T(8,128)S(1)} %shard_map.59.after_ref.mine_ref), channel_id=1, source_target_pairs={{0,4},{4,0},{8,12},{12,8},{16,20},{20,16},{24,28},{28,24},{1,5},{5... | collective-permute-start | bytes 589832 | tf_op jit(solution)/shard_map/ppermute | solution.py:317
  11.4 40.4 %collective-permute-start.5 = (f32[64,256]{1,0:T(8,128)S(1)}, f32[64,256]{1,0:T(8,128)S(1)}, u32[]{:S(2)}, u32[]{:S(2)}) collective-permute-start(f32[64,256]{1,0:T(8,128)S(1)} %get-tuple-element.27.after_ref.refs_0_), channel_id=1, source_target_pairs={{0,3},{1,2},{2,1},{3,0},{4,7},{5,6},{6,5},{7,4},{8,11},{9,10},{10,... | collective-permute-start | bytes 196616 | tf_op jit(solution)/shard_map/ppermute | solution.py:317
  13.8 38.0 %collective-permute-start.4 = (f32[64,256]{1,0:T(8,128)S(1)}, f32[64,256]{1,0:T(8,128)S(1)}, u32[]{:S(2)}, u32[]{:S(2)}) collective-permute-start(f32[64,256]{1,0:T(8,128)S(1)} %get-tuple-element.27.after_ref.refs_0_), channel_id=1, source_target_pairs={{0,2},{1,3},{2,0},{3,1},{4,6},{5,7},{6,4},{7,5},{8,10},{9,11},{10,... | collective-permute-start | bytes 196616 | tf_op jit(solution)/shard_map/ppermute | solution.py:317
  14.0 37.8 %collective-permute-start.3 = (f32[64,256]{1,0:T(8,128)S(1)}, f32[64,256]{1,0:T(8,128)S(1)}, u32[]{:S(2)}, u32[]{:S(2)}) collective-permute-start(f32[64,256]{1,0:T(8,128)S(1)} %get-tuple-element.27.after_ref.refs_0_), channel_id=1, source_target_pairs={{0,1},{1,0},{2,3},{3,2},{4,5},{5,4},{6,7},{7,6},{8,9},{9,8},{10,11... | collective-permute-start | bytes 196616 | tf_op jit(solution)/shard_map/ppermute | solution.py:317
  52.7 1.4 %collective-permute-start.6 = (f32[96,256]{1,0:T(8,128)S(1)}, f32[96,256]{1,0:T(8,128)S(1)}, u32[]{:S(2)}, u32[]{:S(2)}) collective-permute-start(f32[96,256]{1,0:T(8,128)S(1)} %get-tuple-element.35), channel_id=1, source_target_pairs={{0,4},{4,0},{8,12},{12,8},{16,20},{20,16},{24,28},{28,24},{1,5},{5... | collective-permute-start | bytes 294920 | tf_op jit(solution)/shard_map/ppermute | solution.py:317
  54.1 10.2 %collective-permute-start.10 = (f32[128,256]{1,0:T(8,128)S(1)}, f32[128,256]{1,0:T(8,128)S(1)}, u32[]{:S(2)}, u32[]{:S(2)}) collective-permute-start(f32[128,256]{1,0:T(8,128)S(1)} %get-tuple-element.36.own_ref), channel_id=1, source_target_pairs={{0,8},{4,20},{8,0},{12,28},{16,24},{20,4},{24,16},{28,12},{1,9},{5... | collective-permute-start | bytes 393224 | tf_op jit(solution)/shard_map/ppermute | solution.py:373
  55.7 8.7 %collective-permute-start.11 = (f32[64,256]{1,0:T(8,128)S(1)}, f32[64,256]{1,0:T(8,128)S(1)}, u32[]{:S(2)}, u32[]{:S(2)}) collective-permute-start(f32[64,256]{1,0:T(8,128)S(1)} %get-tuple-element.33.raw_ref.refs_0_), channel_id=1, source_target_pairs={{0,24},{4,28},{8,16},{12,20},{16,8},{20,12},{24,0},{28,4},{1,25},{... | collective-permute-start | bytes 196616 | tf_op jit(solution)/shard_map/ppermute | solution.py:317
  57.2 5.8 %collective-permute-start.9 = (f32[32,256]{1,0:T(8,128)S(1)}, f32[32,256]{1,0:T(8,128)S(1)}, u32[]{:S(2)}, u32[]{:S(2)}) collective-permute-start(f32[32,256]{1,0:T(8,128)S(1)} %get-tuple-element.37.refs_0_), channel_id=1, source_target_pairs={{0,3},{1,2},{2,1},{3,0},{4,7},{5,6},{6,5},{7,4},{8,11},{9,10},{10,... | collective-permute-start | bytes 98312 | tf_op jit(solution)/shard_map/ppermute | solution.py:317
  59.5 4.8 %collective-permute-start.8 = (f32[32,256]{1,0:T(8,128)S(1)}, f32[32,256]{1,0:T(8,128)S(1)}, u32[]{:S(2)}, u32[]{:S(2)}) collective-permute-start(f32[32,256]{1,0:T(8,128)S(1)} %get-tuple-element.37.refs_0_), channel_id=1, source_target_pairs={{0,2},{1,3},{2,0},{3,1},{4,6},{5,7},{6,4},{7,5},{8,10},{9,11},{10,... | collective-permute-start | bytes 98312 | tf_op jit(solution)/shard_map/ppermute | solution.py:317
  59.5 4.8 %collective-permute-start.7 = (f32[32,256]{1,0:T(8,128)S(1)}, f32[32,256]{1,0:T(8,128)S(1)}, u32[]{:S(2)}, u32[]{:S(2)}) collective-permute-start(f32[32,256]{1,0:T(8,128)S(1)} %get-tuple-element.37.refs_0_), channel_id=1, source_target_pairs={{0,1},{1,0},{2,3},{3,2},{4,5},{5,4},{6,7},{7,6},{8,9},{9,8},{10,11... | collective-permute-start | bytes 98312 | tf_op jit(solution)/shard_map/ppermute | solution.py:317
  64.4 8.3 %collective-permute-start.12 = (f32[192,256]{1,0:T(8,128)S(1)}, f32[192,256]{1,0:T(8,128)S(1)}, u32[]{:S(2)}, u32[]{:S(2)}) collective-permute-start(f32[192,256]{1,0:T(8,128)S(1)} %shard_map.65.mine_ref), channel_id=1, source_target_pairs={{0,4},{4,0},{8,12},{12,8},{16,20},{20,16},{24,28},{28,24},{1,5},{5... | collective-permute-start | bytes 589832 | tf_op jit(solution)/shard_map/ppermute | solution.py:317
  65.6 4.9 %collective-permute-start.15 = (f32[32,256]{1,0:T(8,128)S(1)}, f32[32,256]{1,0:T(8,128)S(1)}, u32[]{:S(2)}, u32[]{:S(2)}) collective-permute-start(f32[32,256]{1,0:T(8,128)S(1)} %shard_map.64.after_ref.refs_0_), channel_id=1, source_target_pairs={{0,24},{4,28},{8,16},{12,20},{16,8},{20,12},{24,0},{28,4},{1,25},{... | collective-permute-start | bytes 98312 | tf_op jit(solution)/shard_map/ppermute | solution.py:317
  67.1 3.9 %collective-permute-start.14 = (f32[32,256]{1,0:T(8,128)S(1)}, f32[32,256]{1,0:T(8,128)S(1)}, u32[]{:S(2)}, u32[]{:S(2)}) collective-permute-start(f32[32,256]{1,0:T(8,128)S(1)} %shard_map.64.after_ref.refs_0_), channel_id=1, source_target_pairs={{0,16},{4,20},{8,24},{12,28},{16,0},{20,4},{24,8},{28,12},{1,17},{... | collective-permute-start | bytes 98312 | tf_op jit(solution)/shard_map/ppermute | solution.py:317
  68.7 3.9 %collective-permute-start.13 = (f32[32,256]{1,0:T(8,128)S(1)}, f32[32,256]{1,0:T(8,128)S(1)}, u32[]{:S(2)}, u32[]{:S(2)}) collective-permute-start(f32[32,256]{1,0:T(8,128)S(1)} %shard_map.64.after_ref.refs_0_), channel_id=1, source_target_pairs={{0,8},{4,12},{8,0},{12,4},{16,24},{20,28},{24,16},{28,20},{1,9},{5... | collective-permute-start | bytes 98312 | tf_op jit(solution)/shard_map/ppermute | solution.py:317
  72.6 1.6 %collective-permute-start.16 = (f32[32,256]{1,0:T(8,128)S(1)}, f32[32,256]{1,0:T(8,128)S(1)}, u32[]{:S(2)}, u32[]{:S(2)}) collective-permute-start(f32[32,256]{1,0:T(8,128)S(1)} %shard_map.70.mine_ref), channel_id=1, source_target_pairs={{0,4},{4,0},{8,12},{12,8},{16,20},{20,16},{24,28},{28,24},{1,5},{5... | collective-permute-start | bytes 98312 | tf_op jit(solution)/shard_map/ppermute | solution.py:317
  75.2 1.5 %collective-permute-start.17 = (f32[64,256]{1,0:T(8,128)S(1)}, f32[64,256]{1,0:T(8,128)S(1)}, u32[]{:S(2)}, u32[]{:S(2)}) collective-permute-start(f32[64,256]{1,0:T(8,128)S(1)} %get-tuple-element.44), channel_id=1, source_target_pairs={{0,4},{4,0},{8,12},{12,8},{16,20},{20,16},{24,28},{28,24},{1,5},{5... | collective-permute-start | bytes 196616 | tf_op jit(solution)/shard_map/ppermute | solution.py:317
  76.6 5.9 %collective-permute-start.20 = (f32[64,256]{1,0:T(8,128)S(1)}, f32[64,256]{1,0:T(8,128)S(1)}, u32[]{:S(2)}, u32[]{:S(2)}) collective-permute-start(f32[64,256]{1,0:T(8,128)S(1)} %shard_map.75.refs_0_), channel_id=1, source_target_pairs={{0,24},{4,28},{8,16},{12,20},{16,8},{20,12},{24,0},{28,4},{1,25},{... | collective-permute-start | bytes 196616 | tf_op jit(solution)/shard_map/ppermute | solution.py:317
  77.2 5.5 %collective-permute-start.19 = (f32[64,256]{1,0:T(8,128)S(1)}, f32[64,256]{1,0:T(8,128)S(1)}, u32[]{:S(2)}, u32[]{:S(2)}) collective-permute-start(f32[64,256]{1,0:T(8,128)S(1)} %shard_map.75.refs_0_), channel_id=1, source_target_pairs={{0,16},{4,20},{8,24},{12,28},{16,0},{20,4},{24,8},{28,12},{1,17},{... | collective-permute-start | bytes 196616 | tf_op jit(solution)/shard_map/ppermute | solution.py:317
  78.7 4.3 %collective-permute-start.18 = (f32[64,256]{1,0:T(8,128)S(1)}, f32[64,256]{1,0:T(8,128)S(1)}, u32[]{:S(2)}, u32[]{:S(2)}) collective-permute-start(f32[64,256]{1,0:T(8,128)S(1)} %shard_map.75.refs_0_), channel_id=1, source_target_pairs={{0,8},{4,12},{8,0},{12,4},{16,24},{20,28},{24,16},{28,20},{1,9},{5... | collective-permute-start | bytes 196616 | tf_op jit(solution)/shard_map/ppermute | solution.py:317
  83.0 1.9 %collective-permute-start.21 = (f32[64,256]{1,0:T(8,128)S(1)}, f32[64,256]{1,0:T(8,128)S(1)}, u32[]{:S(2)}, u32[]{:S(2)}) collective-permute-start(f32[64,256]{1,0:T(8,128)S(1)} %shard_map.76.mine_ref), channel_id=1, source_target_pairs={{0,4},{4,0},{8,12},{12,8},{16,20},{20,16},{24,28},{28,24},{1,5},{5... | collective-permute-start | bytes 196616 | tf_op jit(solution)/shard_map/ppermute | solution.py:317
  85.1 5.7 %collective-permute-start.24 = (f32[8,256]{1,0:T(8,128)S(1)}, f32[8,256]{1,0:T(8,128)S(1)}, u32[]{:S(2)}, u32[]{:S(2)}) collective-permute-start(f32[8,256]{1,0:T(8,128)S(1)} %get-tuple-element.46.refs_1_), channel_id=1, source_target_pairs={{0,3},{1,2},{2,1},{3,0},{4,7},{5,6},{6,5},{7,4},{8,11},{9,10},{10,... | collective-permute-start | bytes 24584 | tf_op jit(solution)/shard_map/ppermute | solution.py:317
  87.2 4.6 %collective-permute-start.23 = (f32[8,256]{1,0:T(8,128)S(1)}, f32[8,256]{1,0:T(8,128)S(1)}, u32[]{:S(2)}, u32[]{:S(2)}) collective-permute-start(f32[8,256]{1,0:T(8,128)S(1)} %get-tuple-element.46.refs_1_), channel_id=1, source_target_pairs={{0,2},{1,3},{2,0},{3,1},{4,6},{5,7},{6,4},{7,5},{8,10},{9,11},{10,... | collective-permute-start | bytes 24584 | tf_op jit(solution)/shard_map/ppermute | solution.py:317
  87.8 4.0 %collective-permute-start.22 = (f32[8,256]{1,0:T(8,128)S(1)}, f32[8,256]{1,0:T(8,128)S(1)}, u32[]{:S(2)}, u32[]{:S(2)}) collective-permute-start(f32[8,256]{1,0:T(8,128)S(1)} %get-tuple-element.46.refs_1_), channel_id=1, source_target_pairs={{0,1},{1,0},{2,3},{3,2},{4,5},{5,4},{6,7},{7,6},{8,9},{9,8},{10,11... | collective-permute-start | bytes 24584 | tf_op jit(solution)/shard_map/ppermute | solution.py:317
